TPU v7x, 8 devices: a whole 2x2x1 slice. The times are simulated.
8 devices in a mesh: dp: 1 (over z), tp: 2 (over y), ep: 4 (over x, core).
Axes of the slice: x: 2, y: 2, z: 1, core: 2. Of those that a mesh axis runs over, the one named last changes fastest.
Arguments:
- hidden_in: bfloat16 [4, 1024, 2048], P(('dp', 'ep'))
- expert_ids: int32 [4, 1024, 8], P(('dp', 'ep'))
- slot_ids: int32 [4, 1024, 8], P(('dp', 'ep'))
- attn_gain: bfloat16 [2048], replicated
- w_query: bfloat16 [2048, 16, 128], P(None, 'tp')
- w_key: bfloat16 [2048, 16, 128], P(None, 'tp')
- w_value: bfloat16 [2048, 16, 128], P(None, 'tp')
- w_out: bfloat16 [16, 128, 2048], P('tp')
- ffn_gain: bfloat16 [2048], replicated
- w_gate: bfloat16 [2048, 8192], P(None, 'tp')
- w_up: bfloat16 [2048, 8192], P(None, 'tp')
- w_down: bfloat16 [8192, 2048], P('tp')
- moe_gain: bfloat16 [2048], replicated
- w_router: bfloat16 [2048, 64], replicated
- exp_gate: bfloat16 [64, 2048, 1024], P('ep')
- exp_up: bfloat16 [64, 2048, 1024], P('ep')
- exp_down: bfloat16 [64, 1024, 2048], P('ep')
Outputs:
- output: bfloat16 [4, 1024, 2048], P(('dp', 'ep'))
All inputs are finite; a program needn't handle non-finite values.
Results may differ from a plain program's by a relative error of at most 0.00923202.
Values are sent between devices in bfloat16 or wider.
A program may use at most 1.25 GiB of HBM per device.

v0:
```python
import functools
import jax
import jax.numpy as jnp
from jax import lax
from jax.experimental import pallas as pl
from jax.experimental.pallas import tpu as pltpu
from jax.sharding import PartitionSpec as P

EPS = 1e-6
ROPE_BASE = 10000.0
F32 = jnp.float32
BF16 = jnp.bfloat16
SEG = 16
GT = 128
OUT = 96
CHUNKS = 4
CT = 256
VMEM_BIG = 60 * 1024 * 1024


def inv_rms_of(x_f32):
    return lax.rsqrt(jnp.mean(x_f32 * x_f32, axis=-1, keepdims=True) + EPS)


def rms_norm(x_val, gain):
    x_f32 = x_val.astype(F32)
    return (x_f32 * inv_rms_of(x_f32) * gain.astype(F32)).astype(BF16)


def rope_tables(seq_len, head_dim):
    inv_freq = ROPE_BASE ** (-jnp.arange(head_dim // 2, dtype=F32) * (2.0 / head_dim))
    angle = jnp.arange(seq_len, dtype=F32)[:, None] * inv_freq[None, :]
    cos_tab, sin_tab = jnp.cos(angle), jnp.sin(angle)
    return jnp.concatenate([cos_tab, cos_tab], axis=1), jnp.concatenate([-sin_tab, sin_tab], axis=1)


def attn_kernel(q_ref, k_ref, v_ref, cos_ref, sin_ref, o_ref, k_scr):
    seq, hd = q_ref.shape
    blk = 256
    cos_t, sin_t = cos_ref[...], sin_ref[...]
    k_f = k_ref[...]
    k_scr[...] = (k_f * cos_t + pltpu.roll(k_f, hd // 2, 1) * sin_t).astype(BF16)
    for i in range(seq // blk):
        rows = slice(i * blk, (i + 1) * blk)
        q_f = q_ref[rows, :]
        q_b = (q_f * cos_t[rows] + pltpu.roll(q_f, hd // 2, 1) * sin_t[rows]).astype(BF16)
        kv = (i + 1) * blk
        s = lax.dot_general(q_b, k_scr[:kv, :], (((1,), (1,)), ((), ())), preferred_element_type=F32) * hd ** -0.5
        r_id = lax.broadcasted_iota(jnp.int32, (blk, kv), 0) + i * blk
        c_id = lax.broadcasted_iota(jnp.int32, (blk, kv), 1)
        s = jnp.where(r_id >= c_id, s, -1e30)
        p = jnp.exp(s - jnp.max(s, axis=1, keepdims=True))
        p = (p * (1.0 / jnp.sum(p, axis=1, keepdims=True))).astype(BF16)
        o_ref[rows, :] = jnp.dot(p, v_ref[:kv, :], preferred_element_type=F32).astype(BF16)


def attention(q, k, v, cos_t, sin_t, head_dim):
    seq, width = q.shape
    heads = width // head_dim
    col = pl.BlockSpec((seq, head_dim), lambda h: (0, h))
    tab = pl.BlockSpec((seq, head_dim), lambda h: (0, 0))
    return pl.pallas_call(
        attn_kernel, grid=(heads,),
        in_specs=[col, col, col, tab, tab], out_specs=col,
        out_shape=jax.ShapeDtypeStruct((seq, width), BF16),
        scratch_shapes=[pltpu.VMEM((seq, head_dim), BF16)],
        cost_estimate=pl.CostEstimate(flops=heads * seq * seq * head_dim * 4, bytes_accessed=12 * seq * width, transcendentals=heads * seq * seq),
        name="attn",
    )(q, k, v, cos_t, sin_t)


def expert_kernel(n_ref, loc_ref, dst_ref, rank_ref, u0_ref, u1_ref, u2_ref, u3_ref, wg_ref, wu_ref, wd_ref, _after, y_hbm, x_scr, h_scr, y_scr, sem):
    e = pl.program_id(0)
    u_refs = (u0_ref, u1_ref, u2_ref, u3_ref)
    half, d = u0_ref.shape
    fe = wg_ref.shape[2]

    for s in range(4):
        n = n_ref[s, e]
        base = loc_ref[s, e]
        rank_row = rank_ref[s, 0]
        for i in range(2):
            @pl.when(n > i * GT)
            def _():
                rid = lax.broadcasted_iota(jnp.int32, (GT, half), 0) + i * GT
                hot = (rank_row == rid).astype(F32).astype(BF16)
                x_scr[pl.ds(pl.multiple_of(base + i * GT, SEG), GT), :] = jnp.dot(hot, u_refs[s][...], preferred_element_type=F32).astype(BF16)

    total = loc_ref[3, e] + lax.shift_right_logical(n_ref[3, e] + (SEG - 1), 4) * SEG

    def copies(fn, ee):
        for s in range(4):
            for i in range(2):
                @pl.when(n_ref[s, ee] > i * OUT)
                def _():
                    fn(pltpu.make_async_copy(
                        y_scr.at[pl.ds(pl.multiple_of(loc_ref[s, ee] + i * OUT, SEG), OUT), :],
                        y_hbm.at[s, pl.ds(pl.multiple_of(dst_ref[s, ee] + i * OUT, SEG), OUT), :], sem))

    @pl.when(e > 0)
    def _():
        copies(lambda c: c.wait(), e - 1)

    def ffn(m0, rows):
        for c in range(fe // 512):
            cols = slice(c * 512, (c + 1) * 512)
            x = x_scr[pl.ds(m0, rows), :]
            g = jnp.dot(x, wg_ref[0, :, cols], preferred_element_type=F32)
            v = jnp.dot(x, wu_ref[0, :, cols], preferred_element_type=F32)
            h_scr[pl.ds(0, rows), cols] = (g * jax.nn.sigmoid(g) * v).astype(BF16)
        for c in range(d // 1024):
            cols = slice(c * 1024, (c + 1) * 1024)
            y_scr[pl.ds(m0, rows), cols] = jnp.dot(h_scr[pl.ds(0, rows), :], wd_ref[0, :, cols], preferred_element_type=F32).astype(BF16)

    for lo, hi in ((256, 320), (320, 384)):
        @pl.when((total > lo) & (total <= hi))
        def _():
            ffn(0, hi)

    @pl.when((total <= 256) | (total > 384))
    def _():
        def body(i, carry):
            ffn(pl.multiple_of(i * 256, 256), 256)
            return carry

        lax.fori_loop(0, lax.shift_right_logical(total + 255, 8), body, 0)

    copies(lambda c: c.start(), e)

    @pl.when(e == pl.num_programs(0) - 1)
    def _():
        copies(lambda c: c.wait(), e)


def run_experts(n, loc, dst, rank_t, u_four, wg, wu, wd, cap_src, after):
    half, d = u_four[0].shape
    n_exp, _, fe = wg.shape
    whole = pl.BlockSpec((half, d), lambda e, *_: (0, 0), pipeline_mode=pl.Buffered(1))
    grid_spec = pltpu.PrefetchScalarGridSpec(
        num_scalar_prefetch=3, grid=(n_exp,),
        in_specs=[
            pl.BlockSpec((4, 1, 1, half), lambda e, *_: (0, e, 0, 0)),
            whole, whole, whole, whole,
            pl.BlockSpec((1, d, fe), lambda e, *_: (e, 0, 0)),
            pl.BlockSpec((1, d, fe), lambda e, *_: (e, 0, 0)),
            pl.BlockSpec((1, fe, d), lambda e, *_: (e, 0, 0)),
            pl.BlockSpec(memory_space=pl.ANY),
        ],
        out_specs=pl.BlockSpec(memory_space=pl.ANY),
        scratch_shapes=[pltpu.VMEM((1024, d), BF16), pltpu.VMEM((384, fe), BF16), pltpu.VMEM((1024, d), BF16), pltpu.SemaphoreType.DMA],
    )
    return pl.pallas_call(
        expert_kernel, grid_spec=grid_spec,
        out_shape=jax.ShapeDtypeStruct((4, cap_src + 256, d), BF16),
        compiler_params=pltpu.CompilerParams(vmem_limit_bytes=VMEM_BIG),
        cost_estimate=pl.CostEstimate(flops=90_000_000_000, bytes_accessed=n_exp * d * fe * 6 + 40_000_000, transcendentals=0),
        name="experts",
    )(n, loc, dst, rank_t, *u_four, wg, wu, wd, after)


def combine_kernel(src, has_init, rows_ref, pos_ref, gate_ref, y_hbm, _after, *rest):
    init_ref = rest[0] if has_init else None
    *o_refs, y_buf, g_scr, sems = rest[1:] if has_init else rest
    half, top_k = pos_ref.shape
    rc, d = o_refs[0].shape
    n_rows = rows_ref[src]
    n_tiles = lax.shift_right_logical(n_rows + (CT - 1), 8)

    def fetch(i, slot):
        return pltpu.make_async_copy(y_hbm.at[src, pl.ds(pl.multiple_of(i * CT, CT), CT), :], y_buf.at[slot], sems.at[slot])

    @pl.when(n_tiles > 0)
    def _():
        fetch(0, 0).start()

    for k, o_ref in enumerate(o_refs):
        o_ref[...] = init_ref[k * rc:(k + 1) * rc, :] if has_init else jnp.zeros_like(o_ref)

    def body(i, carry):
        slot = lax.rem(i, 2)

        @pl.when(i + 1 < n_tiles)
        def _():
            fetch(i + 1, 1 - slot).start()

        rid = lax.broadcasted_iota(jnp.int32, (half, CT), 1) + i * CT
        g = jnp.zeros((half, CT), F32)
        for j in range(top_k):
            g = jnp.where(pos_ref[:, j:j + 1] == rid, gate_ref[:, j:j + 1], g)
        hi = g.astype(BF16)
        left = g - hi.astype(F32)
        mid = left.astype(BF16)
        g_scr[:, :CT] = (left - mid.astype(F32)).astype(BF16)
        g_scr[:, CT:2 * CT] = mid
        g_scr[:, 2 * CT:] = hi
        fetch(i, slot).wait()

        @pl.when(i == n_tiles - 1)
        def _():
            live = lax.broadcasted_iota(jnp.int32, (CT, 1), 0) + i * CT < n_rows
            y_buf[slot] = jnp.where(live, y_buf[slot].astype(F32), 0.0).astype(BF16)

        for c in range(d // 512):
            cols = slice(c * 512, (c + 1) * 512)
            y = y_buf[slot, :, cols]
            part = jnp.dot(g_scr[...], jnp.concatenate([y, y, y], axis=0), preferred_element_type=F32)
            for k, o_ref in enumerate(o_refs):
                o_ref[:, cols] += part[k * rc:(k + 1) * rc]
        return carry

    lax.fori_loop(0, n_tiles, body, 0)


def run_combine(src, rows, pos, gates, y_all, after, init=None, n_out=1):
    d = y_all.shape[2]
    half, top_k = pos.shape[1:]
    full = pl.BlockSpec((half, d), lambda i, r: (0, 0))
    small = pl.BlockSpec((half, top_k), lambda i, r: (0, 0))
    anywhere = pl.BlockSpec(memory_space=pl.ANY)
    extra = [] if init is None else [init]
    grid_spec = pltpu.PrefetchScalarGridSpec(
        num_scalar_prefetch=1, grid=(1,),
        in_specs=[small, small, anywhere, anywhere] + [full for _ in extra],
        out_specs=[pl.BlockSpec((half // n_out, d), lambda i, r: (0, 0))] * n_out,
        scratch_shapes=[pltpu.VMEM((2, CT, d), BF16), pltpu.VMEM((half, 3 * CT), BF16), pltpu.SemaphoreType.DMA((2,))],
    )
    return pl.pallas_call(
        functools.partial(combine_kernel, src, init is not None), grid_spec=grid_spec,
        out_shape=[jax.ShapeDtypeStruct((half // n_out, d), F32)] * n_out,
        compiler_params=pltpu.CompilerParams(vmem_limit_bytes=40 * 1024 * 1024),
        cost_estimate=pl.CostEstimate(flops=12_000_000_000, bytes_accessed=10_000_000, transcendentals=0),
    )(rows, pos[src], gates[src], y_all, after, *extra)


def out_kernel(q_ref, x_ref, gain_ref, ctx_ref, peer_ref, wo_ref, w0_ref, w1_ref, w2_ref, w3_ref, _after, a_ref, n_ref):
    quarter = w0_ref.shape[0]
    o = jnp.dot(ctx_ref[...], wo_ref[...], preferred_element_type=F32)
    p = None
    for r, w in enumerate((w0_ref, w1_ref, w2_ref, w3_ref)):
        cols = pl.ds(pl.multiple_of(q_ref[r] * quarter, quarter), quarter)
        t = jnp.dot(peer_ref[:, cols], w[...], preferred_element_type=F32)
        p = t if p is None else p + t
    after = (x_ref[...].astype(F32) + (o + p)).astype(BF16)
    a_ref[...] = after
    a_f = after.astype(F32)
    inv = lax.rsqrt(jnp.mean(a_f * a_f, axis=1, keepdims=True) + EPS)
    n_ref[...] = (a_f * inv * gain_ref[...].astype(F32)).astype(BF16)


def run_out(quarters, x2, gain, ctx, ctx_peer, w_o, pieces, after):
    seq, d = x2.shape
    width = w_o.shape[0]
    blk = 256
    row = lambda n: pl.BlockSpec((blk, n), lambda i, q: (i, 0))
    const = lambda m, n: pl.BlockSpec((m, n), lambda i, q: (0, 0), pipeline_mode=pl.Buffered(1))
    grid_spec = pltpu.PrefetchScalarGridSpec(
        num_scalar_prefetch=1, grid=(seq // blk,),
        in_specs=[row(d), const(1, d), row(width), row(width), const(width, d)] + [const(width // 4, d)] * 4 + [pl.BlockSpec(memory_space=pl.ANY)],
        out_specs=[row(d), row(d)],
    )
    return pl.pallas_call(
        out_kernel, grid_spec=grid_spec,
        out_shape=[jax.ShapeDtypeStruct((seq, d), BF16)] * 2,
        compiler_params=pltpu.CompilerParams(vmem_limit_bytes=VMEM_BIG),
        cost_estimate=pl.CostEstimate(flops=10_000_000_000, bytes_accessed=24_000_000, transcendentals=0),
        name="out_proj",
    )(quarters, x2, gain.reshape(1, d), ctx, ctx_peer, w_o, *pieces, after)


def ffn_kernel(n_out, has_add, off_ref, x_ref, wg_ref, wu_ref, wd_ref, _after, *rest):
    add_ref = rest[0] if has_add else None
    outs = rest[1:] if has_add else rest
    o_refs, acc = outs[:n_out], outs[n_out]
    i = pl.program_id(0)
    x = x_ref[...]
    g = jnp.dot(x, wg_ref[...], preferred_element_type=F32)
    u = jnp.dot(x, wu_ref[...], preferred_element_type=F32)
    h = (g * jax.nn.sigmoid(g) * u).astype(BF16)
    part = jnp.dot(h, wd_ref[...], preferred_element_type=F32)

    @pl.when(i == 0)
    def _():
        acc[...] = part

    @pl.when(i > 0)
    def _():
        acc[...] += part

    @pl.when(i == pl.num_programs(0) - 1)
    def _():
        rows = acc.shape[0] // n_out
        for k, o_ref in enumerate(o_refs):
            v = acc[k * rows:(k + 1) * rows, :]
            if has_add:
                v = add_ref[k * rows:(k + 1) * rows, :].astype(F32) + v
            o_ref[...] = v


def run_ffn(which, f_norm, wg, wu, wd, after, add=None, n_out=4):
    seq, d = f_norm.shape
    half = seq // 2
    ff = wg.shape[1]
    blk = 512
    extra = [] if add is None else [add]
    mine = pl.BlockSpec((half, d), lambda i, w: (w[0], 0), pipeline_mode=pl.Buffered(1))
    grid_spec = pltpu.PrefetchScalarGridSpec(
        num_scalar_prefetch=1, grid=(ff // blk,),
        in_specs=[mine,
                  pl.BlockSpec((d, blk), lambda i, w: (0, i)), pl.BlockSpec((d, blk), lambda i, w: (0, i)),
                  pl.BlockSpec((blk, d), lambda i, w: (i, 0)), pl.BlockSpec(memory_space=pl.ANY)] + [mine for _ in extra],
        out_specs=[pl.BlockSpec((half // n_out, d), lambda i, w: (0, 0))] * n_out,
        scratch_shapes=[pltpu.VMEM((half, d), F32)],
    )
    return pl.pallas_call(
        functools.partial(ffn_kernel, n_out, add is not None), grid_spec=grid_spec,
        out_shape=[jax.ShapeDtypeStruct((half // n_out, d), F32)] * n_out,
        compiler_params=pltpu.CompilerParams(vmem_limit_bytes=VMEM_BIG),
        cost_estimate=pl.CostEstimate(flops=28_000_000_000, bytes_accessed=60_000_000, transcendentals=0),
        name="ffn",
    )(which.reshape(1), f_norm, wg, wu, wd, after, *extra)


def solution(mesh):
    tok_spec = P(('dp', 'ep'), None, None)
    col_spec = P(None, 'tp', None)
    exp_spec = P('ep', None, None)
    in_specs = (tok_spec, tok_spec, tok_spec, P(None), col_spec, col_spec, col_spec, P('tp', None, None), P(None), P(None, 'tp'), P(None, 'tp'), P('tp', None), P(None), P(None, None), exp_spec, exp_spec, exp_spec)
    n_ep, n_tp = mesh.shape['ep'], mesh.shape['tp']
    assert n_ep == 4 and n_tp == 2

    def over_x(v):
        return lax.ppermute(v, 'ep', [(i, i ^ 2) for i in range(4)])

    def over_core(v):
        return lax.ppermute(v, 'ep', [(i, i ^ 1) for i in range(4)])

    def over_tp(v):
        return lax.ppermute(v, 'tp', [(0, 1), (1, 0)])

    def layer(hidden_in, expert_ids, slot_ids, attn_gain, w_query, w_key, w_value, w_out, ffn_gain, w_gate, w_up, w_down, moe_gain, w_router, exp_gate, exp_up, exp_down):
        seq, d = hidden_in.shape[1:]
        top_k = expert_ids.shape[2]
        n_all = w_router.shape[1]
        n_exp = exp_gate.shape[0]
        half = seq // 2
        my_tp = lax.axis_index('tp')
        my_ep = lax.axis_index('ep')
        x2 = hidden_in.reshape(seq, d)
        ids = expert_ids.reshape(seq, top_k)

        width = w_out.shape[0] * w_out.shape[1]
        w_o = w_out.reshape(width, d)
        quarter = width // 4
        w_q0 = over_tp(lax.dynamic_slice(w_o, (my_ep * quarter, 0), (quarter, d)))

        x_half = lax.dynamic_slice(x2, (my_tp * half, 0), (half, d))
        ids_half = lax.dynamic_slice(ids, (my_tp * half, 0), (half, top_k))
        u_half = rms_norm(x_half, moe_gain)
        u_x = over_x(u_half)
        u_c = over_core(u_half)
        logits = jnp.dot(u_half, w_router, preferred_element_type=F32)
        is_e = ids_half[:, :, None] == jnp.arange(n_all, dtype=jnp.int32)[None, None, :]
        picked = jnp.sum(jnp.where(is_e, logits[:, None, :], 0.0), axis=2)
        gates = jax.nn.softmax(picked, axis=-1)
        meta = jnp.concatenate([ids_half.astype(F32), gates], axis=1)
        meta_x = over_x(meta)
        meta2 = jnp.stack([meta, meta_x])
        meta_all = jnp.concatenate([meta2, over_core(meta2)])
        u_d = over_core(u_x)
        w_q1 = over_x(w_q0)
        w_q2 = over_core(w_q0)
        w_q3 = over_core(w_q1)

        ids_loc = meta_all[:, :, :top_k].astype(jnp.int32) - my_ep * n_exp
        gates_all = meta_all[:, :, top_k:]
        ids_t = jnp.swapaxes(ids_loc, 1, 2)
        e_ids = jnp.arange(n_exp, dtype=jnp.int32)
        sel_t = jnp.any(ids_t[:, None, :, :] == e_ids[None, :, None, None], axis=2)
        before = (jnp.arange(half)[:, None] < jnp.arange(half)[None, :]).astype(BF16)
        rank_f = jnp.dot(sel_t.reshape(-1, half).astype(BF16), before, preferred_element_type=F32).reshape(4, n_exp, half)
        n = jnp.sum(sel_t.astype(jnp.int32), axis=2)
        seg = (n + SEG - 1) // SEG * SEG
        lower4 = jnp.arange(4)[:, None] > jnp.arange(4)[None, :]
        loc = jnp.sum(jnp.where(lower4[:, :, None], seg[None], 0), axis=1)
        lower_e = jnp.arange(n_exp)[:, None] > jnp.arange(n_exp)[None, :]
        dst = jnp.sum(jnp.where(lower_e[None], seg[:, None, :], 0), axis=2)
        rows = jnp.sum(seg, axis=1)
        rank_i = rank_f.astype(jnp.int32)
        rank_t = jnp.where(sel_t, rank_i, -1)[:, :, None, :]
        pos_e = jnp.swapaxes(rank_i + dst[:, :, None], 1, 2)
        hit = ids_loc[..., None] == e_ids
        pos = jnp.sum(jnp.where(hit, pos_e[:, :, None, :] + 1, 0), axis=3) - 1

        x_norm = rms_norm(x2, attn_gain)
        hd = w_query.shape[2]
        q = jnp.dot(x_norm, w_query.reshape(d, width), preferred_element_type=F32)
        k = jnp.dot(x_norm, w_key.reshape(d, width), preferred_element_type=F32)
        v = jnp.dot(x_norm, w_value.reshape(d, width), preferred_element_type=F32).astype(BF16)
        cos_t, sin_t = rope_tables(seq, hd)
        ctx = attention(q, k, v, cos_t, sin_t, hd)
        ctx_peer = over_tp(ctx)

        cap_src = n_exp * (3 * seq * top_k // (2 * n_all))
        y_all = run_experts(n, loc, dst, rank_t, (u_half, u_x, u_c, u_d), exp_gate, exp_up, exp_down, cap_src, ctx)
        m3, = run_combine(3, rows, pos, gates_all, y_all, y_all)
        got3 = over_core(m3)

        quarters = my_ep ^ jnp.arange(4, dtype=jnp.int32)
        after, f_norm = run_out(quarters, x2, ffn_gain, ctx, ctx_peer, w_o, (w_q0, w_q2, w_q1, w_q3), m3)
        f_far = run_ffn(1 - my_tp, f_norm, w_gate, w_up, w_down, after)
        f_got = [over_tp(c) for c in f_far]

        m1 = run_combine(1, rows, pos, gates_all, y_all, f_far[0], init=got3, n_out=CHUNKS)
        m_x = [over_x(c) for c in m1]
        m2, = run_combine(2, rows, pos, gates_all, y_all, m1[0])
        got2 = over_core(m2)
        f_own = run_ffn(my_tp, f_norm, w_gate, w_up, w_down, m2, add=after)
        m0 = run_combine(0, rows, pos, gates_all, y_all, f_own[0], init=got2, n_out=CHUNKS)
        own, peer = [], []
        for c in range(CHUNKS):
            o_c = ((f_own[c] + f_got[c]) + (m0[c] + m_x[c])).astype(BF16)
            own.append(o_c)
            peer.append(over_tp(o_c))
        first = my_tp == 0
        out = jnp.concatenate([jnp.where(first, a, b) for a, b in zip(own, peer)] + [jnp.where(first, b, a) for a, b in zip(own, peer)], axis=0)
        return out.reshape(1, seq, d)

    return jax.shard_map(layer, mesh=mesh, in_specs=in_specs, out_specs=tok_spec, check_vma=False)
```

profile of v0, /device:TPU:0, one launch (start us, length us, event | category | flops | bytes accessed | tf_op | source)
XLA Modules:
  0.0 518.2 jit_solution(11556822908707056745)
XLA Ops:
  0.7 2.1 fusion
  2.8 2.1 fusion.2.u0_ref
  5.0 3.3 collective-permute-start.7
  9.6 3.2 multiply_reduce_fusion
  13.0 8.8 %fusion.10.q_ref = f32[1024,1024]{1,0:T(8,128)} fusion(bf16[256,8,8,128]{3,2,1,0:T(8,128)(2,1)} %bitcast.71, bf16[1,1024,2048]{2,1,0:T(8,128)(2,1)S(1)} %copy-done.10, f32[2048]{0:T(1024)S(1)} %convert_element_type.64, f32[1024]{0:T(1024)S(1)} %add_rsqrt_fusion), kind=kOutput, calls=%fused_computation.14 | convolution fusion | flops 4303355904 | bytes 12595200 | tf_op jit(solution)/shard_map/dot_general | solution.py:396
  21.8 6.2 %fusion.7.k_ref = f32[1024,1024]{1,0:T(8,128)} fusion(bf16[256,8,8,128]{3,2,1,0:T(8,128)(2,1)S(1)} %bitcast.72, bf16[1,1024,2048]{2,1,0:T(8,128)(2,1)S(1)} %copy-done.10, f32[2048]{0:T(1024)S(1)} %convert_element_type.64, f32[1024]{0:T(1024)S(1)} %add_rsqrt_fusion), kind=kOutput, calls=%fused_computation.11 | convolution fusion | flops 4303355904 | bytes 12595200 | tf_op jit(solution)/shard_map/dot_general | solution.py:397
  31.3 5.8 %fusion.13.v_ref = bf16[1024,1024]{1,0:T(8,128)(2,1)} fusion(bf16[256,8,8,128]{3,2,1,0:T(8,128)(2,1)S(1)} %bitcast.73, bf16[1,1024,2048]{2,1,0:T(8,128)(2,1)S(1)} %copy-done.10, f32[2048]{0:T(1024)S(1)} %convert_element_type.64, f32[1024]{0:T(1024)S(1)} %add_rsqrt_fusion), kind=kOutput, calls=%fused_computation.17 | convolution fusion | flops 4304404480 | bytes 10498048 | tf_op jit(solution)/shard_map/dot_general | solution.py:398
  37.1 21.5 %attn.1._after.ctx_ref = bf16[1024,1024]{1,0:T(8,128)(2,1)} custom-call(f32[1024,1024]{1,0:T(8,128)} %fusion.10.q_ref, f32[1024,1024]{1,0:T(8,128)} %fusion.7.k_ref, bf16[1024,1024]{1,0:T(8,128)(2,1)} %fusion.13.v_ref, f32[1024,128]{1,0:T(8,128)} %get-tuple-element.56.cos_ref, f32[1024,128]{1,0:T(8,128)} %get-tuple-element.57.sin_ref), custom_call_target="tpu_custom_call" | custom-call | flops 4294967296 | bytes 12582912 | tf_op jit(solution)/shard_map/attn/pallas_call | solution.py:62
  60.7 2.3 constant_dynamic-slice_fusion
  67.2 62.2 %collective-permute-done.1.w0_ref = bf16[256,2048]{1,0:T(8,128)(2,1)} collective-permute-done((bf16[256,2048]{1,0:T(8,128)(2,1)}, bf16[256,2048]{1,0:T(8,128)(2,1)}, u32[]{:S(2)}, u32[]{:S(2)}) %collective-permute-start.1) | collective-permute-done | bytes 1048608 | tf_op jit(solution)/shard_map/ppermute | solution.py:338
  135.4 19.0 %collective-permute-done.3.w2_ref = bf16[256,2048]{1,0:T(8,128)(2,1)} collective-permute-done((bf16[256,2048]{1,0:T(8,128)(2,1)}, bf16[256,2048]{1,0:T(8,128)(2,1)}, u32[]{:S(2)}, u32[]{:S(2)}) %collective-permute-start.3) | collective-permute-done | bytes 1048608 | tf_op jit(solution)/shard_map/ppermute | solution.py:332
  154.4 108.1 %experts.1.y_hbm._after = bf16[4,3328,2048]{2,1,0:T(8,128)(2,1)} custom-call(s32[4,16]{1,0:T(4,128)} %copy-done.21, s32[4,16]{1,0:T(4,128)} %select_reduce_fusion.3.loc_ref, s32[4,16]{1,0:T(4,128)} %copy-done.24, s32[4,16,1,512]{3,2,1,0:T(1,128)} %broadcast_in_dim.109.rank_ref, bf16[512,2048]{1,0:T(8,128)(2,1)} %copy-done.11, ...), custom_call_target="tpu_custom_call" | custom-call | flops 89999998976 | bytes 241326592 | tf_op jit(solution)/shard_map/experts/pallas_call | solution.py:152
  262.5 19.2 %shard_map.154._after = f32[512,2048]{1,0:T(8,128)} custom-call(s32[4]{0:T(128)S(1)} %get-tuple-element.41.rows_ref, s32[512,8]{1,0:T(8,128)S(1)} %get-tuple-element.48.pos_ref, f32[512,8]{1,0:T(8,128)S(1)} %get-tuple-element.50.gate_ref, bf16[4,3328,2048]{2,1,0:T(8,128)(2,1)} %experts.1.y_hbm._after, bf16[4,3328,2048]{2,1,0:T(8,128)(2,1)} %experts.1.y_hbm._after), custom_call_target="tpu_custom_call" | custom-call | flops 12000000000 | bytes 10000000 | tf_op jit(solution)/shard_map/pallas_call | solution.py:227
  283.0 16.7 %out_proj.1 = (bf16[1024,2048]{1,0:T(8,128)(2,1)}, bf16[1024,2048]{1,0:T(8,128)(2,1)}) custom-call(s32[4]{0:T(128)} %iota_xor_fusion.q_ref, bf16[1024,2048]{1,0:T(8,128)(2,1)} %bitcast.62, bf16[1,2048]{1,0:T(2,128)(2,1)} %reshape.174.gain_ref, bf16[1024,1024]{1,0:T(8,128)(2,1)} %attn.1._after.ctx_ref, bf16[1024,1024]{1,0:T(8,128)(2,1)} %collective-permute-done.peer_ref, ...), custom_call_target="tpu_custom_call" | custom-call | flops 10000000000 | bytes 24000000 | tf_op jit(solution)/shard_map/out_proj/pallas_call | solution.py:261
  299.7 37.1 %ffn.2 = (f32[128,2048]{1,0:T(8,128)}, f32[128,2048]{1,0:T(8,128)}, f32[128,2048]{1,0:T(8,128)}, f32[128,2048]{1,0:T(8,128)}) custom-call(s32[1]{0:T(128)} %bitcast.18.off_ref, bf16[1024,2048]{1,0:T(8,128)(2,1)} %get-tuple-element.23.x_ref, bf16[2048,4096]{1,0:T(8,128)(2,1)} %wg_ref.5, bf16[2048,4096]{1,0:T(8,128)(2,1)} %wu_ref.5, ...), custom_call_target="tpu_custom_call" | custom-call | flops 28000000000 | bytes 60000000 | tf_op jit(solution)/shard_map/ffn/pallas_call | solution.py:314
  338.0 19.3 %shard_map.155 = (f32[128,2048]{1,0:T(8,128)S(1)}, f32[128,2048]{1,0:T(8,128)S(1)}, f32[128,2048]{1,0:T(8,128)S(1)}, f32[128,2048]{1,0:T(8,128)S(1)}) custom-call(s32[4]{0:T(128)S(1)} %get-tuple-element.41.rows_ref, s32[512,8]{1,0:T(8,128)S(1)} %get-tuple-element.45.pos_ref, f32[512,8]{1,0:T(8,128)S(1)} %slice_bitcast_fusion.2.gate_ref, ...), custom_call_target="tpu_custom_call" | custom-call | flops 12000000000 | bytes 10000000 | tf_op jit(solution)/shard_map/pallas_call | solution.py:227
  357.4 19.6 %shard_map.156._after = f32[512,2048]{1,0:T(8,128)} custom-call(s32[4]{0:T(128)S(1)} %get-tuple-element.41.rows_ref, s32[512,8]{1,0:T(8,128)S(1)} %get-tuple-element.47.pos_ref, f32[512,8]{1,0:T(8,128)S(1)} %get-tuple-element.49.gate_ref, bf16[4,3328,2048]{2,1,0:T(8,128)(2,1)} %experts.1.y_hbm._after, f32[128,2048]{1,0:T(8,128)S(1)} %get-tuple-element.26._after), custom_call_target="tpu_custom_call" | custom-call | flops 12000000000 | bytes 10000000 | tf_op jit(solution)/shard_map/pallas_call | solution.py:227
  381.2 6.6 %collective-permute-start.13 = (f32[128,2048]{1,0:T(8,128)S(1)}, f32[128,2048]{1,0:T(8,128)}, u32[]{:S(2)}, u32[]{:S(2)}) collective-permute-start(f32[128,2048]{1,0:T(8,128)S(1)} %get-tuple-element.26._after), channel_id=1, source_target_pairs={{0,2},{1,3},{2,0},{3,1},{4,6},{5,7},{6,4},{7,5}} | collective-permute-start | bytes 3145736 | tf_op jit(solution)/shard_map/ppermute | solution.py:332
  387.8 37.8 %ffn.3 = (f32[128,2048]{1,0:T(8,128)}, f32[128,2048]{1,0:T(8,128)}, f32[128,2048]{1,0:T(8,128)}, f32[128,2048]{1,0:T(8,128)}) custom-call(s32[1]{0:T(128)} %bitcast.off_ref, bf16[1024,2048]{1,0:T(8,128)(2,1)} %get-tuple-element.23.x_ref, bf16[2048,4096]{1,0:T(8,128)(2,1)} %wg_ref.5, bf16[2048,4096]{1,0:T(8,128)(2,1)} %wu_ref.5, bf16[4096,2048]{1,0:T(8,128)(2,1)} %wd_ref.5, ...), custom_call_target="tpu_custom_call" | custom-call | flops 28000000000 | bytes 60000000 | tf_op jit(solution)/shard_map/ffn/pallas_call | solution.py:314
  426.8 19.4 %shard_map.157 = (f32[128,2048]{1,0:T(8,128)S(1)}, f32[128,2048]{1,0:T(8,128)S(1)}, f32[128,2048]{1,0:T(8,128)S(1)}, f32[128,2048]{1,0:T(8,128)S(1)}) custom-call(s32[4]{0:T(128)S(1)} %get-tuple-element.41.rows_ref, s32[512,8]{1,0:T(8,128)S(1)} %get-tuple-element.46.pos_ref, f32[512,8]{1,0:T(8,128)S(1)} %slice_bitcast_fusion.gate_ref, ...), custom_call_target="tpu_custom_call" | custom-call | flops 12000000000 | bytes 10000000 | tf_op jit(solution)/shard_map/pallas_call | solution.py:227
  455.3 18.8 %collective-permute-done.19 = f32[128,2048]{1,0:T(8,128)S(1)} collective-permute-done((f32[128,2048]{1,0:T(8,128)S(1)}, f32[128,2048]{1,0:T(8,128)S(1)}, u32[]{:S(2)}, u32[]{:S(2)}) %collective-permute-start.19) | collective-permute-done | bytes 1048608 | tf_op jit(solution)/shard_map/ppermute | solution.py:332
  475.9 18.8 %collective-permute-done.22 = f32[128,2048]{1,0:T(8,128)S(1)} collective-permute-done((f32[128,2048]{1,0:T(8,128)S(1)}, f32[128,2048]{1,0:T(8,128)S(1)}, u32[]{:S(2)}, u32[]{:S(2)}) %collective-permute-start.22) | collective-permute-done | bytes 1048608 | tf_op jit(solution)/shard_map/ppermute | solution.py:332
  495.6 10.4 %collective-permute-done.20 = bf16[128,2048]{1,0:T(8,128)(2,1)S(1)} collective-permute-done((bf16[128,2048]{1,0:T(8,128)(2,1)S(1)}, bf16[128,2048]{1,0:T(8,128)(2,1)S(1)}, u32[]{:S(2)}, u32[]{:S(2)}) %collective-permute-start.20) | collective-permute-done | bytes 524320 | tf_op jit(solution)/shard_map/ppermute | solution.py:338
  506.2 9.2 %collective-permute-done.23 = bf16[128,2048]{1,0:T(8,128)(2,1)S(1)} collective-permute-done((bf16[128,2048]{1,0:T(8,128)(2,1)S(1)}, bf16[128,2048]{1,0:T(8,128)(2,1)S(1)}, u32[]{:S(2)}, u32[]{:S(2)}) %collective-permute-start.23) | collective-permute-done | bytes 524320 | tf_op jit(solution)/shard_map/ppermute | solution.py:338
  (147 shorter events, 39.9 us)
Async XLA Ops:
  5.0 58.9 %collective-permute-start.7 = (bf16[512,2048]{1,0:T(8,128)(2,1)S(1)}, bf16[512,2048]{1,0:T(8,128)(2,1)}, u32[]{:S(2)}, u32[]{:S(2)}) collective-permute-start(bf16[512,2048]{1,0:T(8,128)(2,1)S(1)} %fusion.2.u0_ref), channel_id=1, source_target_pairs={{0,2},{1,3},{2,0},{3,1},{4,6},{5,7},{6,4},{7,5}} | collective-permute-start | bytes 6291464 | tf_op jit(solution)/shard_map/ppermute | solution.py:332
  8.3 146.1 %collective-permute-start.8 = (bf16[512,2048]{1,0:T(8,128)(2,1)S(1)}, bf16[512,2048]{1,0:T(8,128)(2,1)}, u32[]{:S(2)}, u32[]{:S(2)}) collective-permute-start(bf16[512,2048]{1,0:T(8,128)(2,1)S(1)} %fusion.2.u0_ref), channel_id=1, source_target_pairs={{0,1},{1,0},{2,3},{3,2},{4,5},{5,4},{6,7},{7,6}} | collective-permute-start | bytes 6291464 | tf_op jit(solution)/shard_map/ppermute | solution.py:335
  9.5 53.5 %collective-permute-start.5 = (f32[512,16]{1,0:T(8,128)S(1)}, f32[512,16]{1,0:T(8,128)S(1)}, u32[]{:S(2)}, u32[]{:S(2)}) collective-permute-start(f32[512,16]{1,0:T(8,128)S(1)} %copy.33), channel_id=1, source_target_pairs={{0,2},{1,3},{2,0},{3,1},{4,6},{5,7},{6,4},{7,5}} | collective-permute-start | bytes 98312 | tf_op jit(solution)/shard_map/ppermute | solution.py:332
  58.6 224.4 %collective-permute-start = (bf16[1024,1024]{1,0:T(8,128)(2,1)}, bf16[1024,1024]{1,0:T(8,128)(2,1)}, u32[]{:S(2)}, u32[]{:S(2)}) collective-permute-start(bf16[1024,1024]{1,0:T(8,128)(2,1)} %attn.1._after.ctx_ref), channel_id=1, source_target_pairs={{0,4},{4,0},{1,5},{5,1},{2,6},{6,2},{3,7},{7,3}} | collective-permute-start | bytes 6291464 | tf_op jit(solution)/shard_map/ppermute | solution.py:338
  63.0 66.4 %collective-permute-start.1 = (bf16[256,2048]{1,0:T(8,128)(2,1)}, bf16[256,2048]{1,0:T(8,128)(2,1)}, u32[]{:S(2)}, u32[]{:S(2)}) collective-permute-start(bf16[256,2048]{1,0:T(8,128)(2,1)} %constant_dynamic-slice_fusion), channel_id=1, source_target_pairs={{0,4},{4,0},{1,5},{5,1},{2,6},{6,2},{3,7},{7,3}} | collective-permute-start | bytes 3145736 | tf_op jit(solution)/shard_map/ppermute | solution.py:338
  63.9 2.1 collective-permute-start.6
  63.9 90.5 %collective-permute-start.9 = (bf16[512,2048]{1,0:T(8,128)(2,1)}, bf16[512,2048]{1,0:T(8,128)(2,1)}, u32[]{:S(2)}, u32[]{:S(2)}) collective-permute-start(bf16[512,2048]{1,0:T(8,128)(2,1)} %collective-permute-done.7.u1_ref), channel_id=1, source_target_pairs={{0,1},{1,0},{2,3},{3,2},{4,5},{5,4},{6,7},{7,6}} | collective-permute-start | bytes 6291464 | tf_op jit(solution)/shard_map/ppermute | solution.py:335
  129.4 25.0 %collective-permute-start.3 = (bf16[256,2048]{1,0:T(8,128)(2,1)}, bf16[256,2048]{1,0:T(8,128)(2,1)}, u32[]{:S(2)}, u32[]{:S(2)}) collective-permute-start(bf16[256,2048]{1,0:T(8,128)(2,1)} %collective-permute-done.1.w0_ref), channel_id=1, source_target_pairs={{0,2},{1,3},{2,0},{3,1},{4,6},{5,7},{6,4},{7,5}} | collective-permute-start | bytes 3145736 | tf_op jit(solution)/shard_map/ppermute | solution.py:332
  135.4 147.6 %collective-permute-start.2 = (bf16[256,2048]{1,0:T(8,128)(2,1)}, bf16[256,2048]{1,0:T(8,128)(2,1)}, u32[]{:S(2)}, u32[]{:S(2)}) collective-permute-start(bf16[256,2048]{1,0:T(8,128)(2,1)} %collective-permute-done.1.w0_ref), channel_id=1, source_target_pairs={{0,1},{1,0},{2,3},{3,2},{4,5},{5,4},{6,7},{7,6}} | collective-permute-start | bytes 3145736 | tf_op jit(solution)/shard_map/ppermute | solution.py:335
  154.4 128.6 %collective-permute-start.4 = (bf16[256,2048]{1,0:T(8,128)(2,1)}, bf16[256,2048]{1,0:T(8,128)(2,1)}, u32[]{:S(2)}, u32[]{:S(2)}) collective-permute-start(bf16[256,2048]{1,0:T(8,128)(2,1)} %collective-permute-done.3.w2_ref), channel_id=1, source_target_pairs={{0,1},{1,0},{2,3},{3,2},{4,5},{5,4},{6,7},{7,6}} | collective-permute-start | bytes 3145736 | tf_op jit(solution)/shard_map/ppermute | solution.py:335
  281.7 55.1 %collective-permute-start.10 = (f32[512,2048]{1,0:T(8,128)}, f32[512,2048]{1,0:T(8,128)}, u32[]{:S(2)}, u32[]{:S(2)}) collective-permute-start(f32[512,2048]{1,0:T(8,128)} %shard_map.154._after), channel_id=1, source_target_pairs={{0,1},{1,0},{2,3},{3,2},{4,5},{5,4},{6,7},{7,6}} | collective-permute-start | bytes 12582920 | tf_op jit(solution)/shard_map/ppermute | solution.py:335
  377.1 48.5 %collective-permute-start.12 = (f32[512,2048]{1,0:T(8,128)}, f32[512,2048]{1,0:T(8,128)}, u32[]{:S(2)}, u32[]{:S(2)}) collective-permute-start(f32[512,2048]{1,0:T(8,128)} %shard_map.156._after), channel_id=1, source_target_pairs={{0,1},{1,0},{2,3},{3,2},{4,5},{5,4},{6,7},{7,6}} | collective-permute-start | bytes 12582920 | tf_op jit(solution)/shard_map/ppermute | solution.py:335
  377.7 68.5 %collective-permute-start.11 = (f32[128,2048]{1,0:T(8,128)S(1)}, f32[128,2048]{1,0:T(8,128)}, u32[]{:S(2)}, u32[]{:S(2)}) collective-permute-start(f32[128,2048]{1,0:T(8,128)S(1)} %copy-done.4), channel_id=1, source_target_pairs={{0,4},{4,0},{1,5},{5,1},{2,6},{6,2},{3,7},{7,3}} | collective-permute-start | bytes 3145736 | tf_op jit(solution)/shard_map/ppermute | solution.py:338
  379.2 71.1 %collective-permute-start.15 = (f32[128,2048]{1,0:T(8,128)}, f32[128,2048]{1,0:T(8,128)}, u32[]{:S(2)}, u32[]{:S(2)}) collective-permute-start(f32[128,2048]{1,0:T(8,128)} %get-tuple-element.30), channel_id=1, source_target_pairs={{0,4},{4,0},{1,5},{5,1},{2,6},{6,2},{3,7},{7,3}} | collective-permute-start | bytes 3145736 | tf_op jit(solution)/shard_map/ppermute | solution.py:338
  379.8 74.1 %collective-permute-start.18 = (f32[128,2048]{1,0:T(8,128)}, f32[128,2048]{1,0:T(8,128)}, u32[]{:S(2)}, u32[]{:S(2)}) collective-permute-start(f32[128,2048]{1,0:T(8,128)} %get-tuple-element.34), channel_id=1, source_target_pairs={{0,4},{4,0},{1,5},{5,1},{2,6},{6,2},{3,7},{7,3}} | collective-permute-start | bytes 3145736 | tf_op jit(solution)/shard_map/ppermute | solution.py:338
  381.2 65.1 %collective-permute-start.13 = (f32[128,2048]{1,0:T(8,128)S(1)}, f32[128,2048]{1,0:T(8,128)}, u32[]{:S(2)}, u32[]{:S(2)}) collective-permute-start(f32[128,2048]{1,0:T(8,128)S(1)} %get-tuple-element.26._after), channel_id=1, source_target_pairs={{0,2},{1,3},{2,0},{3,1},{4,6},{5,7},{6,4},{7,5}} | collective-permute-start | bytes 3145736 | tf_op jit(solution)/shard_map/ppermute | solution.py:332
  425.6 26.1 %collective-permute-start.16 = (f32[128,2048]{1,0:T(8,128)}, f32[128,2048]{1,0:T(8,128)S(1)}, u32[]{:S(2)}, u32[]{:S(2)}) collective-permute-start(f32[128,2048]{1,0:T(8,128)} %copy-done.9), channel_id=1, source_target_pairs={{0,2},{1,3},{2,0},{3,1},{4,6},{5,7},{6,4},{7,5}} | collective-permute-start | bytes 3145736 | tf_op jit(solution)/shard_map/ppermute | solution.py:332
  446.3 29.6 %collective-permute-start.21 = (f32[128,2048]{1,0:T(8,128)S(1)}, f32[128,2048]{1,0:T(8,128)S(1)}, u32[]{:S(2)}, u32[]{:S(2)}) collective-permute-start(f32[128,2048]{1,0:T(8,128)S(1)} %copy-done.27), channel_id=1, source_target_pairs={{0,4},{4,0},{1,5},{5,1},{2,6},{6,2},{3,7},{7,3}} | collective-permute-start | bytes 3145736 | tf_op jit(solution)/shard_map/ppermute | solution.py:338
  446.4 27.8 %collective-permute-start.19 = (f32[128,2048]{1,0:T(8,128)S(1)}, f32[128,2048]{1,0:T(8,128)S(1)}, u32[]{:S(2)}, u32[]{:S(2)}) collective-permute-start(f32[128,2048]{1,0:T(8,128)S(1)} %copy-done.8), channel_id=1, source_target_pairs={{0,2},{1,3},{2,0},{3,1},{4,6},{5,7},{6,4},{7,5}} | collective-permute-start | bytes 3145736 | tf_op jit(solution)/shard_map/ppermute | solution.py:332
  450.3 44.4 %collective-permute-start.22 = (f32[128,2048]{1,0:T(8,128)S(1)}, f32[128,2048]{1,0:T(8,128)S(1)}, u32[]{:S(2)}, u32[]{:S(2)}) collective-permute-start(f32[128,2048]{1,0:T(8,128)S(1)} %copy-done.6), channel_id=1, source_target_pairs={{0,2},{1,3},{2,0},{3,1},{4,6},{5,7},{6,4},{7,5}} | collective-permute-start | bytes 3145736 | tf_op jit(solution)/shard_map/ppermute | solution.py:332
  451.6 43.7 %collective-permute-start.14 = (bf16[128,2048]{1,0:T(8,128)(2,1)S(1)}, bf16[128,2048]{1,0:T(8,128)(2,1)S(1)}, u32[]{:S(2)}, u32[]{:S(2)}) collective-permute-start(bf16[128,2048]{1,0:T(8,128)(2,1)S(1)} %add_convert_fusion.3), channel_id=1, source_target_pairs={{0,4},{4,0},{1,5},{5,1},{2,6},{6,2},{3,7},{7,3}} | collective-permute-start | bytes 1572872 | tf_op jit(solution)/shard_map/ppermute | solution.py:338
  453.9 41.6 %collective-permute-start.17 = (bf16[128,2048]{1,0:T(8,128)(2,1)S(1)}, bf16[128,2048]{1,0:T(8,128)(2,1)S(1)}, u32[]{:S(2)}, u32[]{:S(2)}) collective-permute-start(bf16[128,2048]{1,0:T(8,128)(2,1)S(1)} %add_convert_fusion.2), channel_id=1, source_target_pairs={{0,4},{4,0},{1,5},{5,1},{2,6},{6,2},{3,7},{7,3}} | collective-permute-start | bytes 1572872 | tf_op jit(solution)/shard_map/ppermute | solution.py:338
  475.6 30.4 %collective-permute-start.20 = (bf16[128,2048]{1,0:T(8,128)(2,1)S(1)}, bf16[128,2048]{1,0:T(8,128)(2,1)S(1)}, u32[]{:S(2)}, u32[]{:S(2)}) collective-permute-start(bf16[128,2048]{1,0:T(8,128)(2,1)S(1)} %add_convert_fusion.1), channel_id=1, source_target_pairs={{0,4},{4,0},{1,5},{5,1},{2,6},{6,2},{3,7},{7,3}} | collective-permute-start | bytes 1572872 | tf_op jit(solution)/shard_map/ppermute | solution.py:338
  495.0 20.3 %collective-permute-start.23 = (bf16[128,2048]{1,0:T(8,128)(2,1)S(1)}, bf16[128,2048]{1,0:T(8,128)(2,1)S(1)}, u32[]{:S(2)}, u32[]{:S(2)}) collective-permute-start(bf16[128,2048]{1,0:T(8,128)(2,1)S(1)} %add_convert_fusion), channel_id=1, source_target_pairs={{0,4},{4,0},{1,5},{5,1},{2,6},{6,2},{3,7},{7,3}} | collective-permute-start | bytes 1572872 | tf_op jit(solution)/shard_map/ppermute | solution.py:338
  (28 other events, 631.0 us)
where the time goes:
time: 525 us; the launch traced here: 518 us
  Pallas kernels  299 us (57%)
  waiting for transfers between devices  141 us (27%)
  starting transfers between devices  22.8 us (4%)
  other arithmetic  22.3 us (4%)
  matrix products  21.8 us (4%)
  local copies, waits for them, and re-layouts  10.7 us (2%)
    pallas_call x1, Pallas kernels, run_experts(): pl.pallas_call(expert_kernel, grid_spec=grid_spec, out_shape=jax.ShapeDty...  108 us
    ppermute x10, waiting for transfers between devices, over_tp(): return lax.ppermute(v, 'tp', [(0, 1), (1, 0)])  81.8 us
    pallas_call x4, Pallas kernels, run_combine(): pl.pallas_call(functools.partial(combine_kernel, src, init is not None),...  77.6 us
    pallas_call x2, Pallas kernels, run_ffn(): pl.pallas_call(functools.partial(ffn_kernel, n_out, add is not None), gri...  74.9 us
    ppermute x7, waiting for transfers between devices, over_x(): return lax.ppermute(v, 'ep', [(i, i ^ 2) for i in range(4)])  57.9 us
    pallas_call x1, Pallas kernels, attention(): pl.pallas_call(attn_kernel, grid=(heads,), in_specs=[col, col, col, tab,...  21.5 us
    pallas_call x1, Pallas kernels, run_out(): pl.pallas_call(out_kernel, grid_spec=grid_spec, out_shape=[jax.ShapeDtype...  16.7 us
    ppermute x7, starting transfers between devices, over_x(): return lax.ppermute(v, 'ep', [(i, i ^ 2) for i in range(4)])  13.5 us
  transfers between devices with their start and end apart: 24, of which 8 were waited for; matrix products, arithmetic and copies ran while one was open for 9% of the time, Pallas kernels for 50%

commit v1 on v0

--- a/solution.py
+++ b/solution.py
@@ -1,6 +1,7 @@
 import functools
 import jax
 import jax.numpy as jnp
+import numpy as np
 from jax import lax
 from jax.experimental import pallas as pl
 from jax.experimental.pallas import tpu as pltpu
@@ -22,49 +23,54 @@
     return lax.rsqrt(jnp.mean(x_f32 * x_f32, axis=-1, keepdims=True) + EPS)
 
 
-def rms_norm(x_val, gain):
-    x_f32 = x_val.astype(F32)
-    return (x_f32 * inv_rms_of(x_f32) * gain.astype(F32)).astype(BF16)
+def scaled(x_val, inv, gain):
+    return (x_val.astype(F32) * inv * gain.astype(F32)).astype(BF16)
 
 
 def rope_tables(seq_len, head_dim):
-    inv_freq = ROPE_BASE ** (-jnp.arange(head_dim // 2, dtype=F32) * (2.0 / head_dim))
-    angle = jnp.arange(seq_len, dtype=F32)[:, None] * inv_freq[None, :]
-    cos_tab, sin_tab = jnp.cos(angle), jnp.sin(angle)
-    return jnp.concatenate([cos_tab, cos_tab], axis=1), jnp.concatenate([-sin_tab, sin_tab], axis=1)
+    inv_freq = (np.float32(ROPE_BASE) ** (-np.arange(head_dim // 2, dtype=np.float32) * np.float32(2.0 / head_dim))).astype(np.float32)
+    angle = (np.arange(seq_len, dtype=np.float32)[:, None] * inv_freq[None, :]).astype(np.float64)
+    cos_tab, sin_tab = np.cos(angle).astype(np.float32), np.sin(angle).astype(np.float32)
+    return np.concatenate([cos_tab, cos_tab], axis=1), np.concatenate([-sin_tab, sin_tab], axis=1)
 
 
 def attn_kernel(q_ref, k_ref, v_ref, cos_ref, sin_ref, o_ref, k_scr):
-    seq, hd = q_ref.shape
+    seq, hd = cos_ref.shape
     blk = 256
-    cos_t, sin_t = cos_ref[...], sin_ref[...]
-    k_f = k_ref[...]
-    k_scr[...] = (k_f * cos_t + pltpu.roll(k_f, hd // 2, 1) * sin_t).astype(BF16)
+    pair = q_ref.shape[1] // hd
+    for h in range(pair):
+        hc = slice(h * hd, (h + 1) * hd)
+        k_f = k_ref[:, hc]
+        k_scr[:, hc] = (k_f * cos_ref[...] + pltpu.roll(k_f, hd // 2, 1) * sin_ref[...]).astype(BF16)
     for i in range(seq // blk):
         rows = slice(i * blk, (i + 1) * blk)
-        q_f = q_ref[rows, :]
-        q_b = (q_f * cos_t[rows] + pltpu.roll(q_f, hd // 2, 1) * sin_t[rows]).astype(BF16)
         kv = (i + 1) * blk
-        s = lax.dot_general(q_b, k_scr[:kv, :], (((1,), (1,)), ((), ())), preferred_element_type=F32) * hd ** -0.5
-        r_id = lax.broadcasted_iota(jnp.int32, (blk, kv), 0) + i * blk
-        c_id = lax.broadcasted_iota(jnp.int32, (blk, kv), 1)
-        s = jnp.where(r_id >= c_id, s, -1e30)
-        p = jnp.exp(s - jnp.max(s, axis=1, keepdims=True))
-        p = (p * (1.0 / jnp.sum(p, axis=1, keepdims=True))).astype(BF16)
-        o_ref[rows, :] = jnp.dot(p, v_ref[:kv, :], preferred_element_type=F32).astype(BF16)
+        for h in range(pair):
+            hc = slice(h * hd, (h + 1) * hd)
+            q_f = q_ref[rows, hc]
+            q_b = (q_f * cos_ref[rows] + pltpu.roll(q_f, hd // 2, 1) * sin_ref[rows]).astype(BF16)
+            s = lax.dot_general(q_b, k_scr[:kv, hc], (((1,), (1,)), ((), ())), preferred_element_type=F32) * hd ** -0.5
+            r_id = lax.broadcasted_iota(jnp.int32, (blk, blk), 0)
+            c_id = lax.broadcasted_iota(jnp.int32, (blk, blk), 1)
+            last = jnp.where(r_id >= c_id, s[:, kv - blk:], -1e30)
+            s = last if i == 0 else jnp.concatenate([s[:, :kv - blk], last], axis=1)
+            p = jnp.exp(s - jnp.max(s, axis=1, keepdims=True))
+            p = (p * (1.0 / jnp.sum(p, axis=1, keepdims=True))).astype(BF16)
+            o_ref[rows, hc] = jnp.dot(p, v_ref[:kv, hc], preferred_element_type=F32).astype(BF16)
 
 
 def attention(q, k, v, cos_t, sin_t, head_dim):
     seq, width = q.shape
-    heads = width // head_dim
-    col = pl.BlockSpec((seq, head_dim), lambda h: (0, h))
+    pair = 2
+    steps = width // (pair * head_dim)
+    col = pl.BlockSpec((seq, pair * head_dim), lambda h: (0, h))
     tab = pl.BlockSpec((seq, head_dim), lambda h: (0, 0))
     return pl.pallas_call(
-        attn_kernel, grid=(heads,),
+        attn_kernel, grid=(steps,),
         in_specs=[col, col, col, tab, tab], out_specs=col,
         out_shape=jax.ShapeDtypeStruct((seq, width), BF16),
-        scratch_shapes=[pltpu.VMEM((seq, head_dim), BF16)],
-        cost_estimate=pl.CostEstimate(flops=heads * seq * seq * head_dim * 4, bytes_accessed=12 * seq * width, transcendentals=heads * seq * seq),
+        scratch_shapes=[pltpu.VMEM((seq, pair * head_dim), BF16)],
+        cost_estimate=pl.CostEstimate(flops=width * seq * seq * 4, bytes_accessed=12 * seq * width, transcendentals=0),
         name="attn",
     )(q, k, v, cos_t, sin_t)
 
@@ -79,12 +85,14 @@
         n = n_ref[s, e]
         base = loc_ref[s, e]
         rank_row = rank_ref[s, 0]
-        for i in range(2):
-            @pl.when(n > i * GT)
-            def _():
-                rid = lax.broadcasted_iota(jnp.int32, (GT, half), 0) + i * GT
-                hot = (rank_row == rid).astype(F32).astype(BF16)
-                x_scr[pl.ds(pl.multiple_of(base + i * GT, SEG), GT), :] = jnp.dot(hot, u_refs[s][...], preferred_element_type=F32).astype(BF16)
+
+        def gather(i, carry, s=s, base=base, rank_row=rank_row):
+            rid = lax.broadcasted_iota(jnp.int32, (GT, half), 0) + i * GT
+            hot = (rank_row == rid).astype(F32).astype(BF16)
+            x_scr[pl.ds(pl.multiple_of(base + i * GT, SEG), GT), :] = jnp.dot(hot, u_refs[s][...], preferred_element_type=F32).astype(BF16)
+            return carry
+
+        lax.fori_loop(0, lax.shift_right_logical(n + (GT - 1), 7), gather, 0)
 
     total = loc_ref[3, e] + lax.shift_right_logical(n_ref[3, e] + (SEG - 1), 4) * SEG
 
@@ -112,7 +120,7 @@
             cols = slice(c * 1024, (c + 1) * 1024)
             y_scr[pl.ds(m0, rows), cols] = jnp.dot(h_scr[pl.ds(0, rows), :], wd_ref[0, :, cols], preferred_element_type=F32).astype(BF16)
 
-    for lo, hi in ((256, 320), (320, 384)):
+    for lo, hi in ((256, 288), (288, 320), (320, 352), (352, 384)):
         @pl.when((total > lo) & (total <= hi))
         def _():
             ffn(0, hi)
@@ -183,16 +191,19 @@
         def _():
             fetch(i + 1, 1 - slot).start()
 
-        rid = lax.broadcasted_iota(jnp.int32, (half, CT), 1) + i * CT
-        g = jnp.zeros((half, CT), F32)
-        for j in range(top_k):
-            g = jnp.where(pos_ref[:, j:j + 1] == rid, gate_ref[:, j:j + 1], g)
-        hi = g.astype(BF16)
-        left = g - hi.astype(F32)
-        mid = left.astype(BF16)
-        g_scr[:, :CT] = (left - mid.astype(F32)).astype(BF16)
-        g_scr[:, CT:2 * CT] = mid
-        g_scr[:, 2 * CT:] = hi
+        rid = lax.broadcasted_iota(jnp.int32, (32, CT), 1) + i * CT
+        for b in range(half // 32):
+            tok = slice(b * 32, (b + 1) * 32)
+            pos, gate = pos_ref[tok, :], gate_ref[tok, :]
+            g = jnp.zeros((32, CT), F32)
+            for j in range(top_k):
+                g = jnp.where(pos[:, j:j + 1] == rid, gate[:, j:j + 1], g)
+            hi = g.astype(BF16)
+            left = g - hi.astype(F32)
+            mid = left.astype(BF16)
+            g_scr[tok, :CT] = (left - mid.astype(F32)).astype(BF16)
+            g_scr[tok, CT:2 * CT] = mid
+            g_scr[tok, 2 * CT:] = hi
         fetch(i, slot).wait()
 
         @pl.when(i == n_tiles - 1)
@@ -211,11 +222,11 @@
     lax.fori_loop(0, n_tiles, body, 0)
 
 
-def run_combine(src, rows, pos, gates, y_all, after, init=None, n_out=1):
+def run_combine(src, rows, pos, gates, y_all, after, init=None, n_out=1, part=(0, 1)):
     d = y_all.shape[2]
-    half, top_k = pos.shape[1:]
-    full = pl.BlockSpec((half, d), lambda i, r: (0, 0))
-    small = pl.BlockSpec((half, top_k), lambda i, r: (0, 0))
+    half, top_k = pos.shape[1] // part[1], pos.shape[2]
+    full = pl.BlockSpec((half, d), lambda i, r: (part[0], 0))
+    small = pl.BlockSpec((half, top_k), lambda i, r: (part[0], 0))
     anywhere = pl.BlockSpec(memory_space=pl.ANY)
     extra = [] if init is None else [init]
     grid_spec = pltpu.PrefetchScalarGridSpec(
@@ -296,9 +307,8 @@
             o_ref[...] = v
 
 
-def run_ffn(which, f_norm, wg, wu, wd, after, add=None, n_out=4):
-    seq, d = f_norm.shape
-    half = seq // 2
+def run_ffn(which, half, f_norm, wg, wu, wd, after, add=None, n_out=1):
+    d = f_norm.shape[1]
     ff = wg.shape[1]
     blk = 512
     extra = [] if add is None else [add]
@@ -315,7 +325,7 @@
         functools.partial(ffn_kernel, n_out, add is not None), grid_spec=grid_spec,
         out_shape=[jax.ShapeDtypeStruct((half // n_out, d), F32)] * n_out,
         compiler_params=pltpu.CompilerParams(vmem_limit_bytes=VMEM_BIG),
-        cost_estimate=pl.CostEstimate(flops=28_000_000_000, bytes_accessed=60_000_000, transcendentals=0),
+        cost_estimate=pl.CostEstimate(flops=half * 56_000_000, bytes_accessed=60_000_000, transcendentals=0),
         name="ffn",
     )(which.reshape(1), f_norm, wg, wu, wd, after, *extra)
 
@@ -353,10 +363,11 @@
         quarter = width // 4
         w_q0 = over_tp(lax.dynamic_slice(w_o, (my_ep * quarter, 0), (quarter, d)))
 
+        inv_rms = inv_rms_of(x2.astype(F32))
         x_half = lax.dynamic_slice(x2, (my_tp * half, 0), (half, d))
+        inv_half = lax.dynamic_slice(inv_rms, (my_tp * half, 0), (half, 1))
         ids_half = lax.dynamic_slice(ids, (my_tp * half, 0), (half, top_k))
-        u_half = rms_norm(x_half, moe_gain)
-        u_x = over_x(u_half)
+        u_half = scaled(x_half, inv_half, moe_gain)
         u_c = over_core(u_half)
         logits = jnp.dot(u_half, w_router, preferred_element_type=F32)
         is_e = ids_half[:, :, None] == jnp.arange(n_all, dtype=jnp.int32)[None, None, :]
@@ -364,6 +375,7 @@
         gates = jax.nn.softmax(picked, axis=-1)
         meta = jnp.concatenate([ids_half.astype(F32), gates], axis=1)
         meta_x = over_x(meta)
+        u_x = over_x(u_half)
         meta2 = jnp.stack([meta, meta_x])
         meta_all = jnp.concatenate([meta2, over_core(meta2)])
         u_d = over_core(u_x)
@@ -391,7 +403,7 @@
         hit = ids_loc[..., None] == e_ids
         pos = jnp.sum(jnp.where(hit, pos_e[:, :, None, :] + 1, 0), axis=3) - 1
 
-        x_norm = rms_norm(x2, attn_gain)
+        x_norm = scaled(x2, inv_rms, attn_gain)
         hd = w_query.shape[2]
         q = jnp.dot(x_norm, w_query.reshape(d, width), preferred_element_type=F32)
         k = jnp.dot(x_norm, w_key.reshape(d, width), preferred_element_type=F32)
@@ -402,25 +414,35 @@
 
         cap_src = n_exp * (3 * seq * top_k // (2 * n_all))
         y_all = run_experts(n, loc, dst, rank_t, (u_half, u_x, u_c, u_d), exp_gate, exp_up, exp_down, cap_src, ctx)
-        m3, = run_combine(3, rows, pos, gates_all, y_all, y_all)
+
+        quarters = my_ep ^ jnp.arange(4, dtype=jnp.int32)
+        after, f_norm = run_out(quarters, x2, ffn_gain, ctx, ctx_peer, w_o, (w_q0, w_q2, w_q1, w_q3), y_all)
+        f_far = run_ffn(1 - my_tp, half, f_norm, w_gate, w_up, w_down, after, n_out=2)
+        f_got = []
+        for c in range(2):
+            f_got.append(over_tp(f_far[c]))
+
+        m3, = run_combine(3, rows, pos, gates_all, y_all, f_far[0])
         got3 = over_core(m3)
-
-        quarters = my_ep ^ jnp.arange(4, dtype=jnp.int32)
-        after, f_norm = run_out(quarters, x2, ffn_gain, ctx, ctx_peer, w_o, (w_q0, w_q2, w_q1, w_q3), m3)
-        f_far = run_ffn(1 - my_tp, f_norm, w_gate, w_up, w_down, after)
-        f_got = [over_tp(c) for c in f_far]
-
-        m1 = run_combine(1, rows, pos, gates_all, y_all, f_far[0], init=got3, n_out=CHUNKS)
-        m_x = [over_x(c) for c in m1]
-        m2, = run_combine(2, rows, pos, gates_all, y_all, m1[0])
+        m2, = run_combine(2, rows, pos, gates_all, y_all, m3)
         got2 = over_core(m2)
-        f_own = run_ffn(my_tp, f_norm, w_gate, w_up, w_down, m2, add=after)
-        m0 = run_combine(0, rows, pos, gates_all, y_all, f_own[0], init=got2, n_out=CHUNKS)
+        m1 = run_combine(1, rows, pos, gates_all, y_all, m2, init=got3, n_out=CHUNKS)
+        m_x = []
+        for c in range(CHUNKS):
+            m_x.append(over_x(m1[c]))
+        rc = half // CHUNKS
         own, peer = [], []
-        for c in range(CHUNKS):
-            o_c = ((f_own[c] + f_got[c]) + (m0[c] + m_x[c])).astype(BF16)
-            own.append(o_c)
-            peer.append(over_tp(o_c))
+        tie = m1[0]
+        for p in range(2):
+            f_own, = run_ffn(2 * my_tp + p, half // 2, f_norm, w_gate, w_up, w_down, tie, add=after)
+            m0 = run_combine(0, rows, pos, gates_all, y_all, f_own, init=got2, n_out=CHUNKS // 2, part=(p, 2))
+            tie = m0[0]
+            for k in range(CHUNKS // 2):
+                c = p * (CHUNKS // 2) + k
+                sl = slice(k * rc, (k + 1) * rc)
+                o_c = ((f_own[sl] + f_got[p][sl]) + (m0[k] + m_x[c])).astype(BF16)
+                own.append(o_c)
+                peer.append(over_tp(o_c))
         first = my_tp == 0
         out = jnp.concatenate([jnp.where(first, a, b) for a, b in zip(own, peer)] + [jnp.where(first, b, a) for a, b in zip(own, peer)], axis=0)
         return out.reshape(1, seq, d)

time: 525 us -> 468 us (0.89)
  waiting for transfers between devices: 141 us -> 70.3 us
  Pallas kernels: 299 us -> 312 us
  other arithmetic: 22.3 us -> 15.6 us
    ppermute x10 -> x8, waiting for transfers between devices: 81.8 us -> 38.3 us  [over_tp(): return lax.ppermute(v, 'tp', [(0, 1), (1, 0)])]
    ppermute x7, waiting for transfers between devices: 57.9 us -> 31.9 us  [over_x(): return lax.ppermute(v, 'ep', [(i, i ^ 2) for i in range(4)])]
    pallas_call x2 -> x3, Pallas kernels: 74.9 us -> 87 us  [run_ffn(): pl.pallas_call(functools.partial(ffn_kernel, n_out, add is not None), gri...]
    unnamed x56 -> x60, local copies, waits for them, and re-layouts: 4.75 us -> 10.8 us
    pallas_call x4 -> x5, Pallas kernels: 77.6 us -> 82 us  [run_combine(): pl.pallas_call(functools.partial(combine_kernel, src, init is not None),...]
  transfers between devices with their start and end apart: 24 -> 22, of which waited for: 8 -> 8; matrix products, arithmetic and copies ran while one was open for 9% -> 8% of each run, Pallas kernels for 50% -> 52%
where the time goes in v1:
time: 468 us; the launch traced here: 463 us
  Pallas kernels  312 us (67%)
  waiting for transfers between devices  70.3 us (15%)
  matrix products  24.9 us (5%)
  starting transfers between devices  23.6 us (5%)
  local copies, waits for them, and re-layouts  15.6 us (3%)
  other arithmetic  15.6 us (3%)
    pallas_call x1, Pallas kernels, run_experts(): pl.pallas_call(expert_kernel, grid_spec=grid_spec, out_shape=jax.ShapeDty...  106 us
    pallas_call x3, Pallas kernels, run_ffn(): pl.pallas_call(functools.partial(ffn_kernel, n_out, add is not None), gri...  87 us
    pallas_call x5, Pallas kernels, run_combine(): pl.pallas_call(functools.partial(combine_kernel, src, init is not None),...  82 us
    ppermute x8, waiting for transfers between devices, over_tp(): return lax.ppermute(v, 'tp', [(0, 1), (1, 0)])  38.3 us
    ppermute x7, waiting for transfers between devices, over_x(): return lax.ppermute(v, 'ep', [(i, i ^ 2) for i in range(4)])  31.9 us
    pallas_call x1, Pallas kernels, attention(): pl.pallas_call(attn_kernel, grid=(steps,), in_specs=[col, col, col, tab,...  20.8 us
    pallas_call x1, Pallas kernels, run_out(): pl.pallas_call(out_kernel, grid_spec=grid_spec, out_shape=[jax.ShapeDtype...  16.7 us
    ppermute x7, starting transfers between devices, over_x(): return lax.ppermute(v, 'ep', [(i, i ^ 2) for i in range(4)])  14.1 us
  transfers between devices with their start and end apart: 22, of which 8 were waited for; matrix products, arithmetic and copies ran while one was open for 8% of the time, Pallas kernels for 52%

profile of v1, /device:TPU:0, one launch (start us, length us, event | category | flops | bytes accessed | tf_op | source)
XLA Modules:
  0.0 463.1 jit_solution(18316544624773862017)
XLA Ops:
  0.0 3.1 multiply_reduce_fusion
  3.3 3.5 fusion.11.u0_ref
  6.7 3.3 collective-permute-start.7
  16.2 10.1 %fusion.4.k_ref = f32[1024,1024]{1,0:T(8,128)} fusion(bf16[256,8,8,128]{3,2,1,0:T(8,128)(2,1)} %bitcast.71, bf16[1,1024,2048]{2,1,0:T(8,128)(2,1)} %param.19, f32[2048]{0:T(1024)S(1)} %convert_element_type.65, f32[1024]{0:T(1024)S(1)} %add_rsqrt_fusion), kind=kOutput, calls=%fused_computation.6 | convolution fusion | flops 4303355904 | bytes 12595200 | tf_op jit(solution)/shard_map/dot_general | solution.py:409
  26.3 6.3 %fusion.7.q_ref = f32[1024,1024]{1,0:T(8,128)} fusion(bf16[256,8,8,128]{3,2,1,0:T(8,128)(2,1)S(1)} %bitcast.72, bf16[1,1024,2048]{2,1,0:T(8,128)(2,1)S(1)} %copy-done.15, f32[2048]{0:T(1024)S(1)} %convert_element_type.65, f32[1024]{0:T(1024)S(1)} %add_rsqrt_fusion), kind=kOutput, calls=%fused_computation.9 | convolution fusion | flops 4303355904 | bytes 12595200 | tf_op jit(solution)/shard_map/dot_general | solution.py:408
  32.7 5.8 %fusion.12.v_ref = bf16[1024,1024]{1,0:T(8,128)(2,1)} fusion(bf16[256,8,8,128]{3,2,1,0:T(8,128)(2,1)S(1)} %bitcast.73, bf16[1,1024,2048]{2,1,0:T(8,128)(2,1)S(1)} %copy-done.15, f32[2048]{0:T(1024)S(1)} %convert_element_type.65, f32[1024]{0:T(1024)S(1)} %add_rsqrt_fusion), kind=kOutput, calls=%fused_computation.15 | convolution fusion | flops 4304404480 | bytes 10498048 | tf_op jit(solution)/shard_map/dot_general | solution.py:410
  38.5 20.8 %attn.1._after.ctx_ref = bf16[1024,1024]{1,0:T(8,128)(2,1)} custom-call(f32[1024,1024]{1,0:T(8,128)} %fusion.7.q_ref, f32[1024,1024]{1,0:T(8,128)} %fusion.4.k_ref, bf16[1024,1024]{1,0:T(8,128)(2,1)} %fusion.12.v_ref, f32[1024,128]{1,0:T(8,128)} %constant.64.clone.cos_ref, f32[1024,128]{1,0:T(8,128)} %constant.65.clone.sin_ref), custom_call_target="tpu_custom_call" | custom-call | flops 4294967296 | bytes 12582912 | tf_op jit(solution)/shard_map/attn/pallas_call | solution.py:68
  69.5 20.7 %collective-permute-done.3.w2_ref = bf16[256,2048]{1,0:T(8,128)(2,1)} collective-permute-done((bf16[256,2048]{1,0:T(8,128)(2,1)}, bf16[256,2048]{1,0:T(8,128)(2,1)}, u32[]{:S(2)}, u32[]{:S(2)}) %collective-permute-start.3) | collective-permute-done | bytes 1048608 | tf_op jit(solution)/shard_map/ppermute | solution.py:342
  90.2 105.9 %experts.1._after.y_hbm = bf16[4,3328,2048]{2,1,0:T(8,128)(2,1)} custom-call(s32[4,16]{1,0:T(4,128)} %copy-done.23, s32[4,16]{1,0:T(4,128)} %select_reduce_fusion.3.loc_ref, s32[4,16]{1,0:T(4,128)} %copy-done.27, s32[4,16,1,512]{3,2,1,0:T(1,128)} %broadcast_in_dim.104.rank_ref, bf16[512,2048]{1,0:T(8,128)(2,1)} %fusion.11.u0_ref, ...), custom_call_target="tpu_custom_call" | custom-call | flops 89999998976 | bytes 241326592 | tf_op jit(solution)/shard_map/experts/pallas_call | solution.py:160
  197.1 16.7 %out_proj.1 = (bf16[1024,2048]{1,0:T(8,128)(2,1)}, bf16[1024,2048]{1,0:T(8,128)(2,1)}) custom-call(s32[4]{0:T(128)} %iota_xor_fusion.q_ref, bf16[1024,2048]{1,0:T(8,128)(2,1)} %bitcast.62, bf16[1,2048]{1,0:T(2,128)(2,1)} %reshape.178.gain_ref, bf16[1024,1024]{1,0:T(8,128)(2,1)} %attn.1._after.ctx_ref, bf16[1024,1024]{1,0:T(8,128)(2,1)} %collective-permute-done.peer_ref, ...), custom_call_target="tpu_custom_call" | custom-call | flops 10000000000 | bytes 24000000 | tf_op jit(solution)/shard_map/out_proj/pallas_call | solution.py:272
  213.8 37.0 %ffn.3 = (f32[256,2048]{1,0:T(8,128)}, f32[256,2048]{1,0:T(8,128)}) custom-call(s32[1]{0:T(128)} %bitcast.17.off_ref, bf16[1024,2048]{1,0:T(8,128)(2,1)} %get-tuple-element.17.x_ref, bf16[2048,4096]{1,0:T(8,128)(2,1)} %wg_ref.7, bf16[2048,4096]{1,0:T(8,128)(2,1)} %wu_ref.7, bf16[4096,2048]{1,0:T(8,128)(2,1)} %wd_ref.7, ...), custom_call_target="tpu_custom_call" | custom-call | flops 28672000000 | bytes 60000000 | tf_op jit(solution)/shard_map/ffn/pallas_call | solution.py:324
  252.5 19.0 %shard_map.172._after = f32[512,2048]{1,0:T(8,128)} custom-call(s32[4]{0:T(128)S(1)} %get-tuple-element.29.rows_ref, s32[512,8]{1,0:T(8,128)S(1)} %get-tuple-element.38.pos_ref, f32[512,8]{1,0:T(8,128)S(1)} %get-tuple-element.41.gate_ref, bf16[4,3328,2048]{2,1,0:T(8,128)(2,1)} %experts.1._after.y_hbm, f32[256,2048]{1,0:T(8,128)S(1)} %copy-done.7), custom_call_target="tpu_custom_call" | custom-call | flops 12000000000 | bytes 10000000 | tf_op jit(solution)/shard_map/pallas_call | solution.py:238
  271.5 19.0 %shard_map.173._after = f32[512,2048]{1,0:T(8,128)} custom-call(s32[4]{0:T(128)S(1)} %get-tuple-element.29.rows_ref, s32[512,8]{1,0:T(8,128)S(1)} %get-tuple-element.39.pos_ref, f32[512,8]{1,0:T(8,128)S(1)} %get-tuple-element.42.gate_ref, bf16[4,3328,2048]{2,1,0:T(8,128)(2,1)} %experts.1._after.y_hbm, f32[512,2048]{1,0:T(8,128)} %shard_map.172._after), custom_call_target="tpu_custom_call" | custom-call | flops 12000000000 | bytes 10000000 | tf_op jit(solution)/shard_map/pallas_call | solution.py:238
  294.5 20.5 %shard_map.174 = (f32[128,2048]{1,0:T(8,128)S(1)}, f32[128,2048]{1,0:T(8,128)S(1)}, f32[128,2048]{1,0:T(8,128)}, f32[128,2048]{1,0:T(8,128)S(1)}) custom-call(s32[4]{0:T(128)S(1)} %get-tuple-element.29.rows_ref, s32[512,8]{1,0:T(8,128)S(1)} %copy-done.10, f32[512,8]{1,0:T(8,128)S(1)} %slice_bitcast_fusion.6.gate_ref, ...), custom_call_target="tpu_custom_call" | custom-call | flops 12000000000 | bytes 10000000 | tf_op jit(solution)/shard_map/pallas_call | solution.py:238
  315.0 5.7 %collective-permute-start.18 = (f32[128,2048]{1,0:T(8,128)}, f32[128,2048]{1,0:T(8,128)}, u32[]{:S(2)}, u32[]{:S(2)}) collective-permute-start(f32[128,2048]{1,0:T(8,128)} %get-tuple-element.26), channel_id=1, source_target_pairs={{0,2},{1,3},{2,0},{3,1},{4,6},{5,7},{6,4},{7,5}} | collective-permute-start | bytes 3145736 | tf_op jit(solution)/shard_map/ppermute | solution.py:342
  322.0 25.0 %ffn.4._after = f32[256,2048]{1,0:T(8,128)} custom-call(s32[1]{0:T(128)} %bitcast.off_ref, bf16[1024,2048]{1,0:T(8,128)(2,1)} %get-tuple-element.17.x_ref, bf16[2048,4096]{1,0:T(8,128)(2,1)} %wg_ref.7, bf16[2048,4096]{1,0:T(8,128)(2,1)} %wu_ref.7, bf16[4096,2048]{1,0:T(8,128)(2,1)} %wd_ref.7, f32[128,2048]{1,0:T(8,128)} %copy-done.9, ...), custom_call_target="tpu_custom_call" | custom-call | flops 14336000000 | bytes 60000000 | tf_op jit(solution)/shard_map/ffn/pallas_call | solution.py:324
  349.3 11.5 %shard_map.175 = (f32[128,2048]{1,0:T(8,128)S(1)}, f32[128,2048]{1,0:T(8,128)S(1)}) custom-call(s32[4]{0:T(128)S(1)} %get-tuple-element.29.rows_ref, s32[512,8]{1,0:T(8,128)S(1)} %get-tuple-element.37.pos_ref, f32[512,8]{1,0:T(8,128)S(1)} %slice_bitcast_fusion.gate_ref, bf16[4,3328,2048]{2,1,0:T(8,128)(2,1)} %experts.1._after.y_hbm, ...), custom_call_target="tpu_custom_call" | custom-call | flops 12000000000 | bytes 10000000 | tf_op jit(solution)/shard_map/pallas_call | solution.py:238
  362.8 24.9 %ffn.5._after = f32[256,2048]{1,0:T(8,128)} custom-call(s32[1]{0:T(128)} %bitcast.20.off_ref, bf16[1024,2048]{1,0:T(8,128)(2,1)} %get-tuple-element.17.x_ref, bf16[2048,4096]{1,0:T(8,128)(2,1)} %wg_ref.7, bf16[2048,4096]{1,0:T(8,128)(2,1)} %wu_ref.7, bf16[4096,2048]{1,0:T(8,128)(2,1)} %wd_ref.7, f32[128,2048]{1,0:T(8,128)} %copy-done.5, ...), custom_call_target="tpu_custom_call" | custom-call | flops 14336000000 | bytes 60000000 | tf_op jit(solution)/shard_map/ffn/pallas_call | solution.py:324
  390.6 12.0 %shard_map.176 = (f32[128,2048]{1,0:T(8,128)S(1)}, f32[128,2048]{1,0:T(8,128)S(1)}) custom-call(s32[4]{0:T(128)S(1)} %get-tuple-element.29.rows_ref, s32[512,8]{1,0:T(8,128)S(1)} %get-tuple-element.37.pos_ref, f32[512,8]{1,0:T(8,128)S(1)} %slice_bitcast_fusion.gate_ref, bf16[4,3328,2048]{2,1,0:T(8,128)(2,1)} %experts.1._after.y_hbm, ...), custom_call_target="tpu_custom_call" | custom-call | flops 12000000000 | bytes 10000000 | tf_op jit(solution)/shard_map/pallas_call | solution.py:238
  402.6 9.1 %collective-permute-done.15 = f32[128,2048]{1,0:T(8,128)S(1)} collective-permute-done((f32[128,2048]{1,0:T(8,128)}, f32[128,2048]{1,0:T(8,128)S(1)}, u32[]{:S(2)}, u32[]{:S(2)}) %collective-permute-start.15) | collective-permute-done | bytes 1048608 | tf_op jit(solution)/shard_map/ppermute | solution.py:342
  421.4 7.8 %collective-permute-done.14 = bf16[128,2048]{1,0:T(8,128)(2,1)S(1)} collective-permute-done((bf16[128,2048]{1,0:T(8,128)(2,1)S(1)}, bf16[128,2048]{1,0:T(8,128)(2,1)S(1)}, u32[]{:S(2)}, u32[]{:S(2)}) %collective-permute-start.14) | collective-permute-done | bytes 524320 | tf_op jit(solution)/shard_map/ppermute | solution.py:348
  429.3 11.1 %collective-permute-done.16 = bf16[128,2048]{1,0:T(8,128)(2,1)S(1)} collective-permute-done((bf16[128,2048]{1,0:T(8,128)(2,1)S(1)}, bf16[128,2048]{1,0:T(8,128)(2,1)S(1)}, u32[]{:S(2)}, u32[]{:S(2)}) %collective-permute-start.16) | collective-permute-done | bytes 524320 | tf_op jit(solution)/shard_map/ppermute | solution.py:348
  440.6 11.1 %collective-permute-done.19 = bf16[128,2048]{1,0:T(8,128)(2,1)S(1)} collective-permute-done((bf16[128,2048]{1,0:T(8,128)(2,1)S(1)}, bf16[128,2048]{1,0:T(8,128)(2,1)S(1)}, u32[]{:S(2)}, u32[]{:S(2)}) %collective-permute-start.19) | collective-permute-done | bytes 524320 | tf_op jit(solution)/shard_map/ppermute | solution.py:348
  451.8 8.3 %collective-permute-done.21 = bf16[128,2048]{1,0:T(8,128)(2,1)S(1)} collective-permute-done((bf16[128,2048]{1,0:T(8,128)(2,1)S(1)}, bf16[128,2048]{1,0:T(8,128)(2,1)S(1)}, u32[]{:S(2)}, u32[]{:S(2)}) %collective-permute-start.21) | collective-permute-done | bytes 524320 | tf_op jit(solution)/shard_map/ppermute | solution.py:348
  (143 shorter events, 44.0 us)
Async XLA Ops:
  6.7 54.8 %collective-permute-start.7 = (bf16[512,2048]{1,0:T(8,128)(2,1)}, bf16[512,2048]{1,0:T(8,128)(2,1)}, u32[]{:S(2)}, u32[]{:S(2)}) collective-permute-start(bf16[512,2048]{1,0:T(8,128)(2,1)} %fusion.11.u0_ref), channel_id=1, source_target_pairs={{0,2},{1,3},{2,0},{3,1},{4,6},{5,7},{6,4},{7,5}} | collective-permute-start | bytes 6291464 | tf_op jit(solution)/shard_map/ppermute | solution.py:342
  10.0 80.2 %collective-permute-start.8 = (bf16[512,2048]{1,0:T(8,128)(2,1)}, bf16[512,2048]{1,0:T(8,128)(2,1)}, u32[]{:S(2)}, u32[]{:S(2)}) collective-permute-start(bf16[512,2048]{1,0:T(8,128)(2,1)} %fusion.11.u0_ref), channel_id=1, source_target_pairs={{0,1},{1,0},{2,3},{3,2},{4,5},{5,4},{6,7},{7,6}} | collective-permute-start | bytes 6291464 | tf_op jit(solution)/shard_map/ppermute | solution.py:345
  12.8 49.8 %copy-start.16 = (f32[512,16]{1,0:T(8,128)}, f32[512,16]{1,0:T(8,128)S(1)}, u32[]{:S(2)}) copy-start(f32[512,16]{1,0:T(8,128)S(1)} %copy.35) | copy-start | bytes 98308
  12.8 48.7 %collective-permute-start.5 = (f32[512,16]{1,0:T(8,128)S(1)}, f32[512,16]{1,0:T(8,128)S(1)}, u32[]{:S(2)}, u32[]{:S(2)}) collective-permute-start(f32[512,16]{1,0:T(8,128)S(1)} %copy.35), channel_id=1, source_target_pairs={{0,2},{1,3},{2,0},{3,1},{4,6},{5,7},{6,4},{7,5}} | collective-permute-start | bytes 98312 | tf_op jit(solution)/shard_map/ppermute | solution.py:342
  14.2 50.4 %collective-permute-start.1 = (bf16[256,2048]{1,0:T(8,128)(2,1)S(1)}, bf16[256,2048]{1,0:T(8,128)(2,1)}, u32[]{:S(2)}, u32[]{:S(2)}) collective-permute-start(bf16[256,2048]{1,0:T(8,128)(2,1)S(1)} %constant_dynamic-slice_fusion), channel_id=1, source_target_pairs={{0,4},{4,0},{1,5},{5,1},{2,6},{6,2},{3,7},{7,3}} | collective-permute-start | bytes 3145736 | tf_op jit(solution)/shard_map/ppermute | solution.py:348
  59.3 136.8 %collective-permute-start = (bf16[1024,1024]{1,0:T(8,128)(2,1)}, bf16[1024,1024]{1,0:T(8,128)(2,1)}, u32[]{:S(2)}, u32[]{:S(2)}) collective-permute-start(bf16[1024,1024]{1,0:T(8,128)(2,1)} %attn.1._after.ctx_ref), channel_id=1, source_target_pairs={{0,4},{4,0},{1,5},{5,1},{2,6},{6,2},{3,7},{7,3}} | collective-permute-start | bytes 6291464 | tf_op jit(solution)/shard_map/ppermute | solution.py:348
  61.5 1.9 collective-permute-start.6
  61.6 28.6 %collective-permute-start.9 = (bf16[512,2048]{1,0:T(8,128)(2,1)}, bf16[512,2048]{1,0:T(8,128)(2,1)}, u32[]{:S(2)}, u32[]{:S(2)}) collective-permute-start(bf16[512,2048]{1,0:T(8,128)(2,1)} %collective-permute-done.7.u1_ref), channel_id=1, source_target_pairs={{0,1},{1,0},{2,3},{3,2},{4,5},{5,4},{6,7},{7,6}} | collective-permute-start | bytes 6291464 | tf_op jit(solution)/shard_map/ppermute | solution.py:345
  64.1 26.1 %copy-start.23 = (s32[4,16]{1,0:T(4,128)}, s32[4,16]{1,0:T(4,128)S(1)}, u32[]{:S(2)}) copy-start(s32[4,16]{1,0:T(4,128)S(1)} %convert_reduce_fusion.n_ref) | copy-start | bytes 772
  64.6 25.5 %collective-permute-start.3 = (bf16[256,2048]{1,0:T(8,128)(2,1)}, bf16[256,2048]{1,0:T(8,128)(2,1)}, u32[]{:S(2)}, u32[]{:S(2)}) collective-permute-start(bf16[256,2048]{1,0:T(8,128)(2,1)} %collective-permute-done.1.w0_ref), channel_id=1, source_target_pairs={{0,2},{1,3},{2,0},{3,1},{4,6},{5,7},{6,4},{7,5}} | collective-permute-start | bytes 3145736 | tf_op jit(solution)/shard_map/ppermute | solution.py:342
  69.5 126.6 %collective-permute-start.2 = (bf16[256,2048]{1,0:T(8,128)(2,1)}, bf16[256,2048]{1,0:T(8,128)(2,1)S(1)}, u32[]{:S(2)}, u32[]{:S(2)}) collective-permute-start(bf16[256,2048]{1,0:T(8,128)(2,1)} %collective-permute-done.1.w0_ref), channel_id=1, source_target_pairs={{0,1},{1,0},{2,3},{3,2},{4,5},{5,4},{6,7},{7,6}} | collective-permute-start | bytes 3145736 | tf_op jit(solution)/shard_map/ppermute | solution.py:345
  90.2 106.0 %collective-permute-start.4 = (bf16[256,2048]{1,0:T(8,128)(2,1)}, bf16[256,2048]{1,0:T(8,128)(2,1)}, u32[]{:S(2)}, u32[]{:S(2)}) collective-permute-start(bf16[256,2048]{1,0:T(8,128)(2,1)} %collective-permute-done.3.w2_ref), channel_id=1, source_target_pairs={{0,1},{1,0},{2,3},{3,2},{4,5},{5,4},{6,7},{7,6}} | collective-permute-start | bytes 3145736 | tf_op jit(solution)/shard_map/ppermute | solution.py:345
  271.5 22.1 %collective-permute-start.10 = (f32[512,2048]{1,0:T(8,128)}, f32[512,2048]{1,0:T(8,128)}, u32[]{:S(2)}, u32[]{:S(2)}) collective-permute-start(f32[512,2048]{1,0:T(8,128)} %shard_map.172._after), channel_id=1, source_target_pairs={{0,1},{1,0},{2,3},{3,2},{4,5},{5,4},{6,7},{7,6}} | collective-permute-start | bytes 12582920 | tf_op jit(solution)/shard_map/ppermute | solution.py:345
  290.5 56.4 %collective-permute-start.12 = (f32[512,2048]{1,0:T(8,128)}, f32[512,2048]{1,0:T(8,128)}, u32[]{:S(2)}, u32[]{:S(2)}) collective-permute-start(f32[512,2048]{1,0:T(8,128)} %shard_map.173._after), channel_id=1, source_target_pairs={{0,1},{1,0},{2,3},{3,2},{4,5},{5,4},{6,7},{7,6}} | collective-permute-start | bytes 12582920 | tf_op jit(solution)/shard_map/ppermute | solution.py:345
  291.3 96.4 %collective-permute-start.11 = (f32[256,2048]{1,0:T(8,128)S(1)}, f32[256,2048]{1,0:T(8,128)}, u32[]{:S(2)}, u32[]{:S(2)}) collective-permute-start(f32[256,2048]{1,0:T(8,128)S(1)} %copy-done.8), channel_id=1, source_target_pairs={{0,4},{4,0},{1,5},{5,1},{2,6},{6,2},{3,7},{7,3}} | collective-permute-start | bytes 6291464 | tf_op jit(solution)/shard_map/ppermute | solution.py:348
  293.5 123.0 %collective-permute-start.17 = (f32[256,2048]{1,0:T(8,128)}, f32[256,2048]{1,0:T(8,128)}, u32[]{:S(2)}, u32[]{:S(2)}) collective-permute-start(f32[256,2048]{1,0:T(8,128)} %get-tuple-element.24), channel_id=1, source_target_pairs={{0,4},{4,0},{1,5},{5,1},{2,6},{6,2},{3,7},{7,3}} | collective-permute-start | bytes 6291464 | tf_op jit(solution)/shard_map/ppermute | solution.py:348
  315.0 101.5 %collective-permute-start.18 = (f32[128,2048]{1,0:T(8,128)}, f32[128,2048]{1,0:T(8,128)}, u32[]{:S(2)}, u32[]{:S(2)}) collective-permute-start(f32[128,2048]{1,0:T(8,128)} %get-tuple-element.26), channel_id=1, source_target_pairs={{0,2},{1,3},{2,0},{3,1},{4,6},{5,7},{6,4},{7,5}} | collective-permute-start | bytes 3145736 | tf_op jit(solution)/shard_map/ppermute | solution.py:342
  320.7 81.9 %collective-permute-start.13 = (f32[128,2048]{1,0:T(8,128)S(1)}, f32[128,2048]{1,0:T(8,128)}, u32[]{:S(2)}, u32[]{:S(2)}) collective-permute-start(f32[128,2048]{1,0:T(8,128)S(1)} %get-tuple-element.20._after), channel_id=1, source_target_pairs={{0,2},{1,3},{2,0},{3,1},{4,6},{5,7},{6,4},{7,5}} | collective-permute-start | bytes 3145736 | tf_op jit(solution)/shard_map/ppermute | solution.py:342
  346.9 69.5 %collective-permute-start.20 = (f32[128,2048]{1,0:T(8,128)}, f32[128,2048]{1,0:T(8,128)}, u32[]{:S(2)}, u32[]{:S(2)}) collective-permute-start(f32[128,2048]{1,0:T(8,128)} %copy-done.13), channel_id=1, source_target_pairs={{0,2},{1,3},{2,0},{3,1},{4,6},{5,7},{6,4},{7,5}} | collective-permute-start | bytes 3145736 | tf_op jit(solution)/shard_map/ppermute | solution.py:342
  387.7 24.0 %collective-permute-start.15 = (f32[128,2048]{1,0:T(8,128)}, f32[128,2048]{1,0:T(8,128)S(1)}, u32[]{:S(2)}, u32[]{:S(2)}) collective-permute-start(f32[128,2048]{1,0:T(8,128)} %copy-done.14), channel_id=1, source_target_pairs={{0,2},{1,3},{2,0},{3,1},{4,6},{5,7},{6,4},{7,5}} | collective-permute-start | bytes 3145736 | tf_op jit(solution)/shard_map/ppermute | solution.py:342
  414.3 14.9 %collective-permute-start.14 = (bf16[128,2048]{1,0:T(8,128)(2,1)S(1)}, bf16[128,2048]{1,0:T(8,128)(2,1)S(1)}, u32[]{:S(2)}, u32[]{:S(2)}) collective-permute-start(bf16[128,2048]{1,0:T(8,128)(2,1)S(1)} %get-tuple-element.36), channel_id=1, source_target_pairs={{0,4},{4,0},{1,5},{5,1},{2,6},{6,2},{3,7},{7,3}} | collective-permute-start | bytes 1572872 | tf_op jit(solution)/shard_map/ppermute | solution.py:348
  416.4 24.0 %collective-permute-start.16 = (bf16[128,2048]{1,0:T(8,128)(2,1)S(1)}, bf16[128,2048]{1,0:T(8,128)(2,1)S(1)}, u32[]{:S(2)}, u32[]{:S(2)}) collective-permute-start(bf16[128,2048]{1,0:T(8,128)(2,1)S(1)} %get-tuple-element.35), channel_id=1, source_target_pairs={{0,4},{4,0},{1,5},{5,1},{2,6},{6,2},{3,7},{7,3}} | collective-permute-start | bytes 1572872 | tf_op jit(solution)/shard_map/ppermute | solution.py:348
  419.4 32.3 %collective-permute-start.19 = (bf16[128,2048]{1,0:T(8,128)(2,1)S(1)}, bf16[128,2048]{1,0:T(8,128)(2,1)S(1)}, u32[]{:S(2)}, u32[]{:S(2)}) collective-permute-start(bf16[128,2048]{1,0:T(8,128)(2,1)S(1)} %get-tuple-element.34), channel_id=1, source_target_pairs={{0,4},{4,0},{1,5},{5,1},{2,6},{6,2},{3,7},{7,3}} | collective-permute-start | bytes 1572872 | tf_op jit(solution)/shard_map/ppermute | solution.py:348
  421.4 38.7 %collective-permute-start.21 = (bf16[128,2048]{1,0:T(8,128)(2,1)S(1)}, bf16[128,2048]{1,0:T(8,128)(2,1)S(1)}, u32[]{:S(2)}, u32[]{:S(2)}) collective-permute-start(bf16[128,2048]{1,0:T(8,128)(2,1)S(1)} %get-tuple-element.33), channel_id=1, source_target_pairs={{0,4},{4,0},{1,5},{5,1},{2,6},{6,2},{3,7},{7,3}} | collective-permute-start | bytes 1572872 | tf_op jit(solution)/shard_map/ppermute | solution.py:348
  (28 other events, 280.3 us)

commit v2 on v1

--- a/solution.py
+++ b/solution.py
@@ -81,18 +81,17 @@
     half, d = u0_ref.shape
     fe = wg_ref.shape[2]
 
+    def gather(s, i):
+        rid = lax.broadcasted_iota(jnp.int32, (GT, half), 0) + i * GT
+        hot = (rank_ref[s, 0] == rid).astype(F32).astype(BF16)
+        x_scr[pl.ds(pl.multiple_of(loc_ref[s, e] + i * GT, SEG), GT), :] = jnp.dot(hot, u_refs[s][...], preferred_element_type=F32).astype(BF16)
+
     for s in range(4):
-        n = n_ref[s, e]
-        base = loc_ref[s, e]
-        rank_row = rank_ref[s, 0]
-
-        def gather(i, carry, s=s, base=base, rank_row=rank_row):
-            rid = lax.broadcasted_iota(jnp.int32, (GT, half), 0) + i * GT
-            hot = (rank_row == rid).astype(F32).astype(BF16)
-            x_scr[pl.ds(pl.multiple_of(base + i * GT, SEG), GT), :] = jnp.dot(hot, u_refs[s][...], preferred_element_type=F32).astype(BF16)
-            return carry
-
-        lax.fori_loop(0, lax.shift_right_logical(n + (GT - 1), 7), gather, 0)
+        @pl.when(n_ref[s, e] > GT)
+        def _():
+            gather(s, 1)
+    for s in range(4):
+        gather(s, 0)
 
     total = loc_ref[3, e] + lax.shift_right_logical(n_ref[3, e] + (SEG - 1), 4) * SEG
 
@@ -168,58 +167,77 @@
 
 def combine_kernel(src, has_init, rows_ref, pos_ref, gate_ref, y_hbm, _after, *rest):
     init_ref = rest[0] if has_init else None
-    *o_refs, y_buf, g_scr, sems = rest[1:] if has_init else rest
+    *o_refs, y_a, y_b, g_a, g_b, sems = rest[1:] if has_init else rest
     half, top_k = pos_ref.shape
     rc, d = o_refs[0].shape
     n_rows = rows_ref[src]
     n_tiles = lax.shift_right_logical(n_rows + (CT - 1), 8)
 
-    def fetch(i, slot):
-        return pltpu.make_async_copy(y_hbm.at[src, pl.ds(pl.multiple_of(i * CT, CT), CT), :], y_buf.at[slot], sems.at[slot])
-
-    @pl.when(n_tiles > 0)
-    def _():
-        fetch(0, 0).start()
-
+    def fetch(i, buf, k):
+        return pltpu.make_async_copy(y_hbm.at[src, pl.ds(pl.multiple_of(i * CT, CT), CT), :], buf, sems.at[k])
+
+    def start(i, buf, k):
+        @pl.when(i < n_tiles)
+        def _():
+            fetch(i, buf, k).start()
+
+    def arrive(i, buf, k):
+        @pl.when(i < n_tiles)
+        def _():
+            fetch(i, buf, k).wait()
+
+        @pl.when(i >= n_tiles - 1)
+        def _():
+            live = lax.broadcasted_iota(jnp.int32, (CT, 1), 0) + i * CT < n_rows
+            buf[...] = jnp.where(live, buf[...].astype(F32), 0.0).astype(BF16)
+
+    def build(i, g_scr, b):
+        rid = lax.broadcasted_iota(jnp.int32, (32, CT), 1) + i * CT
+        tok = slice(b * 32, (b + 1) * 32)
+        pos, gate = pos_ref[tok, :], gate_ref[tok, :]
+        g = jnp.zeros((32, CT), F32)
+        for j in range(top_k):
+            g = jnp.where(pos[:, j:j + 1] == rid, gate[:, j:j + 1], g)
+        hi = g.astype(BF16)
+        left = g - hi.astype(F32)
+        mid = left.astype(BF16)
+        g_scr[tok, :CT] = (left - mid.astype(F32)).astype(BF16)
+        g_scr[tok, CT:2 * CT] = mid
+        g_scr[tok, 2 * CT:] = hi
+
+    def multiply(g_scr, buf, i_next, g_next):
+        n_c = d // 512
+        blocks = half // 32
+        for c in range(n_c):
+            cols = slice(c * 512, (c + 1) * 512)
+            y = buf[:, cols]
+            part = jnp.dot(g_scr[...], jnp.concatenate([y, y, y], axis=0), preferred_element_type=F32)
+            for b in range(c * blocks // n_c, (c + 1) * blocks // n_c):
+                build(i_next, g_next, b)
+            for k, o_ref in enumerate(o_refs):
+                o_ref[:, cols] += part[k * rc:(k + 1) * rc]
+
+    start(0, y_a, 0)
+    for b in range(half // 32):
+        build(0, g_a, b)
     for k, o_ref in enumerate(o_refs):
         o_ref[...] = init_ref[k * rc:(k + 1) * rc, :] if has_init else jnp.zeros_like(o_ref)
 
-    def body(i, carry):
-        slot = lax.rem(i, 2)
+    def body(p, carry):
+        i = 2 * p
+        start(i + 1, y_b, 1)
+        arrive(i, y_a, 0)
+        multiply(g_a, y_a, i + 1, g_b)
 
         @pl.when(i + 1 < n_tiles)
         def _():
-            fetch(i + 1, 1 - slot).start()
-
-        rid = lax.broadcasted_iota(jnp.int32, (32, CT), 1) + i * CT
-        for b in range(half // 32):
-            tok = slice(b * 32, (b + 1) * 32)
-            pos, gate = pos_ref[tok, :], gate_ref[tok, :]
-            g = jnp.zeros((32, CT), F32)
-            for j in range(top_k):
-                g = jnp.where(pos[:, j:j + 1] == rid, gate[:, j:j + 1], g)
-            hi = g.astype(BF16)
-            left = g - hi.astype(F32)
-            mid = left.astype(BF16)
-            g_scr[tok, :CT] = (left - mid.astype(F32)).astype(BF16)
-            g_scr[tok, CT:2 * CT] = mid
-            g_scr[tok, 2 * CT:] = hi
-        fetch(i, slot).wait()
-
-        @pl.when(i == n_tiles - 1)
-        def _():
-            live = lax.broadcasted_iota(jnp.int32, (CT, 1), 0) + i * CT < n_rows
-            y_buf[slot] = jnp.where(live, y_buf[slot].astype(F32), 0.0).astype(BF16)
-
-        for c in range(d // 512):
-            cols = slice(c * 512, (c + 1) * 512)
-            y = y_buf[slot, :, cols]
-            part = jnp.dot(g_scr[...], jnp.concatenate([y, y, y], axis=0), preferred_element_type=F32)
-            for k, o_ref in enumerate(o_refs):
-                o_ref[:, cols] += part[k * rc:(k + 1) * rc]
+            start(i + 2, y_a, 0)
+            arrive(i + 1, y_b, 1)
+            multiply(g_b, y_b, i + 2, g_a)
+
         return carry
 
-    lax.fori_loop(0, n_tiles, body, 0)
+    lax.fori_loop(0, lax.shift_right_logical(n_tiles + 1, 1), body, 0)
 
 
 def run_combine(src, rows, pos, gates, y_all, after, init=None, n_out=1, part=(0, 1)):
@@ -233,7 +251,7 @@
         num_scalar_prefetch=1, grid=(1,),
         in_specs=[small, small, anywhere, anywhere] + [full for _ in extra],
         out_specs=[pl.BlockSpec((half // n_out, d), lambda i, r: (0, 0))] * n_out,
-        scratch_shapes=[pltpu.VMEM((2, CT, d), BF16), pltpu.VMEM((half, 3 * CT), BF16), pltpu.SemaphoreType.DMA((2,))],
+        scratch_shapes=[pltpu.VMEM((CT, d), BF16)] * 2 + [pltpu.VMEM((half, 3 * CT), BF16)] * 2 + [pltpu.SemaphoreType.DMA((2,))],
     )
     return pl.pallas_call(
         functools.partial(combine_kernel, src, init is not None), grid_spec=grid_spec,
@@ -328,6 +346,23 @@
         cost_estimate=pl.CostEstimate(flops=half * 56_000_000, bytes_accessed=60_000_000, transcendentals=0),
         name="ffn",
     )(which.reshape(1), f_norm, wg, wu, wd, after, *extra)
+
+
+def final_kernel(f_ref, g_ref, m_ref, x_ref, o_ref):
+    o_ref[...] = ((f_ref[...] + g_ref[...]) + (m_ref[...] + x_ref[...])).astype(BF16)
+
+
+def run_final(f_own, f_got, got_block, m_own, m_got):
+    rows, d = f_own.shape
+    blk = rows // 2
+    here = pl.BlockSpec((blk, d), lambda i: (i, 0))
+    there = pl.BlockSpec((blk, d), lambda i: (2 * got_block + i, 0))
+    return pl.pallas_call(
+        final_kernel, grid=(2,), in_specs=[here, there, here, here], out_specs=here,
+        out_shape=jax.ShapeDtypeStruct((rows, d), BF16),
+        cost_estimate=pl.CostEstimate(flops=3 * rows * d, bytes_accessed=18 * rows * d, transcendentals=0),
+        name="final",
+    )(f_own, f_got, m_own, m_got)
 
 
 def solution(mesh):
@@ -430,17 +465,15 @@
         m_x = []
         for c in range(CHUNKS):
             m_x.append(over_x(m1[c]))
-        rc = half // CHUNKS
+        f_own = run_ffn(my_tp, half, f_norm, w_gate, w_up, w_down, m1[0], add=after, n_out=CHUNKS)
         own, peer = [], []
-        tie = m1[0]
+        tie = f_own[0]
         for p in range(2):
-            f_own, = run_ffn(2 * my_tp + p, half // 2, f_norm, w_gate, w_up, w_down, tie, add=after)
-            m0 = run_combine(0, rows, pos, gates_all, y_all, f_own, init=got2, n_out=CHUNKS // 2, part=(p, 2))
+            m0 = run_combine(0, rows, pos, gates_all, y_all, tie, init=got2, n_out=CHUNKS // 2, part=(p, 2))
             tie = m0[0]
             for k in range(CHUNKS // 2):
                 c = p * (CHUNKS // 2) + k
-                sl = slice(k * rc, (k + 1) * rc)
-                o_c = ((f_own[sl] + f_got[p][sl]) + (m0[k] + m_x[c])).astype(BF16)
+                o_c = run_final(f_own[c], f_got[p], k, m0[k], m_x[c])
                 own.append(o_c)
                 peer.append(over_tp(o_c))
         first = my_tp == 0

time: 468 us -> 486 us (1.038)
  waiting for transfers between devices: 70.3 us -> 119 us
  Pallas kernels: 312 us -> 284 us
    ppermute x8, waiting for transfers between devices: 38.3 us -> 63.4 us  [over_tp(): return lax.ppermute(v, 'tp', [(0, 1), (1, 0)])]
    ppermute x7, waiting for transfers between devices: 31.9 us -> 54.6 us  [over_x(): return lax.ppermute(v, 'ep', [(i, i ^ 2) for i in range(4)])]
    pallas_call x5, Pallas kernels: 82 us -> 62.1 us  [run_combine(): pl.pallas_call(functools.partial(combine_kernel, src, init is not None),...]
    pallas_call x3 -> x2, Pallas kernels: 87 us -> 74.9 us  [run_ffn(): pl.pallas_call(functools.partial(ffn_kernel, n_out, add is not None), gri...]
    pallas_call x0 -> x4, Pallas kernels: none -> 11.8 us  [run_final(): pl.pallas_call(final_kernel, grid=(2,), in_specs=[here, there, here, here...]
    pallas_call x1, Pallas kernels: 106 us -> 97.6 us  [run_experts(): pl.pallas_call(expert_kernel, grid_spec=grid_spec, out_shape=jax.ShapeDty...]
    convert_element_type x2 -> x0, other arithmetic: 5.52 us -> none  [layer(): o_c = (f_own[sl] + f_got[p][sl] + (m0[k] + m_x[c])).astype(BF16)]
    unnamed x60 -> x58, local copies, waits for them, and re-layouts: 10.8 us -> 8.19 us
  transfers between devices with their start and end apart: 22 -> 22, of which waited for: 8 -> 8; matrix products, arithmetic and copies ran while one was open for 8% -> 7% of each run, Pallas kernels for 52% -> 45%
where the time goes in v2:
time: 486 us; the launch traced here: 477 us
  Pallas kernels  284 us (58%)
  waiting for transfers between devices  119 us (24%)
  starting transfers between devices  22.5 us (5%)
  matrix products  21.6 us (4%)
  local copies, waits for them, and re-layouts  15.2 us (3%)
  other arithmetic  13.2 us (3%)
    pallas_call x1, Pallas kernels, run_experts(): pl.pallas_call(expert_kernel, grid_spec=grid_spec, out_shape=jax.ShapeDty...  97.6 us
    pallas_call x2, Pallas kernels, run_ffn(): pl.pallas_call(functools.partial(ffn_kernel, n_out, add is not None), gri...  74.9 us
    ppermute x8, waiting for transfers between devices, over_tp(): return lax.ppermute(v, 'tp', [(0, 1), (1, 0)])  63.4 us
    pallas_call x5, Pallas kernels, run_combine(): pl.pallas_call(functools.partial(combine_kernel, src, init is not None),...  62.1 us
    ppermute x7, waiting for transfers between devices, over_x(): return lax.ppermute(v, 'ep', [(i, i ^ 2) for i in range(4)])  54.6 us
    pallas_call x1, Pallas kernels, attention(): pl.pallas_call(attn_kernel, grid=(steps,), in_specs=[col, col, col, tab,...  21.2 us
    pallas_call x1, Pallas kernels, run_out(): pl.pallas_call(out_kernel, grid_spec=grid_spec, out_shape=[jax.ShapeDtype...  16.7 us
    pallas_call x4, Pallas kernels, run_final(): pl.pallas_call(final_kernel, grid=(2,), in_specs=[here, there, here, here...  11.8 us
  transfers between devices with their start and end apart: 22, of which 8 were waited for; matrix products, arithmetic and copies ran while one was open for 7% of the time, Pallas kernels for 45%

profile of v2, /device:TPU:0, one launch (start us, length us, event | category | flops | bytes accessed | tf_op | source)
XLA Modules:
  0.0 476.7 jit_solution(10909788121482013647)
XLA Ops:
  0.0 3.1 multiply_reduce_fusion
  5.5 3.3 collective-permute-start.7
  8.9 8.6 %fusion.7.q_ref = f32[1024,1024]{1,0:T(8,128)} fusion(bf16[256,8,8,128]{3,2,1,0:T(8,128)(2,1)} %bitcast.70, bf16[1,1024,2048]{2,1,0:T(8,128)(2,1)S(1)} %copy-done.8, f32[2048]{0:T(1024)S(1)} %convert_element_type.53, f32[1024]{0:T(1024)S(1)} %add_rsqrt_fusion), kind=kOutput, calls=%fused_computation.9 | convolution fusion | flops 4303355904 | bytes 12595200 | tf_op jit(solution)/shard_map/dot_general | solution.py:443
  17.5 6.2 %fusion.4.k_ref = f32[1024,1024]{1,0:T(8,128)} fusion(bf16[256,8,8,128]{3,2,1,0:T(8,128)(2,1)S(1)} %bitcast.71, bf16[1,1024,2048]{2,1,0:T(8,128)(2,1)S(1)} %copy-done.8, f32[2048]{0:T(1024)S(1)} %convert_element_type.53, f32[1024]{0:T(1024)S(1)} %add_rsqrt_fusion), kind=kOutput, calls=%fused_computation.6 | convolution fusion | flops 4303355904 | bytes 12595200 | tf_op jit(solution)/shard_map/dot_general | solution.py:444
  23.7 5.8 %fusion.12.v_ref = bf16[1024,1024]{1,0:T(8,128)(2,1)} fusion(bf16[256,8,8,128]{3,2,1,0:T(8,128)(2,1)S(1)} %bitcast.72, bf16[1,1024,2048]{2,1,0:T(8,128)(2,1)S(1)} %copy-done.8, f32[2048]{0:T(1024)S(1)} %convert_element_type.53, f32[1024]{0:T(1024)S(1)} %add_rsqrt_fusion), kind=kOutput, calls=%fused_computation.15 | convolution fusion | flops 4304404480 | bytes 10498048 | tf_op jit(solution)/shard_map/dot_general | solution.py:445
  29.6 21.2 %attn.1._after.ctx_ref = bf16[1024,1024]{1,0:T(8,128)(2,1)} custom-call(f32[1024,1024]{1,0:T(8,128)} %fusion.7.q_ref, f32[1024,1024]{1,0:T(8,128)} %fusion.4.k_ref, bf16[1024,1024]{1,0:T(8,128)(2,1)} %fusion.12.v_ref, f32[1024,128]{1,0:T(8,128)} %constant.62.clone.cos_ref, f32[1024,128]{1,0:T(8,128)} %constant.63.clone.sin_ref), custom_call_target="tpu_custom_call" | custom-call | flops 4294967296 | bytes 12582912 | tf_op jit(solution)/shard_map/attn/pallas_call | solution.py:68
  57.3 7.0 %collective-permute-done.5 = f32[512,16]{1,0:T(8,128)S(1)} collective-permute-done((f32[512,16]{1,0:T(8,128)S(1)}, f32[512,16]{1,0:T(8,128)S(1)}, u32[]{:S(2)}, u32[]{:S(2)}) %collective-permute-start.5) | collective-permute-done | bytes 32800 | tf_op jit(solution)/shard_map/ppermute | solution.py:377
  68.6 53.0 %collective-permute-done.1.w0_ref = bf16[256,2048]{1,0:T(8,128)(2,1)} collective-permute-done((bf16[256,2048]{1,0:T(8,128)(2,1)}, bf16[256,2048]{1,0:T(8,128)(2,1)}, u32[]{:S(2)}, u32[]{:S(2)}) %collective-permute-start.1) | collective-permute-done | bytes 1048608 | tf_op jit(solution)/shard_map/ppermute | solution.py:383
  127.5 19.1 %collective-permute-done.3.w2_ref = bf16[256,2048]{1,0:T(8,128)(2,1)} collective-permute-done((bf16[256,2048]{1,0:T(8,128)(2,1)}, bf16[256,2048]{1,0:T(8,128)(2,1)}, u32[]{:S(2)}, u32[]{:S(2)}) %collective-permute-start.3) | collective-permute-done | bytes 1048608 | tf_op jit(solution)/shard_map/ppermute | solution.py:377
  146.6 97.6 %experts.1._after.y_hbm = bf16[4,3328,2048]{2,1,0:T(8,128)(2,1)} custom-call(s32[4,16]{1,0:T(4,128)} %copy-done.22, s32[4,16]{1,0:T(4,128)} %select_reduce_fusion.3.loc_ref, s32[4,16]{1,0:T(4,128)} %copy-done.26, s32[4,16,1,512]{3,2,1,0:T(1,128)} %broadcast_in_dim.104.rank_ref, bf16[512,2048]{1,0:T(8,128)(2,1)} %copy-done.9, ...), custom_call_target="tpu_custom_call" | custom-call | flops 89999998976 | bytes 241326592 | tf_op jit(solution)/shard_map/experts/pallas_call | solution.py:159
  244.3 16.7 %out_proj.1 = (bf16[1024,2048]{1,0:T(8,128)(2,1)}, bf16[1024,2048]{1,0:T(8,128)(2,1)}) custom-call(s32[4]{0:T(128)} %iota_xor_fusion.q_ref, bf16[1024,2048]{1,0:T(8,128)(2,1)} %bitcast.61, bf16[1,2048]{1,0:T(2,128)(2,1)} %reshape.175.gain_ref, bf16[1024,1024]{1,0:T(8,128)(2,1)} %attn.1._after.ctx_ref, bf16[1024,1024]{1,0:T(8,128)(2,1)} %collective-permute-done.peer_ref, ...), custom_call_target="tpu_custom_call" | custom-call | flops 10000000000 | bytes 24000000 | tf_op jit(solution)/shard_map/out_proj/pallas_call | solution.py:290
  261.0 37.1 %ffn.2 = (f32[256,2048]{1,0:T(8,128)}, f32[256,2048]{1,0:T(8,128)}) custom-call(s32[1]{0:T(128)} %bitcast.17.off_ref, bf16[1024,2048]{1,0:T(8,128)(2,1)} %get-tuple-element.21.x_ref, bf16[2048,4096]{1,0:T(8,128)(2,1)} %wg_ref.5, bf16[2048,4096]{1,0:T(8,128)(2,1)} %wu_ref.5, bf16[4096,2048]{1,0:T(8,128)(2,1)} %wd_ref.5, ...), custom_call_target="tpu_custom_call" | custom-call | flops 28672000000 | bytes 60000000 | tf_op jit(solution)/shard_map/ffn/pallas_call | solution.py:342
  298.0 14.0 %shard_map.172._after = f32[512,2048]{1,0:T(8,128)} custom-call(s32[4]{0:T(128)S(1)} %get-tuple-element.37.rows_ref, s32[512,8]{1,0:T(8,128)S(1)} %get-tuple-element.42.pos_ref, f32[512,8]{1,0:T(8,128)S(1)} %get-tuple-element.45.gate_ref, bf16[4,3328,2048]{2,1,0:T(8,128)(2,1)} %experts.1._after.y_hbm, f32[256,2048]{1,0:T(8,128)} %get-tuple-element.23._after), custom_call_target="tpu_custom_call" | custom-call | flops 12000000000 | bytes 10000000 | tf_op jit(solution)/shard_map/pallas_call | solution.py:256
  312.2 13.8 %shard_map.173._after = f32[512,2048]{1,0:T(8,128)} custom-call(s32[4]{0:T(128)S(1)} %get-tuple-element.37.rows_ref, s32[512,8]{1,0:T(8,128)S(1)} %get-tuple-element.43.pos_ref, f32[512,8]{1,0:T(8,128)S(1)} %get-tuple-element.46.gate_ref, bf16[4,3328,2048]{2,1,0:T(8,128)(2,1)} %experts.1._after.y_hbm, f32[512,2048]{1,0:T(8,128)} %shard_map.172._after), custom_call_target="tpu_custom_call" | custom-call | flops 12000000000 | bytes 10000000 | tf_op jit(solution)/shard_map/pallas_call | solution.py:256
  328.8 16.0 %shard_map.174 = (f32[128,2048]{1,0:T(8,128)}, f32[128,2048]{1,0:T(8,128)}, f32[128,2048]{1,0:T(8,128)}, f32[128,2048]{1,0:T(8,128)S(1)}) custom-call(s32[4]{0:T(128)S(1)} %get-tuple-element.37.rows_ref, s32[512,8]{1,0:T(8,128)S(1)} %get-tuple-element.44.pos_ref, f32[512,8]{1,0:T(8,128)S(1)} %slice_bitcast_fusion.6.gate_ref, ...), custom_call_target="tpu_custom_call" | custom-call | flops 12000000000 | bytes 10000000 | tf_op jit(solution)/shard_map/pallas_call | solution.py:256
  344.8 3.4 collective-permute-start.13
  348.2 37.8 %ffn.3 = (f32[128,2048]{1,0:T(8,128)}, f32[128,2048]{1,0:T(8,128)}, f32[128,2048]{1,0:T(8,128)}, f32[128,2048]{1,0:T(8,128)}) custom-call(s32[1]{0:T(128)} %bitcast.off_ref, bf16[1024,2048]{1,0:T(8,128)(2,1)} %get-tuple-element.21.x_ref, bf16[2048,4096]{1,0:T(8,128)(2,1)} %wg_ref.5, bf16[2048,4096]{1,0:T(8,128)(2,1)} %wu_ref.5, bf16[4096,2048]{1,0:T(8,128)(2,1)} %wd_ref.5, ...), custom_call_target="tpu_custom_call" | custom-call | flops 28672000000 | bytes 60000000 | tf_op jit(solution)/shard_map/ffn/pallas_call | solution.py:342
  389.3 9.1 %shard_map.175 = (f32[128,2048]{1,0:T(8,128)S(1)}, f32[128,2048]{1,0:T(8,128)S(1)}) custom-call(s32[4]{0:T(128)S(1)} %get-tuple-element.37.rows_ref, s32[512,8]{1,0:T(8,128)S(1)} %get-tuple-element.41.pos_ref, f32[512,8]{1,0:T(8,128)S(1)} %slice_bitcast_fusion.gate_ref, bf16[4,3328,2048]{2,1,0:T(8,128)(2,1)} %experts.1._after.y_hbm, ...), custom_call_target="tpu_custom_call" | custom-call | flops 12000000000 | bytes 10000000 | tf_op jit(solution)/shard_map/pallas_call | solution.py:256
  406.3 6.1 %collective-permute-done.15.x_ref = f32[128,2048]{1,0:T(8,128)} collective-permute-done((f32[128,2048]{1,0:T(8,128)}, f32[128,2048]{1,0:T(8,128)}, u32[]{:S(2)}, u32[]{:S(2)}) %collective-permute-start.15) | collective-permute-done | bytes 1048608 | tf_op jit(solution)/shard_map/ppermute | solution.py:377
  417.3 9.1 %shard_map.176 = (f32[128,2048]{1,0:T(8,128)S(1)}, f32[128,2048]{1,0:T(8,128)S(1)}) custom-call(s32[4]{0:T(128)S(1)} %get-tuple-element.37.rows_ref, s32[512,8]{1,0:T(8,128)S(1)} %get-tuple-element.41.pos_ref, f32[512,8]{1,0:T(8,128)S(1)} %slice_bitcast_fusion.gate_ref, bf16[4,3328,2048]{2,1,0:T(8,128)(2,1)} %experts.1._after.y_hbm, ...), custom_call_target="tpu_custom_call" | custom-call | flops 12000000000 | bytes 10000000 | tf_op jit(solution)/shard_map/pallas_call | solution.py:256
  428.4 6.4 %collective-permute-done.18.x_ref = f32[128,2048]{1,0:T(8,128)} collective-permute-done((f32[128,2048]{1,0:T(8,128)}, f32[128,2048]{1,0:T(8,128)}, u32[]{:S(2)}, u32[]{:S(2)}) %collective-permute-start.18) | collective-permute-done | bytes 1048608 | tf_op jit(solution)/shard_map/ppermute | solution.py:377
  439.8 16.0 %collective-permute-done.20.x_ref = f32[128,2048]{1,0:T(8,128)} collective-permute-done((f32[128,2048]{1,0:T(8,128)S(1)}, f32[128,2048]{1,0:T(8,128)}, u32[]{:S(2)}, u32[]{:S(2)}) %collective-permute-start.20) | collective-permute-done | bytes 1048608 | tf_op jit(solution)/shard_map/ppermute | solution.py:377
  455.8 3.0 final.7
  461.0 10.5 %collective-permute-done.21 = bf16[128,2048]{1,0:T(8,128)(2,1)S(1)} collective-permute-done((bf16[128,2048]{1,0:T(8,128)(2,1)}, bf16[128,2048]{1,0:T(8,128)(2,1)S(1)}, u32[]{:S(2)}, u32[]{:S(2)}) %collective-permute-start.21) | collective-permute-done | bytes 524320 | tf_op jit(solution)/shard_map/ppermute | solution.py:383
  (142 shorter events, 51.7 us)
Async XLA Ops:
  5.5 59.8 %collective-permute-start.7 = (bf16[512,2048]{1,0:T(8,128)(2,1)S(1)}, bf16[512,2048]{1,0:T(8,128)(2,1)}, u32[]{:S(2)}, u32[]{:S(2)}) collective-permute-start(bf16[512,2048]{1,0:T(8,128)(2,1)S(1)} %fusion.11.u0_ref), channel_id=1, source_target_pairs={{0,2},{1,3},{2,0},{3,1},{4,6},{5,7},{6,4},{7,5}} | collective-permute-start | bytes 6291464 | tf_op jit(solution)/shard_map/ppermute | solution.py:377
  8.9 137.7 %collective-permute-start.8 = (bf16[512,2048]{1,0:T(8,128)(2,1)S(1)}, bf16[512,2048]{1,0:T(8,128)(2,1)}, u32[]{:S(2)}, u32[]{:S(2)}) collective-permute-start(bf16[512,2048]{1,0:T(8,128)(2,1)S(1)} %fusion.11.u0_ref), channel_id=1, source_target_pairs={{0,1},{1,0},{2,3},{3,2},{4,5},{5,4},{6,7},{7,6}} | collective-permute-start | bytes 6291464 | tf_op jit(solution)/shard_map/ppermute | solution.py:380
  50.7 193.5 %collective-permute-start = (bf16[1024,1024]{1,0:T(8,128)(2,1)}, bf16[1024,1024]{1,0:T(8,128)(2,1)}, u32[]{:S(2)}, u32[]{:S(2)}) collective-permute-start(bf16[1024,1024]{1,0:T(8,128)(2,1)} %attn.1._after.ctx_ref), channel_id=1, source_target_pairs={{0,4},{4,0},{1,5},{5,1},{2,6},{6,2},{3,7},{7,3}} | collective-permute-start | bytes 6291464 | tf_op jit(solution)/shard_map/ppermute | solution.py:383
  54.6 67.0 %collective-permute-start.1 = (bf16[256,2048]{1,0:T(8,128)(2,1)}, bf16[256,2048]{1,0:T(8,128)(2,1)}, u32[]{:S(2)}, u32[]{:S(2)}) collective-permute-start(bf16[256,2048]{1,0:T(8,128)(2,1)} %constant_dynamic-slice_fusion), channel_id=1, source_target_pairs={{0,4},{4,0},{1,5},{5,1},{2,6},{6,2},{3,7},{7,3}} | collective-permute-start | bytes 3145736 | tf_op jit(solution)/shard_map/ppermute | solution.py:383
  56.2 8.2 %collective-permute-start.5 = (f32[512,16]{1,0:T(8,128)S(1)}, f32[512,16]{1,0:T(8,128)S(1)}, u32[]{:S(2)}, u32[]{:S(2)}) collective-permute-start(f32[512,16]{1,0:T(8,128)S(1)} %copy.35), channel_id=1, source_target_pairs={{0,2},{1,3},{2,0},{3,1},{4,6},{5,7},{6,4},{7,5}} | collective-permute-start | bytes 98312 | tf_op jit(solution)/shard_map/ppermute | solution.py:377
  65.3 2.1 collective-permute-start.6
  65.3 81.3 %collective-permute-start.9 = (bf16[512,2048]{1,0:T(8,128)(2,1)}, bf16[512,2048]{1,0:T(8,128)(2,1)}, u32[]{:S(2)}, u32[]{:S(2)}) collective-permute-start(bf16[512,2048]{1,0:T(8,128)(2,1)} %collective-permute-done.7.u1_ref), channel_id=1, source_target_pairs={{0,1},{1,0},{2,3},{3,2},{4,5},{5,4},{6,7},{7,6}} | collective-permute-start | bytes 6291464 | tf_op jit(solution)/shard_map/ppermute | solution.py:380
  68.1 78.5 %copy-start.22 = (s32[4,16]{1,0:T(4,128)}, s32[4,16]{1,0:T(4,128)S(1)}, u32[]{:S(2)}) copy-start(s32[4,16]{1,0:T(4,128)S(1)} %convert_reduce_fusion.n_ref) | copy-start | bytes 772
  68.4 78.2 %copy-start.26 = (s32[4,16]{1,0:T(4,128)}, s32[4,16]{1,0:T(4,128)S(1)}, u32[]{:S(2)}) copy-start(s32[4,16]{1,0:T(4,128)S(1)} %select_reduce_fusion.2.dst_ref) | copy-start | bytes 772
  121.6 25.0 %collective-permute-start.3 = (bf16[256,2048]{1,0:T(8,128)(2,1)}, bf16[256,2048]{1,0:T(8,128)(2,1)}, u32[]{:S(2)}, u32[]{:S(2)}) collective-permute-start(bf16[256,2048]{1,0:T(8,128)(2,1)} %collective-permute-done.1.w0_ref), channel_id=1, source_target_pairs={{0,2},{1,3},{2,0},{3,1},{4,6},{5,7},{6,4},{7,5}} | collective-permute-start | bytes 3145736 | tf_op jit(solution)/shard_map/ppermute | solution.py:377
  127.5 116.8 %collective-permute-start.2 = (bf16[256,2048]{1,0:T(8,128)(2,1)}, bf16[256,2048]{1,0:T(8,128)(2,1)}, u32[]{:S(2)}, u32[]{:S(2)}) collective-permute-start(bf16[256,2048]{1,0:T(8,128)(2,1)} %collective-permute-done.1.w0_ref), channel_id=1, source_target_pairs={{0,1},{1,0},{2,3},{3,2},{4,5},{5,4},{6,7},{7,6}} | collective-permute-start | bytes 3145736 | tf_op jit(solution)/shard_map/ppermute | solution.py:380
  146.6 97.7 %collective-permute-start.4 = (bf16[256,2048]{1,0:T(8,128)(2,1)}, bf16[256,2048]{1,0:T(8,128)(2,1)}, u32[]{:S(2)}, u32[]{:S(2)}) collective-permute-start(bf16[256,2048]{1,0:T(8,128)(2,1)} %collective-permute-done.3.w2_ref), channel_id=1, source_target_pairs={{0,1},{1,0},{2,3},{3,2},{4,5},{5,4},{6,7},{7,6}} | collective-permute-start | bytes 3145736 | tf_op jit(solution)/shard_map/ppermute | solution.py:380
  312.1 16.7 %collective-permute-start.10 = (f32[512,2048]{1,0:T(8,128)}, f32[512,2048]{1,0:T(8,128)}, u32[]{:S(2)}, u32[]{:S(2)}) collective-permute-start(f32[512,2048]{1,0:T(8,128)} %shard_map.172._after), channel_id=1, source_target_pairs={{0,1},{1,0},{2,3},{3,2},{4,5},{5,4},{6,7},{7,6}} | collective-permute-start | bytes 12582920 | tf_op jit(solution)/shard_map/ppermute | solution.py:380
  326.0 60.1 %collective-permute-start.12 = (f32[512,2048]{1,0:T(8,128)}, f32[512,2048]{1,0:T(8,128)}, u32[]{:S(2)}, u32[]{:S(2)}) collective-permute-start(f32[512,2048]{1,0:T(8,128)} %shard_map.173._after), channel_id=1, source_target_pairs={{0,1},{1,0},{2,3},{3,2},{4,5},{5,4},{6,7},{7,6}} | collective-permute-start | bytes 12582920 | tf_op jit(solution)/shard_map/ppermute | solution.py:380
  326.8 73.6 %collective-permute-start.11 = (f32[256,2048]{1,0:T(8,128)}, f32[256,2048]{1,0:T(8,128)}, u32[]{:S(2)}, u32[]{:S(2)}) collective-permute-start(f32[256,2048]{1,0:T(8,128)} %get-tuple-element.23._after), channel_id=1, source_target_pairs={{0,4},{4,0},{1,5},{5,1},{2,6},{6,2},{3,7},{7,3}} | collective-permute-start | bytes 6291464 | tf_op jit(solution)/shard_map/ppermute | solution.py:383
  328.6 99.8 %collective-permute-start.17 = (f32[256,2048]{1,0:T(8,128)}, f32[256,2048]{1,0:T(8,128)}, u32[]{:S(2)}, u32[]{:S(2)}) collective-permute-start(f32[256,2048]{1,0:T(8,128)} %get-tuple-element.31), channel_id=1, source_target_pairs={{0,4},{4,0},{1,5},{5,1},{2,6},{6,2},{3,7},{7,3}} | collective-permute-start | bytes 6291464 | tf_op jit(solution)/shard_map/ppermute | solution.py:383
  344.8 55.6 %collective-permute-start.13 = (f32[128,2048]{1,0:T(8,128)}, f32[128,2048]{1,0:T(8,128)S(1)}, u32[]{:S(2)}, u32[]{:S(2)}) collective-permute-start(f32[128,2048]{1,0:T(8,128)} %get-tuple-element.24._after), channel_id=1, source_target_pairs={{0,2},{1,3},{2,0},{3,1},{4,6},{5,7},{6,4},{7,5}} | collective-permute-start | bytes 3145736 | tf_op jit(solution)/shard_map/ppermute | solution.py:377
  386.0 26.3 %collective-permute-start.15 = (f32[128,2048]{1,0:T(8,128)}, f32[128,2048]{1,0:T(8,128)}, u32[]{:S(2)}, u32[]{:S(2)}) collective-permute-start(f32[128,2048]{1,0:T(8,128)} %get-tuple-element.29), channel_id=1, source_target_pairs={{0,2},{1,3},{2,0},{3,1},{4,6},{5,7},{6,4},{7,5}} | collective-permute-start | bytes 3145736 | tf_op jit(solution)/shard_map/ppermute | solution.py:377
  386.1 48.8 %collective-permute-start.18 = (f32[128,2048]{1,0:T(8,128)}, f32[128,2048]{1,0:T(8,128)}, u32[]{:S(2)}, u32[]{:S(2)}) collective-permute-start(f32[128,2048]{1,0:T(8,128)} %get-tuple-element.33), channel_id=1, source_target_pairs={{0,2},{1,3},{2,0},{3,1},{4,6},{5,7},{6,4},{7,5}} | collective-permute-start | bytes 3145736 | tf_op jit(solution)/shard_map/ppermute | solution.py:377
  400.4 55.5 %collective-permute-start.20 = (f32[128,2048]{1,0:T(8,128)S(1)}, f32[128,2048]{1,0:T(8,128)}, u32[]{:S(2)}, u32[]{:S(2)}) collective-permute-start(f32[128,2048]{1,0:T(8,128)S(1)} %get-tuple-element.36), channel_id=1, source_target_pairs={{0,2},{1,3},{2,0},{3,1},{4,6},{5,7},{6,4},{7,5}} | collective-permute-start | bytes 3145736 | tf_op jit(solution)/shard_map/ppermute | solution.py:377
  404.3 56.2 %collective-permute-start.14 = (bf16[128,2048]{1,0:T(8,128)(2,1)}, bf16[128,2048]{1,0:T(8,128)(2,1)}, u32[]{:S(2)}, u32[]{:S(2)}) collective-permute-start(bf16[128,2048]{1,0:T(8,128)(2,1)} %final.4), channel_id=1, source_target_pairs={{0,4},{4,0},{1,5},{5,1},{2,6},{6,2},{3,7},{7,3}} | collective-permute-start | bytes 1572872 | tf_op jit(solution)/shard_map/ppermute | solution.py:383
  415.3 45.4 %collective-permute-start.16 = (bf16[128,2048]{1,0:T(8,128)(2,1)}, bf16[128,2048]{1,0:T(8,128)(2,1)}, u32[]{:S(2)}, u32[]{:S(2)}) collective-permute-start(bf16[128,2048]{1,0:T(8,128)(2,1)} %final.5), channel_id=1, source_target_pairs={{0,4},{4,0},{1,5},{5,1},{2,6},{6,2},{3,7},{7,3}} | collective-permute-start | bytes 1572872 | tf_op jit(solution)/shard_map/ppermute | solution.py:383
  437.8 23.0 %collective-permute-start.19 = (bf16[128,2048]{1,0:T(8,128)(2,1)}, bf16[128,2048]{1,0:T(8,128)(2,1)S(1)}, u32[]{:S(2)}, u32[]{:S(2)}) collective-permute-start(bf16[128,2048]{1,0:T(8,128)(2,1)} %final.6), channel_id=1, source_target_pairs={{0,4},{4,0},{1,5},{5,1},{2,6},{6,2},{3,7},{7,3}} | collective-permute-start | bytes 1572872 | tf_op jit(solution)/shard_map/ppermute | solution.py:383
  458.8 12.6 %collective-permute-start.21 = (bf16[128,2048]{1,0:T(8,128)(2,1)}, bf16[128,2048]{1,0:T(8,128)(2,1)S(1)}, u32[]{:S(2)}, u32[]{:S(2)}) collective-permute-start(bf16[128,2048]{1,0:T(8,128)(2,1)} %final.7), channel_id=1, source_target_pairs={{0,4},{4,0},{1,5},{5,1},{2,6},{6,2},{3,7},{7,3}} | collective-permute-start | bytes 1572872 | tf_op jit(solution)/shard_map/ppermute | solution.py:383
  (27 other events, 436.7 us)

commit v3 on v2

--- a/solution.py
+++ b/solution.py
@@ -243,13 +243,12 @@
 def run_combine(src, rows, pos, gates, y_all, after, init=None, n_out=1, part=(0, 1)):
     d = y_all.shape[2]
     half, top_k = pos.shape[1] // part[1], pos.shape[2]
-    full = pl.BlockSpec((half, d), lambda i, r: (part[0], 0))
     small = pl.BlockSpec((half, top_k), lambda i, r: (part[0], 0))
     anywhere = pl.BlockSpec(memory_space=pl.ANY)
     extra = [] if init is None else [init]
     grid_spec = pltpu.PrefetchScalarGridSpec(
         num_scalar_prefetch=1, grid=(1,),
-        in_specs=[small, small, anywhere, anywhere] + [full for _ in extra],
+        in_specs=[small, small, anywhere, anywhere] + [pl.BlockSpec((half, d), lambda i, r: (0, 0)) for _ in extra],
         out_specs=[pl.BlockSpec((half // n_out, d), lambda i, r: (0, 0))] * n_out,
         scratch_shapes=[pltpu.VMEM((CT, d), BF16)] * 2 + [pltpu.VMEM((half, 3 * CT), BF16)] * 2 + [pltpu.SemaphoreType.DMA((2,))],
     )
@@ -296,73 +295,67 @@
     )(quarters, x2, gain.reshape(1, d), ctx, ctx_peer, w_o, *pieces, after)
 
 
-def ffn_kernel(n_out, has_add, off_ref, x_ref, wg_ref, wu_ref, wd_ref, _after, *rest):
-    add_ref = rest[0] if has_add else None
-    outs = rest[1:] if has_add else rest
-    o_refs, acc = outs[:n_out], outs[n_out]
+def ffn_kernel(n_up, n_add, off_ref, x_ref, wg_ref, wu_ref, wd_ref, _after, *rest):
+    adds, (*o_refs, h_scr) = rest[:n_add], rest[n_add:]
     i = pl.program_id(0)
-    x = x_ref[...]
-    g = jnp.dot(x, wg_ref[...], preferred_element_type=F32)
-    u = jnp.dot(x, wu_ref[...], preferred_element_type=F32)
-    h = (g * jax.nn.sigmoid(g) * u).astype(BF16)
-    part = jnp.dot(h, wd_ref[...], preferred_element_type=F32)
-
-    @pl.when(i == 0)
+    blk = wg_ref.shape[1]
+
+    @pl.when(i < n_up)
     def _():
-        acc[...] = part
-
-    @pl.when(i > 0)
+        x = x_ref[...]
+        g = jnp.dot(x, wg_ref[...], preferred_element_type=F32)
+        u = jnp.dot(x, wu_ref[...], preferred_element_type=F32)
+        h_scr[:, pl.ds(pl.multiple_of(i * blk, blk), blk)] = (g * jax.nn.sigmoid(g) * u).astype(BF16)
+
+    @pl.when(i >= n_up)
     def _():
-        acc[...] += part
-
-    @pl.when(i == pl.num_programs(0) - 1)
-    def _():
-        rows = acc.shape[0] // n_out
+        v = jnp.dot(h_scr[...], wd_ref[...], preferred_element_type=F32)
+        for r in adds:
+            v = r[...].astype(F32) + v
+        rows = v.shape[0] // len(o_refs)
         for k, o_ref in enumerate(o_refs):
-            v = acc[k * rows:(k + 1) * rows, :]
-            if has_add:
-                v = add_ref[k * rows:(k + 1) * rows, :].astype(F32) + v
-            o_ref[...] = v
-
-
-def run_ffn(which, half, f_norm, wg, wu, wd, after, add=None, n_out=1):
-    d = f_norm.shape[1]
-    ff = wg.shape[1]
-    blk = 512
-    extra = [] if add is None else [add]
-    mine = pl.BlockSpec((half, d), lambda i, w: (w[0], 0), pipeline_mode=pl.Buffered(1))
+            o_ref[...] = v[k * rows:(k + 1) * rows]
+
+
+def run_ffn(which, rows, f_norm, wg, wu, wd, after, adds=(), n_out=1):
+    d, ff = wg.shape
+    blk, out_blk = 512, 512
+    n_up, n_down = ff // blk, d // out_blk
+    down = lambda i: jnp.maximum(i - n_up, 0)
+    up = lambda i: jnp.minimum(i, n_up - 1)
+    add_specs = [
+        pl.BlockSpec((rows, out_blk), (lambda i, w: (w[0], down(i))) if at is None else (lambda i, w, at=at: (at, down(i))))
+        for _, at in adds]
     grid_spec = pltpu.PrefetchScalarGridSpec(
-        num_scalar_prefetch=1, grid=(ff // blk,),
-        in_specs=[mine,
-                  pl.BlockSpec((d, blk), lambda i, w: (0, i)), pl.BlockSpec((d, blk), lambda i, w: (0, i)),
-                  pl.BlockSpec((blk, d), lambda i, w: (i, 0)), pl.BlockSpec(memory_space=pl.ANY)] + [mine for _ in extra],
-        out_specs=[pl.BlockSpec((half // n_out, d), lambda i, w: (0, 0))] * n_out,
-        scratch_shapes=[pltpu.VMEM((half, d), F32)],
+        num_scalar_prefetch=1, grid=(n_up + n_down,),
+        in_specs=[pl.BlockSpec((rows, d), lambda i, w: (w[0], 0), pipeline_mode=pl.Buffered(1)),
+                  pl.BlockSpec((d, blk), lambda i, w: (0, up(i))), pl.BlockSpec((d, blk), lambda i, w: (0, up(i))),
+                  pl.BlockSpec((ff, out_blk), lambda i, w: (0, down(i))), pl.BlockSpec(memory_space=pl.ANY)] + add_specs,
+        out_specs=[pl.BlockSpec((rows // n_out, out_blk), lambda i, w: (0, down(i)))] * n_out,
+        scratch_shapes=[pltpu.VMEM((rows, ff), BF16)],
     )
     return pl.pallas_call(
-        functools.partial(ffn_kernel, n_out, add is not None), grid_spec=grid_spec,
-        out_shape=[jax.ShapeDtypeStruct((half // n_out, d), F32)] * n_out,
+        functools.partial(ffn_kernel, n_up, len(adds)), grid_spec=grid_spec,
+        out_shape=[jax.ShapeDtypeStruct((rows // n_out, d), F32)] * n_out,
         compiler_params=pltpu.CompilerParams(vmem_limit_bytes=VMEM_BIG),
-        cost_estimate=pl.CostEstimate(flops=half * 56_000_000, bytes_accessed=60_000_000, transcendentals=0),
+        cost_estimate=pl.CostEstimate(flops=rows * 56_000_000, bytes_accessed=60_000_000, transcendentals=0),
         name="ffn",
-    )(which.reshape(1), f_norm, wg, wu, wd, after, *extra)
-
-
-def final_kernel(f_ref, g_ref, m_ref, x_ref, o_ref):
-    o_ref[...] = ((f_ref[...] + g_ref[...]) + (m_ref[...] + x_ref[...])).astype(BF16)
-
-
-def run_final(f_own, f_got, got_block, m_own, m_got):
-    rows, d = f_own.shape
-    blk = rows // 2
-    here = pl.BlockSpec((blk, d), lambda i: (i, 0))
-    there = pl.BlockSpec((blk, d), lambda i: (2 * got_block + i, 0))
-    return pl.pallas_call(
-        final_kernel, grid=(2,), in_specs=[here, there, here, here], out_specs=here,
+    )(which.reshape(1), f_norm, wg, wu, wd, after, *[v for v, _ in adds])
+
+
+def final_kernel(s_ref, g_ref, x_ref, o_ref):
+    o_ref[...] = ((s_ref[...] + g_ref[...]) + x_ref[...]).astype(BF16)
+
+
+def run_final(s_own, f_got, got_block, m_got, m_block):
+    rows, d = s_own.shape
+    row = lambda b: pl.BlockSpec((rows, d), lambda i, b=b: (b, 0))
+    return pl.pallas_call(
+        final_kernel, grid=(1,), in_specs=[row(0), row(got_block), row(m_block)], out_specs=row(0),
         out_shape=jax.ShapeDtypeStruct((rows, d), BF16),
-        cost_estimate=pl.CostEstimate(flops=3 * rows * d, bytes_accessed=18 * rows * d, transcendentals=0),
+        cost_estimate=pl.CostEstimate(flops=3 * rows * d, bytes_accessed=14 * rows * d, transcendentals=0),
         name="final",
-    )(f_own, f_got, m_own, m_got)
+    )(s_own, f_got, m_got)
 
 
 def solution(mesh):
@@ -412,7 +405,8 @@
         meta_x = over_x(meta)
         u_x = over_x(u_half)
         meta2 = jnp.stack([meta, meta_x])
-        meta_all = jnp.concatenate([meta2, over_core(meta2)])
+        meta_c = over_core(meta2)
+        meta_all = jnp.concatenate([meta2, meta_c])
         u_d = over_core(u_x)
         w_q1 = over_x(w_q0)
         w_q2 = over_core(w_q0)
@@ -457,23 +451,30 @@
         for c in range(2):
             f_got.append(over_tp(f_far[c]))
 
-        m3, = run_combine(3, rows, pos, gates_all, y_all, f_far[0])
-        got3 = over_core(m3)
-        m2, = run_combine(2, rows, pos, gates_all, y_all, m3)
+        got3, m_x = [], []
+        tie = f_far[0]
+        for p in range(2):
+            m3, = run_combine(3, rows, pos, gates_all, y_all, tie, part=(p, 2))
+            tie = m3
+            got3.append(over_core(m3))
+        for p in range(2):
+            m1 = run_combine(1, rows, pos, gates_all, y_all, tie, init=got3[p], n_out=CHUNKS // 2, part=(p, 2))
+            tie = m1[0]
+            for k in range(CHUNKS // 2):
+                m_x.append(over_x(m1[k]))
+        m2, = run_combine(2, rows, pos, gates_all, y_all, tie)
         got2 = over_core(m2)
-        m1 = run_combine(1, rows, pos, gates_all, y_all, m2, init=got3, n_out=CHUNKS)
-        m_x = []
-        for c in range(CHUNKS):
-            m_x.append(over_x(m1[c]))
-        f_own = run_ffn(my_tp, half, f_norm, w_gate, w_up, w_down, m1[0], add=after, n_out=CHUNKS)
+        m0, = run_combine(0, rows, pos, gates_all, y_all, m2)
+
         own, peer = [], []
-        tie = f_own[0]
+        tie = m0
         for p in range(2):
-            m0 = run_combine(0, rows, pos, gates_all, y_all, tie, init=got2, n_out=CHUNKS // 2, part=(p, 2))
-            tie = m0[0]
+            s_own = run_ffn(2 * my_tp + p, half // 2, f_norm, w_gate, w_up, w_down, tie,
+                            adds=((after, None), (m0, p), (got2, p)), n_out=CHUNKS // 2)
             for k in range(CHUNKS // 2):
                 c = p * (CHUNKS // 2) + k
-                o_c = run_final(f_own[c], f_got[p], k, m0[k], m_x[c])
+                o_c = run_final(s_own[k], f_got[p], k, m_x[c], 0)
+                tie = o_c
                 own.append(o_c)
                 peer.append(over_tp(o_c))
         first = my_tp == 0

time: 486 us -> 496 us (1.021)
  Pallas kernels: 284 us -> 293 us
    pallas_call x6 -> x7, Pallas kernels: 86.7 us -> 101 us  [the longest x3 89.2 us: run_ffn(): pl.pallas_call(functools.partial(ffn_kernel, n_up, len(adds)), grid_spec=...]
    ppermute x8, waiting for transfers between devices: 63.4 us -> 75.7 us  [over_tp(): return lax.ppermute(v, 'tp', [(0, 1), (1, 0)])]
    ppermute x7, waiting for transfers between devices: 54.6 us -> 43.6 us  [over_x(): return lax.ppermute(v, 'ep', [(i, i ^ 2) for i in range(4)])]
    pallas_call x5 -> x6, Pallas kernels: 62.1 us -> 57.1 us  [run_combine(): pl.pallas_call(functools.partial(combine_kernel, src, init is not None),...]
  transfers between devices with their start and end apart: 22 -> 23, of which waited for: 8 -> 8; matrix products, arithmetic and copies ran while one was open for 7% -> 7% of each run, Pallas kernels for 45% -> 44%
where the time goes in v3:
time: 496 us; the launch traced here: 486 us
  Pallas kernels  293 us (59%)
  waiting for transfers between devices  120 us (24%)
  starting transfers between devices  23.6 us (5%)
  matrix products  21.6 us (4%)
  local copies, waits for them, and re-layouts  16 us (3%)
  other arithmetic  11.1 us (2%)
    pallas_call x1, Pallas kernels, run_experts(): pl.pallas_call(expert_kernel, grid_spec=grid_spec, out_shape=jax.ShapeDty...  97.6 us
    pallas_call x3, Pallas kernels, run_ffn(): pl.pallas_call(functools.partial(ffn_kernel, n_up, len(adds)), grid_spec=...  89.2 us
    ppermute x8, waiting for transfers between devices, over_tp(): return lax.ppermute(v, 'tp', [(0, 1), (1, 0)])  75.7 us
    pallas_call x6, Pallas kernels, run_combine(): pl.pallas_call(functools.partial(combine_kernel, src, init is not None),...  57.1 us
    ppermute x7, waiting for transfers between devices, over_x(): return lax.ppermute(v, 'ep', [(i, i ^ 2) for i in range(4)])  43.6 us
    pallas_call x1, Pallas kernels, attention(): pl.pallas_call(attn_kernel, grid=(steps,), in_specs=[col, col, col, tab,...  21.2 us
    pallas_call x1, Pallas kernels, run_out(): pl.pallas_call(out_kernel, grid_spec=grid_spec, out_shape=[jax.ShapeDtype...  16.7 us
    ppermute x7, starting transfers between devices, over_x(): return lax.ppermute(v, 'ep', [(i, i ^ 2) for i in range(4)])  12.4 us
  transfers between devices with their start and end apart: 23, of which 8 were waited for; matrix products, arithmetic and copies ran while one was open for 7% of the time, Pallas kernels for 44%

profile of v3, /device:TPU:0, one launch (start us, length us, event | category | flops | bytes accessed | tf_op | source)
XLA Modules:
  0.0 486.5 jit_solution(7088265468056618569)
XLA Ops:
  0.0 3.1 multiply_reduce_fusion
  5.5 3.3 collective-permute-start.7
  8.9 8.6 %fusion.7.q_ref = f32[1024,1024]{1,0:T(8,128)} fusion(bf16[256,8,8,128]{3,2,1,0:T(8,128)(2,1)} %bitcast.71, bf16[1,1024,2048]{2,1,0:T(8,128)(2,1)S(1)} %copy-done.10, f32[2048]{0:T(1024)S(1)} %convert_element_type.53, f32[1024]{0:T(1024)S(1)} %add_rsqrt_fusion), kind=kOutput, calls=%fused_computation.9 | convolution fusion | flops 4303355904 | bytes 12595200 | tf_op jit(solution)/shard_map/dot_general | solution.py:437
  17.5 6.2 %fusion.4.k_ref = f32[1024,1024]{1,0:T(8,128)} fusion(bf16[256,8,8,128]{3,2,1,0:T(8,128)(2,1)S(1)} %bitcast.72, bf16[1,1024,2048]{2,1,0:T(8,128)(2,1)S(1)} %copy-done.10, f32[2048]{0:T(1024)S(1)} %convert_element_type.53, f32[1024]{0:T(1024)S(1)} %add_rsqrt_fusion), kind=kOutput, calls=%fused_computation.6 | convolution fusion | flops 4303355904 | bytes 12595200 | tf_op jit(solution)/shard_map/dot_general | solution.py:438
  23.7 5.8 %fusion.12.v_ref = bf16[1024,1024]{1,0:T(8,128)(2,1)} fusion(bf16[256,8,8,128]{3,2,1,0:T(8,128)(2,1)S(1)} %bitcast.73, bf16[1,1024,2048]{2,1,0:T(8,128)(2,1)S(1)} %copy-done.10, f32[2048]{0:T(1024)S(1)} %convert_element_type.53, f32[1024]{0:T(1024)S(1)} %add_rsqrt_fusion), kind=kOutput, calls=%fused_computation.15 | convolution fusion | flops 4304404480 | bytes 10498048 | tf_op jit(solution)/shard_map/dot_general | solution.py:439
  29.5 21.2 %attn.1._after.ctx_ref = bf16[1024,1024]{1,0:T(8,128)(2,1)} custom-call(f32[1024,1024]{1,0:T(8,128)} %fusion.7.q_ref, f32[1024,1024]{1,0:T(8,128)} %fusion.4.k_ref, bf16[1024,1024]{1,0:T(8,128)(2,1)} %fusion.12.v_ref, f32[1024,128]{1,0:T(8,128)} %constant.64.clone.cos_ref, f32[1024,128]{1,0:T(8,128)} %constant.65.clone.sin_ref), custom_call_target="tpu_custom_call" | custom-call | flops 4294967296 | bytes 12582912 | tf_op jit(solution)/shard_map/attn/pallas_call | solution.py:68
  57.4 7.0 %collective-permute-done.5 = f32[512,16]{1,0:T(8,128)S(1)} collective-permute-done((f32[512,16]{1,0:T(8,128)S(1)}, f32[512,16]{1,0:T(8,128)S(1)}, u32[]{:S(2)}, u32[]{:S(2)}) %collective-permute-start.5) | collective-permute-done | bytes 32800 | tf_op jit(solution)/shard_map/ppermute | solution.py:370
  68.6 53.0 %collective-permute-done.1.w0_ref = bf16[256,2048]{1,0:T(8,128)(2,1)} collective-permute-done((bf16[256,2048]{1,0:T(8,128)(2,1)}, bf16[256,2048]{1,0:T(8,128)(2,1)}, u32[]{:S(2)}, u32[]{:S(2)}) %collective-permute-start.1) | collective-permute-done | bytes 1048608 | tf_op jit(solution)/shard_map/ppermute | solution.py:376
  127.9 18.7 %collective-permute-done.3.w2_ref = bf16[256,2048]{1,0:T(8,128)(2,1)} collective-permute-done((bf16[256,2048]{1,0:T(8,128)(2,1)}, bf16[256,2048]{1,0:T(8,128)(2,1)}, u32[]{:S(2)}, u32[]{:S(2)}) %collective-permute-start.3) | collective-permute-done | bytes 1048608 | tf_op jit(solution)/shard_map/ppermute | solution.py:370
  146.6 97.6 %experts.1._after.y_hbm = bf16[4,3328,2048]{2,1,0:T(8,128)(2,1)} custom-call(s32[4,16]{1,0:T(4,128)} %copy-done.21, s32[4,16]{1,0:T(4,128)} %select_reduce_fusion.3.loc_ref, s32[4,16]{1,0:T(4,128)} %copy-done.25, s32[4,16,1,512]{3,2,1,0:T(1,128)} %broadcast_in_dim.104.rank_ref, bf16[512,2048]{1,0:T(8,128)(2,1)} %copy-done.12, ...), custom_call_target="tpu_custom_call" | custom-call | flops 89999998976 | bytes 241326592 | tf_op jit(solution)/shard_map/experts/pallas_call | solution.py:159
  244.3 16.7 %out_proj.1 = (bf16[1024,2048]{1,0:T(8,128)(2,1)}, bf16[1024,2048]{1,0:T(8,128)(2,1)}) custom-call(s32[4]{0:T(128)} %iota_xor_fusion.q_ref, bf16[1024,2048]{1,0:T(8,128)(2,1)} %bitcast.62, bf16[1,2048]{1,0:T(2,128)(2,1)} %reshape.178.gain_ref, bf16[1024,1024]{1,0:T(8,128)(2,1)} %attn.1._after.ctx_ref, bf16[1024,1024]{1,0:T(8,128)(2,1)} %collective-permute-done.peer_ref, ...), custom_call_target="tpu_custom_call" | custom-call | flops 10000000000 | bytes 24000000 | tf_op jit(solution)/shard_map/out_proj/pallas_call | solution.py:289
  261.0 34.5 %ffn.3 = (f32[256,2048]{1,0:T(8,128)}, f32[256,2048]{1,0:T(8,128)}) custom-call(s32[1]{0:T(128)} %bitcast.19.off_ref, bf16[1024,2048]{1,0:T(8,128)(2,1)} %get-tuple-element.17.x_ref, bf16[2048,4096]{1,0:T(8,128)(2,1)} %wg_ref.7, bf16[2048,4096]{1,0:T(8,128)(2,1)} %wu_ref.7, bf16[4096,2048]{1,0:T(8,128)(2,1)} %wd_ref.7, ...), custom_call_target="tpu_custom_call" | custom-call | flops 28672000000 | bytes 60000000 | tf_op jit(solution)/shard_map/ffn/pallas_call | solution.py:337
  297.2 7.5 %shard_map.172._after = f32[256,2048]{1,0:T(8,128)S(1)} custom-call(s32[4]{0:T(128)S(1)} %get-tuple-element.29.rows_ref, s32[512,8]{1,0:T(8,128)S(1)} %get-tuple-element.33.pos_ref, f32[512,8]{1,0:T(8,128)S(1)} %get-tuple-element.37.gate_ref, bf16[4,3328,2048]{2,1,0:T(8,128)(2,1)} %experts.1._after.y_hbm, f32[256,2048]{1,0:T(8,128)S(1)} %copy-done.3), custom_call_target="tpu_custom_call" | custom-call | flops 12000000000 | bytes 10000000 | tf_op jit(solution)/shard_map/pallas_call | solution.py:255
  304.7 7.5 %shard_map.173._after = f32[256,2048]{1,0:T(8,128)S(1)} custom-call(s32[4]{0:T(128)S(1)} %get-tuple-element.29.rows_ref, s32[512,8]{1,0:T(8,128)S(1)} %get-tuple-element.33.pos_ref, f32[512,8]{1,0:T(8,128)S(1)} %get-tuple-element.37.gate_ref, bf16[4,3328,2048]{2,1,0:T(8,128)(2,1)} %experts.1._after.y_hbm, f32[256,2048]{1,0:T(8,128)S(1)} %shard_map.172._after), custom_call_target="tpu_custom_call" | custom-call | flops 12000000000 | bytes 10000000 | tf_op jit(solution)/shard_map/pallas_call | solution.py:255
  312.9 8.6 %shard_map.174 = (f32[128,2048]{1,0:T(8,128)S(1)}, f32[128,2048]{1,0:T(8,128)}) custom-call(s32[4]{0:T(128)S(1)} %get-tuple-element.29.rows_ref, s32[512,8]{1,0:T(8,128)S(1)} %get-tuple-element.34.pos_ref, f32[512,8]{1,0:T(8,128)S(1)} %slice_bitcast_fusion.2.gate_ref, bf16[4,3328,2048]{2,1,0:T(8,128)(2,1)} %experts.1._after.y_hbm, ...), custom_call_target="tpu_custom_call" | custom-call | flops 12000000000 | bytes 10000000 | tf_op jit(solution)/shard_map/pallas_call | solution.py:255
  321.6 7.5 %shard_map.175 = (f32[128,2048]{1,0:T(8,128)S(1)}, f32[128,2048]{1,0:T(8,128)S(1)}) custom-call(s32[4]{0:T(128)S(1)} %get-tuple-element.29.rows_ref, s32[512,8]{1,0:T(8,128)S(1)} %get-tuple-element.34.pos_ref, f32[512,8]{1,0:T(8,128)S(1)} %slice_bitcast_fusion.2.gate_ref, bf16[4,3328,2048]{2,1,0:T(8,128)(2,1)} %experts.1._after.y_hbm, ...), custom_call_target="tpu_custom_call" | custom-call | flops 12000000000 | bytes 10000000 | tf_op jit(solution)/shard_map/pallas_call | solution.py:255
  330.1 14.1 %shard_map.176._after = f32[512,2048]{1,0:T(8,128)} custom-call(s32[4]{0:T(128)S(1)} %get-tuple-element.29.rows_ref, s32[512,8]{1,0:T(8,128)S(1)} %copy-done.8, f32[512,8]{1,0:T(8,128)S(1)} %copy-done.6, bf16[4,3328,2048]{2,1,0:T(8,128)(2,1)} %experts.1._after.y_hbm, f32[128,2048]{1,0:T(8,128)S(1)} %get-tuple-element.21._after), custom_call_target="tpu_custom_call" | custom-call | flops 12000000000 | bytes 10000000 | tf_op jit(solution)/shard_map/pallas_call | solution.py:255
  347.4 3.8 collective-permute-start.14
  352.1 11.8 %shard_map.177._after.rest_1_ = f32[512,2048]{1,0:T(8,128)S(1)} custom-call(s32[4]{0:T(128)S(1)} %get-tuple-element.29.rows_ref, s32[512,8]{1,0:T(8,128)S(1)} %copy-done.7, f32[512,8]{1,0:T(8,128)S(1)} %slice_bitcast_fusion.6.gate_ref, bf16[4,3328,2048]{2,1,0:T(8,128)(2,1)} %experts.1._after.y_hbm, f32[512,2048]{1,0:T(8,128)} %shard_map.176._after), custom_call_target="tpu_custom_call" | custom-call | flops 12000000000 | bytes 10000000 | tf_op jit(solution)/shard_map/pallas_call | solution.py:255
  367.9 27.4 %ffn.4 = (f32[128,2048]{1,0:T(8,128)}, f32[128,2048]{1,0:T(8,128)}) custom-call(s32[1]{0:T(128)} %bitcast.off_ref, bf16[1024,2048]{1,0:T(8,128)(2,1)} %get-tuple-element.17.x_ref, bf16[2048,4096]{1,0:T(8,128)(2,1)} %wg_ref.7, bf16[2048,4096]{1,0:T(8,128)(2,1)} %wu_ref.7, bf16[4096,2048]{1,0:T(8,128)(2,1)} %wd_ref.7, f32[512,2048]{1,0:T(8,128)} %copy-done.2, ...), custom_call_target="tpu_custom_call" | custom-call | flops 14336000000 | bytes 60000000 | tf_op jit(solution)/shard_map/ffn/pallas_call | solution.py:337
  402.5 17.9 %collective-permute-done.16.x_ref = f32[128,2048]{1,0:T(8,128)} collective-permute-done((f32[128,2048]{1,0:T(8,128)}, f32[128,2048]{1,0:T(8,128)}, u32[]{:S(2)}, u32[]{:S(2)}) %collective-permute-start.16) | collective-permute-done | bytes 1048608 | tf_op jit(solution)/shard_map/ppermute | solution.py:370
  425.2 27.3 %ffn.5 = (f32[128,2048]{1,0:T(8,128)}, f32[128,2048]{1,0:T(8,128)}) custom-call(s32[1]{0:T(128)} %bitcast.20.off_ref, bf16[1024,2048]{1,0:T(8,128)(2,1)} %get-tuple-element.17.x_ref, bf16[2048,4096]{1,0:T(8,128)(2,1)} %wg_ref.7, bf16[2048,4096]{1,0:T(8,128)(2,1)} %wu_ref.7, bf16[4096,2048]{1,0:T(8,128)(2,1)} %wd_ref.7, bf16[128,2048]{1,0:T(8,128)(2,1)} %final.5._after, ...), custom_call_target="tpu_custom_call" | custom-call | flops 14336000000 | bytes 60000000 | tf_op jit(solution)/shard_map/ffn/pallas_call | solution.py:337
  461.4 11.1 %collective-permute-done.20 = bf16[128,2048]{1,0:T(8,128)(2,1)S(1)} collective-permute-done((bf16[128,2048]{1,0:T(8,128)(2,1)}, bf16[128,2048]{1,0:T(8,128)(2,1)S(1)}, u32[]{:S(2)}, u32[]{:S(2)}) %collective-permute-start.20) | collective-permute-done | bytes 524320 | tf_op jit(solution)/shard_map/ppermute | solution.py:376
  472.6 10.7 %collective-permute-done.22 = bf16[128,2048]{1,0:T(8,128)(2,1)S(1)} collective-permute-done((bf16[128,2048]{1,0:T(8,128)(2,1)}, bf16[128,2048]{1,0:T(8,128)(2,1)S(1)}, u32[]{:S(2)}, u32[]{:S(2)}) %collective-permute-start.22) | collective-permute-done | bytes 524320 | tf_op jit(solution)/shard_map/ppermute | solution.py:376
  (144 shorter events, 54.4 us)
Async XLA Ops:
  5.5 59.8 %collective-permute-start.7 = (bf16[512,2048]{1,0:T(8,128)(2,1)S(1)}, bf16[512,2048]{1,0:T(8,128)(2,1)}, u32[]{:S(2)}, u32[]{:S(2)}) collective-permute-start(bf16[512,2048]{1,0:T(8,128)(2,1)S(1)} %fusion.11.u0_ref), channel_id=1, source_target_pairs={{0,2},{1,3},{2,0},{3,1},{4,6},{5,7},{6,4},{7,5}} | collective-permute-start | bytes 6291464 | tf_op jit(solution)/shard_map/ppermute | solution.py:370
  8.9 137.7 %collective-permute-start.8 = (bf16[512,2048]{1,0:T(8,128)(2,1)S(1)}, bf16[512,2048]{1,0:T(8,128)(2,1)}, u32[]{:S(2)}, u32[]{:S(2)}) collective-permute-start(bf16[512,2048]{1,0:T(8,128)(2,1)S(1)} %fusion.11.u0_ref), channel_id=1, source_target_pairs={{0,1},{1,0},{2,3},{3,2},{4,5},{5,4},{6,7},{7,6}} | collective-permute-start | bytes 6291464 | tf_op jit(solution)/shard_map/ppermute | solution.py:373
  50.7 193.5 %collective-permute-start = (bf16[1024,1024]{1,0:T(8,128)(2,1)}, bf16[1024,1024]{1,0:T(8,128)(2,1)}, u32[]{:S(2)}, u32[]{:S(2)}) collective-permute-start(bf16[1024,1024]{1,0:T(8,128)(2,1)} %attn.1._after.ctx_ref), channel_id=1, source_target_pairs={{0,4},{4,0},{1,5},{5,1},{2,6},{6,2},{3,7},{7,3}} | collective-permute-start | bytes 6291464 | tf_op jit(solution)/shard_map/ppermute | solution.py:376
  54.6 67.0 %collective-permute-start.1 = (bf16[256,2048]{1,0:T(8,128)(2,1)}, bf16[256,2048]{1,0:T(8,128)(2,1)}, u32[]{:S(2)}, u32[]{:S(2)}) collective-permute-start(bf16[256,2048]{1,0:T(8,128)(2,1)} %constant_dynamic-slice_fusion), channel_id=1, source_target_pairs={{0,4},{4,0},{1,5},{5,1},{2,6},{6,2},{3,7},{7,3}} | collective-permute-start | bytes 3145736 | tf_op jit(solution)/shard_map/ppermute | solution.py:376
  56.2 8.2 %collective-permute-start.5 = (f32[512,16]{1,0:T(8,128)S(1)}, f32[512,16]{1,0:T(8,128)S(1)}, u32[]{:S(2)}, u32[]{:S(2)}) collective-permute-start(f32[512,16]{1,0:T(8,128)S(1)} %copy.35), channel_id=1, source_target_pairs={{0,2},{1,3},{2,0},{3,1},{4,6},{5,7},{6,4},{7,5}} | collective-permute-start | bytes 98312 | tf_op jit(solution)/shard_map/ppermute | solution.py:370
  65.3 2.1 collective-permute-start.6
  65.3 81.3 %collective-permute-start.9 = (bf16[512,2048]{1,0:T(8,128)(2,1)}, bf16[512,2048]{1,0:T(8,128)(2,1)}, u32[]{:S(2)}, u32[]{:S(2)}) collective-permute-start(bf16[512,2048]{1,0:T(8,128)(2,1)} %collective-permute-done.7.u1_ref), channel_id=1, source_target_pairs={{0,1},{1,0},{2,3},{3,2},{4,5},{5,4},{6,7},{7,6}} | collective-permute-start | bytes 6291464 | tf_op jit(solution)/shard_map/ppermute | solution.py:373
  68.1 78.5 %copy-start.21 = (s32[4,16]{1,0:T(4,128)}, s32[4,16]{1,0:T(4,128)S(1)}, u32[]{:S(2)}) copy-start(s32[4,16]{1,0:T(4,128)S(1)} %convert_reduce_fusion.n_ref) | copy-start | bytes 772
  121.6 25.0 %collective-permute-start.3 = (bf16[256,2048]{1,0:T(8,128)(2,1)}, bf16[256,2048]{1,0:T(8,128)(2,1)}, u32[]{:S(2)}, u32[]{:S(2)}) collective-permute-start(bf16[256,2048]{1,0:T(8,128)(2,1)} %collective-permute-done.1.w0_ref), channel_id=1, source_target_pairs={{0,2},{1,3},{2,0},{3,1},{4,6},{5,7},{6,4},{7,5}} | collective-permute-start | bytes 3145736 | tf_op jit(solution)/shard_map/ppermute | solution.py:370
  127.9 116.4 %collective-permute-start.2 = (bf16[256,2048]{1,0:T(8,128)(2,1)}, bf16[256,2048]{1,0:T(8,128)(2,1)}, u32[]{:S(2)}, u32[]{:S(2)}) collective-permute-start(bf16[256,2048]{1,0:T(8,128)(2,1)} %collective-permute-done.1.w0_ref), channel_id=1, source_target_pairs={{0,1},{1,0},{2,3},{3,2},{4,5},{5,4},{6,7},{7,6}} | collective-permute-start | bytes 3145736 | tf_op jit(solution)/shard_map/ppermute | solution.py:373
  146.6 97.7 %collective-permute-start.4 = (bf16[256,2048]{1,0:T(8,128)(2,1)}, bf16[256,2048]{1,0:T(8,128)(2,1)}, u32[]{:S(2)}, u32[]{:S(2)}) collective-permute-start(bf16[256,2048]{1,0:T(8,128)(2,1)} %collective-permute-done.3.w2_ref), channel_id=1, source_target_pairs={{0,1},{1,0},{2,3},{3,2},{4,5},{5,4},{6,7},{7,6}} | collective-permute-start | bytes 3145736 | tf_op jit(solution)/shard_map/ppermute | solution.py:373
  304.7 8.2 %collective-permute-start.10 = (f32[256,2048]{1,0:T(8,128)S(1)}, f32[256,2048]{1,0:T(8,128)S(1)}, u32[]{:S(2)}, u32[]{:S(2)}) collective-permute-start(f32[256,2048]{1,0:T(8,128)S(1)} %shard_map.172._after), channel_id=1, source_target_pairs={{0,1},{1,0},{2,3},{3,2},{4,5},{5,4},{6,7},{7,6}} | collective-permute-start | bytes 6291464 | tf_op jit(solution)/shard_map/ppermute | solution.py:373
  312.3 9.3 %collective-permute-start.11 = (f32[256,2048]{1,0:T(8,128)S(1)}, f32[256,2048]{1,0:T(8,128)S(1)}, u32[]{:S(2)}, u32[]{:S(2)}) collective-permute-start(f32[256,2048]{1,0:T(8,128)S(1)} %shard_map.173._after), channel_id=1, source_target_pairs={{0,1},{1,0},{2,3},{3,2},{4,5},{5,4},{6,7},{7,6}} | collective-permute-start | bytes 6291464 | tf_op jit(solution)/shard_map/ppermute | solution.py:373
  344.2 21.8 %collective-permute-start.12 = (f32[512,2048]{1,0:T(8,128)}, f32[512,2048]{1,0:T(8,128)}, u32[]{:S(2)}, u32[]{:S(2)}) collective-permute-start(f32[512,2048]{1,0:T(8,128)} %shard_map.176._after), channel_id=1, source_target_pairs={{0,1},{1,0},{2,3},{3,2},{4,5},{5,4},{6,7},{7,6}} | collective-permute-start | bytes 12582920 | tf_op jit(solution)/shard_map/ppermute | solution.py:373
  345.3 50.0 %collective-permute-start.13 = (f32[256,2048]{1,0:T(8,128)S(1)}, f32[256,2048]{1,0:T(8,128)}, u32[]{:S(2)}, u32[]{:S(2)}) collective-permute-start(f32[256,2048]{1,0:T(8,128)S(1)} %copy-done.4), channel_id=1, source_target_pairs={{0,4},{4,0},{1,5},{5,1},{2,6},{6,2},{3,7},{7,3}} | collective-permute-start | bytes 6291464 | tf_op jit(solution)/shard_map/ppermute | solution.py:376
  347.2 105.3 %collective-permute-start.18 = (f32[256,2048]{1,0:T(8,128)}, f32[256,2048]{1,0:T(8,128)}, u32[]{:S(2)}, u32[]{:S(2)}) collective-permute-start(f32[256,2048]{1,0:T(8,128)} %get-tuple-element.26), channel_id=1, source_target_pairs={{0,4},{4,0},{1,5},{5,1},{2,6},{6,2},{3,7},{7,3}} | collective-permute-start | bytes 6291464 | tf_op jit(solution)/shard_map/ppermute | solution.py:376
  347.4 50.3 %collective-permute-start.14 = (f32[128,2048]{1,0:T(8,128)}, f32[128,2048]{1,0:T(8,128)}, u32[]{:S(2)}, u32[]{:S(2)}) collective-permute-start(f32[128,2048]{1,0:T(8,128)} %copy-done.5), channel_id=1, source_target_pairs={{0,2},{1,3},{2,0},{3,1},{4,6},{5,7},{6,4},{7,5}} | collective-permute-start | bytes 3145736 | tf_op jit(solution)/shard_map/ppermute | solution.py:370
  351.1 101.4 %collective-permute-start.19 = (f32[128,2048]{1,0:T(8,128)S(1)}, f32[128,2048]{1,0:T(8,128)}, u32[]{:S(2)}, u32[]{:S(2)}) collective-permute-start(f32[128,2048]{1,0:T(8,128)S(1)} %get-tuple-element.21._after), channel_id=1, source_target_pairs={{0,2},{1,3},{2,0},{3,1},{4,6},{5,7},{6,4},{7,5}} | collective-permute-start | bytes 3145736 | tf_op jit(solution)/shard_map/ppermute | solution.py:370
  365.9 54.5 %collective-permute-start.16 = (f32[128,2048]{1,0:T(8,128)}, f32[128,2048]{1,0:T(8,128)}, u32[]{:S(2)}, u32[]{:S(2)}) collective-permute-start(f32[128,2048]{1,0:T(8,128)} %get-tuple-element.24), channel_id=1, source_target_pairs={{0,2},{1,3},{2,0},{3,1},{4,6},{5,7},{6,4},{7,5}} | collective-permute-start | bytes 3145736 | tf_op jit(solution)/shard_map/ppermute | solution.py:370
  395.3 60.1 %collective-permute-start.21 = (f32[128,2048]{1,0:T(8,128)}, f32[128,2048]{1,0:T(8,128)}, u32[]{:S(2)}, u32[]{:S(2)}) collective-permute-start(f32[128,2048]{1,0:T(8,128)} %copy-done.9), channel_id=1, source_target_pairs={{0,2},{1,3},{2,0},{3,1},{4,6},{5,7},{6,4},{7,5}} | collective-permute-start | bytes 3145736 | tf_op jit(solution)/shard_map/ppermute | solution.py:370
  400.5 59.8 %collective-permute-start.15 = (bf16[128,2048]{1,0:T(8,128)(2,1)}, bf16[128,2048]{1,0:T(8,128)(2,1)S(1)}, u32[]{:S(2)}, u32[]{:S(2)}) collective-permute-start(bf16[128,2048]{1,0:T(8,128)(2,1)} %final.4), channel_id=1, source_target_pairs={{0,4},{4,0},{1,5},{5,1},{2,6},{6,2},{3,7},{7,3}} | collective-permute-start | bytes 1572872 | tf_op jit(solution)/shard_map/ppermute | solution.py:376
  423.2 38.1 %collective-permute-start.17 = (bf16[128,2048]{1,0:T(8,128)(2,1)}, bf16[128,2048]{1,0:T(8,128)(2,1)S(1)}, u32[]{:S(2)}, u32[]{:S(2)}) collective-permute-start(bf16[128,2048]{1,0:T(8,128)(2,1)} %final.5._after), channel_id=1, source_target_pairs={{0,4},{4,0},{1,5},{5,1},{2,6},{6,2},{3,7},{7,3}} | collective-permute-start | bytes 1572872 | tf_op jit(solution)/shard_map/ppermute | solution.py:376
  455.4 17.1 %collective-permute-start.20 = (bf16[128,2048]{1,0:T(8,128)(2,1)}, bf16[128,2048]{1,0:T(8,128)(2,1)S(1)}, u32[]{:S(2)}, u32[]{:S(2)}) collective-permute-start(bf16[128,2048]{1,0:T(8,128)(2,1)} %final.6), channel_id=1, source_target_pairs={{0,4},{4,0},{1,5},{5,1},{2,6},{6,2},{3,7},{7,3}} | collective-permute-start | bytes 1572872 | tf_op jit(solution)/shard_map/ppermute | solution.py:376
  458.3 25.0 %collective-permute-start.22 = (bf16[128,2048]{1,0:T(8,128)(2,1)}, bf16[128,2048]{1,0:T(8,128)(2,1)S(1)}, u32[]{:S(2)}, u32[]{:S(2)}) collective-permute-start(bf16[128,2048]{1,0:T(8,128)(2,1)} %final.7), channel_id=1, source_target_pairs={{0,4},{4,0},{1,5},{5,1},{2,6},{6,2},{3,7},{7,3}} | collective-permute-start | bytes 1572872 | tf_op jit(solution)/shard_map/ppermute | solution.py:376
  (27 other events, 456.2 us)

commit v4 on v3

--- a/solution.py
+++ b/solution.py
@@ -34,29 +34,38 @@
     return np.concatenate([cos_tab, cos_tab], axis=1), np.concatenate([-sin_tab, sin_tab], axis=1)
 
 
-def attn_kernel(q_ref, k_ref, v_ref, cos_ref, sin_ref, o_ref, k_scr):
+def attn_kernel(q_ref, k_ref, v_ref, cos_ref, sin_ref, o_ref, k_scr, *bufs):
     seq, hd = cos_ref.shape
-    blk = 256
+    blk, strip = 256, 32
+    factor = hd ** -0.5 * 1.4426950408889634
     pair = q_ref.shape[1] // hd
     for h in range(pair):
         hc = slice(h * hd, (h + 1) * hd)
         k_f = k_ref[:, hc]
         k_scr[:, hc] = (k_f * cos_ref[...] + pltpu.roll(k_f, hd // 2, 1) * sin_ref[...]).astype(BF16)
+    r_id = lax.broadcasted_iota(jnp.int32, (strip, blk), 0)
+    c_id = lax.broadcasted_iota(jnp.int32, (strip, blk), 1)
     for i in range(seq // blk):
         rows = slice(i * blk, (i + 1) * blk)
         kv = (i + 1) * blk
         for h in range(pair):
+            s_scr, p_scr = bufs[2 * h], bufs[2 * h + 1]
             hc = slice(h * hd, (h + 1) * hd)
             q_f = q_ref[rows, hc]
             q_b = (q_f * cos_ref[rows] + pltpu.roll(q_f, hd // 2, 1) * sin_ref[rows]).astype(BF16)
-            s = lax.dot_general(q_b, k_scr[:kv, hc], (((1,), (1,)), ((), ())), preferred_element_type=F32) * hd ** -0.5
-            r_id = lax.broadcasted_iota(jnp.int32, (blk, blk), 0)
-            c_id = lax.broadcasted_iota(jnp.int32, (blk, blk), 1)
-            last = jnp.where(r_id >= c_id, s[:, kv - blk:], -1e30)
-            s = last if i == 0 else jnp.concatenate([s[:, :kv - blk], last], axis=1)
-            p = jnp.exp(s - jnp.max(s, axis=1, keepdims=True))
-            p = (p * (1.0 / jnp.sum(p, axis=1, keepdims=True))).astype(BF16)
-            o_ref[rows, hc] = jnp.dot(p, v_ref[:kv, hc], preferred_element_type=F32).astype(BF16)
+            s_scr[:, :kv] = lax.dot_general(q_b, k_scr[:kv, hc], (((1,), (1,)), ((), ())), preferred_element_type=F32)
+        for h in range(pair):
+            s_scr, p_scr = bufs[2 * h], bufs[2 * h + 1]
+            for t in range(blk // strip):
+                sr = slice(t * strip, (t + 1) * strip)
+                last = jnp.where(r_id + t * strip >= c_id, s_scr[sr, kv - blk:kv], -1e30)
+                s = last if i == 0 else jnp.concatenate([s_scr[sr, :kv - blk], last], axis=1)
+                p = jnp.exp2((s - jnp.max(s, axis=1, keepdims=True)) * factor)
+                p_scr[sr, :kv] = (p * (1.0 / jnp.sum(p, axis=1, keepdims=True))).astype(BF16)
+        for h in range(pair):
+            s_scr, p_scr = bufs[2 * h], bufs[2 * h + 1]
+            hc = slice(h * hd, (h + 1) * hd)
+            o_ref[rows, hc] = jnp.dot(p_scr[:, :kv], v_ref[:kv, hc], preferred_element_type=F32).astype(BF16)
 
 
 def attention(q, k, v, cos_t, sin_t, head_dim):
@@ -69,7 +78,7 @@
         attn_kernel, grid=(steps,),
         in_specs=[col, col, col, tab, tab], out_specs=col,
         out_shape=jax.ShapeDtypeStruct((seq, width), BF16),
-        scratch_shapes=[pltpu.VMEM((seq, pair * head_dim), BF16)],
+        scratch_shapes=[pltpu.VMEM((seq, pair * head_dim), BF16)] + [pltpu.VMEM((256, seq), F32), pltpu.VMEM((256, seq), BF16)] * pair,
         cost_estimate=pl.CostEstimate(flops=width * seq * seq * 4, bytes_accessed=12 * seq * width, transcendentals=0),
         name="attn",
     )(q, k, v, cos_t, sin_t)
@@ -343,19 +352,19 @@
     )(which.reshape(1), f_norm, wg, wu, wd, after, *[v for v, _ in adds])
 
 
-def final_kernel(s_ref, g_ref, x_ref, o_ref):
-    o_ref[...] = ((s_ref[...] + g_ref[...]) + x_ref[...]).astype(BF16)
-
-
-def run_final(s_own, f_got, got_block, m_got, m_block):
-    rows, d = s_own.shape
-    row = lambda b: pl.BlockSpec((rows, d), lambda i, b=b: (b, 0))
-    return pl.pallas_call(
-        final_kernel, grid=(1,), in_specs=[row(0), row(got_block), row(m_block)], out_specs=row(0),
+def final_kernel(s_ref, g_ref, m_ref, c_ref, x_ref, o_ref):
+    o_ref[...] = ((s_ref[...] + g_ref[...]) + ((m_ref[...] + c_ref[...]) + x_ref[...])).astype(BF16)
+
+
+def run_final(arrays):
+    rows, d = arrays[-1][0].shape
+    in_specs = [pl.BlockSpec((rows, d), lambda i, b=b: (b, 0)) for _, b in arrays]
+    return pl.pallas_call(
+        final_kernel, grid=(1,), in_specs=in_specs, out_specs=pl.BlockSpec((rows, d), lambda i: (0, 0)),
         out_shape=jax.ShapeDtypeStruct((rows, d), BF16),
-        cost_estimate=pl.CostEstimate(flops=3 * rows * d, bytes_accessed=14 * rows * d, transcendentals=0),
+        cost_estimate=pl.CostEstimate(flops=5 * rows * d, bytes_accessed=22 * rows * d, transcendentals=0),
         name="final",
-    )(s_own, f_got, m_got)
+    )(*[v for v, _ in arrays])
 
 
 def solution(mesh):
@@ -462,18 +471,19 @@
             tie = m1[0]
             for k in range(CHUNKS // 2):
                 m_x.append(over_x(m1[k]))
-        m2, = run_combine(2, rows, pos, gates_all, y_all, tie)
-        got2 = over_core(m2)
-        m0, = run_combine(0, rows, pos, gates_all, y_all, m2)
-
+
+        s_own, = run_ffn(my_tp, half, f_norm, w_gate, w_up, w_down, tie, adds=((after, None),))
         own, peer = [], []
-        tie = m0
+        tie = s_own
+        per = CHUNKS // 2
         for p in range(2):
-            s_own = run_ffn(2 * my_tp + p, half // 2, f_norm, w_gate, w_up, w_down, tie,
-                            adds=((after, None), (m0, p), (got2, p)), n_out=CHUNKS // 2)
-            for k in range(CHUNKS // 2):
-                c = p * (CHUNKS // 2) + k
-                o_c = run_final(s_own[k], f_got[p], k, m_x[c], 0)
+            m2, = run_combine(2, rows, pos, gates_all, y_all, tie, part=(p, 2))
+            got2 = over_core(m2)
+            m0, = run_combine(0, rows, pos, gates_all, y_all, m2, part=(p, 2))
+            tie = m0
+            for k in range(per):
+                c = p * per + k
+                o_c = run_final(((s_own, c), (f_got[p], k), (m0, k), (got2, k), (m_x[c], 0)))
                 tie = o_c
                 own.append(o_c)
                 peer.append(over_tp(o_c))

time: 496 us -> 466 us (0.940)
  waiting for transfers between devices: 120 us -> 100 us
  Pallas kernels: 293 us -> 276 us
  other arithmetic: 11.1 us -> 20.4 us
    ppermute x8, waiting for transfers between devices: 75.7 us -> 10.8 us  [over_tp(): return lax.ppermute(v, 'tp', [(0, 1), (1, 0)])]
    ppermute x7, waiting for transfers between devices: 43.6 us -> 88.3 us  [over_x(): return lax.ppermute(v, 'ep', [(i, i ^ 2) for i in range(4)])]
    pallas_call x3 -> x2, Pallas kernels: 89.2 us -> 69.4 us  [run_ffn(): pl.pallas_call(functools.partial(ffn_kernel, n_up, len(adds)), grid_spec=...]
    unnamed x7, other arithmetic: 0.88 us -> 9.58 us
    pallas_call x1, Pallas kernels: 21.2 us -> 15.6 us  [attention(): pl.pallas_call(attn_kernel, grid=(steps,), in_specs=[col, col, col, tab,...]
    pallas_call x6 -> x8, Pallas kernels: 57.1 us -> 62.2 us  [run_combine(): pl.pallas_call(functools.partial(combine_kernel, src, init is not None),...]
    unnamed x56 -> x68, local copies, waits for them, and re-layouts: 7.58 us -> 11.4 us
  transfers between devices with their start and end apart: 23 -> 24, of which waited for: 8 -> 7; matrix products, arithmetic and copies ran while one was open for 7% -> 8% of each run, Pallas kernels for 44% -> 47%
where the time goes in v4:
time: 466 us; the launch traced here: 460 us
  Pallas kernels  276 us (59%)
  waiting for transfers between devices  100 us (21%)
  matrix products  23.1 us (5%)
  starting transfers between devices  21.4 us (5%)
  other arithmetic  20.4 us (4%)
  local copies, waits for them, and re-layouts  18.5 us (4%)
    pallas_call x1, Pallas kernels, run_experts(): pl.pallas_call(expert_kernel, grid_spec=grid_spec, out_shape=jax.ShapeDty...  98.1 us
    ppermute x7, waiting for transfers between devices, over_x(): return lax.ppermute(v, 'ep', [(i, i ^ 2) for i in range(4)])  88.3 us
    pallas_call x2, Pallas kernels, run_ffn(): pl.pallas_call(functools.partial(ffn_kernel, n_up, len(adds)), grid_spec=...  69.4 us
    pallas_call x8, Pallas kernels, run_combine(): pl.pallas_call(functools.partial(combine_kernel, src, init is not None),...  62.2 us
    pallas_call x1, Pallas kernels, run_out(): pl.pallas_call(out_kernel, grid_spec=grid_spec, out_shape=[jax.ShapeDtype...  16.7 us
    pallas_call x1, Pallas kernels, attention(): pl.pallas_call(attn_kernel, grid=(steps,), in_specs=[col, col, col, tab,...  15.6 us
    pallas_call x4, Pallas kernels, run_final(): pl.pallas_call(final_kernel, grid=(1,), in_specs=in_specs, out_specs=pl.B...  14.1 us
    unnamed x68, local copies, waits for them, and re-layouts  11.4 us
  transfers between devices with their start and end apart: 24, of which 7 were waited for; matrix products, arithmetic and copies ran while one was open for 8% of the time, Pallas kernels for 47%

profile of v4, /device:TPU:0, one launch (start us, length us, event | category | flops | bytes accessed | tf_op | source)
XLA Modules:
  0.0 460.4 jit_solution(7871970561703358710)
XLA Ops:
  14.5 9.5 %fusion.12.v_ref = bf16[1024,1024]{1,0:T(8,128)(2,1)} fusion(bf16[256,8,8,128]{3,2,1,0:T(8,128)(2,1)} %bitcast.70, bf16[1,1024,2048]{2,1,0:T(8,128)(2,1)} %param.19, f32[2048]{0:T(1024)S(1)} %convert_element_type.53, f32[1024]{0:T(1024)S(1)} %add_rsqrt_fusion), kind=kOutput, calls=%fused_computation.15 | convolution fusion | flops 4304404480 | bytes 10498048 | tf_op jit(solution)/shard_map/dot_general | solution.py:448
  24.0 6.5 %fusion.4.k_ref = f32[1024,1024]{1,0:T(8,128)} fusion(bf16[256,8,8,128]{3,2,1,0:T(8,128)(2,1)S(1)} %bitcast.71, bf16[1,1024,2048]{2,1,0:T(8,128)(2,1)S(1)} %copy-done.15, f32[2048]{0:T(1024)S(1)} %convert_element_type.53, f32[1024]{0:T(1024)S(1)} %add_rsqrt_fusion), kind=kOutput, calls=%fused_computation.6 | convolution fusion | flops 4303355904 | bytes 12595200 | tf_op jit(solution)/shard_map/dot_general | solution.py:447
  30.5 6.1 %fusion.7.q_ref = f32[1024,1024]{1,0:T(8,128)} fusion(bf16[256,8,8,128]{3,2,1,0:T(8,128)(2,1)S(1)} %bitcast.72, bf16[1,1024,2048]{2,1,0:T(8,128)(2,1)S(1)} %copy-done.15, f32[2048]{0:T(1024)S(1)} %convert_element_type.53, f32[1024]{0:T(1024)S(1)} %add_rsqrt_fusion), kind=kOutput, calls=%fused_computation.9 | convolution fusion | flops 4303355904 | bytes 12595200 | tf_op jit(solution)/shard_map/dot_general | solution.py:446
  36.6 15.6 %attn.1._after.ctx_ref = bf16[1024,1024]{1,0:T(8,128)(2,1)} custom-call(f32[1024,1024]{1,0:T(8,128)} %fusion.7.q_ref, f32[1024,1024]{1,0:T(8,128)} %fusion.4.k_ref, bf16[1024,1024]{1,0:T(8,128)(2,1)} %fusion.12.v_ref, f32[1024,128]{1,0:T(8,128)} %constant.62.clone.cos_ref, f32[1024,128]{1,0:T(8,128)} %constant.63.clone.sin_ref), custom_call_target="tpu_custom_call" | custom-call | flops 4294967296 | bytes 12582912 | tf_op jit(solution)/shard_map/attn/pallas_call | solution.py:77
  53.4 7.3 %collective-permute-done.5 = f32[512,16]{1,0:T(8,128)S(1)} collective-permute-done((f32[512,16]{1,0:T(8,128)S(1)}, f32[512,16]{1,0:T(8,128)S(1)}, u32[]{:S(2)}, u32[]{:S(2)}) %collective-permute-start.5) | collective-permute-done | bytes 32800 | tf_op jit(solution)/shard_map/ppermute | solution.py:379
  72.3 18.1 %collective-permute-done.3.w2_ref = bf16[256,2048]{1,0:T(8,128)(2,1)} collective-permute-done((bf16[256,2048]{1,0:T(8,128)(2,1)}, bf16[256,2048]{1,0:T(8,128)(2,1)}, u32[]{:S(2)}, u32[]{:S(2)}) %collective-permute-start.3) | collective-permute-done | bytes 1048608 | tf_op jit(solution)/shard_map/ppermute | solution.py:379
  90.4 98.1 %experts.1._after.y_hbm = bf16[4,3328,2048]{2,1,0:T(8,128)(2,1)} custom-call(s32[4,16]{1,0:T(4,128)} %copy-done.27, s32[4,16]{1,0:T(4,128)} %select_reduce_fusion.3.loc_ref, s32[4,16]{1,0:T(4,128)} %copy-done.31, s32[4,16,1,512]{3,2,1,0:T(1,128)} %broadcast_in_dim.104.rank_ref, bf16[512,2048]{1,0:T(8,128)(2,1)} %copy-done.16, ...), custom_call_target="tpu_custom_call" | custom-call | flops 89999998976 | bytes 241326592 | tf_op jit(solution)/shard_map/experts/pallas_call | solution.py:168
  188.6 16.7 %out_proj.1 = (bf16[1024,2048]{1,0:T(8,128)(2,1)}, bf16[1024,2048]{1,0:T(8,128)(2,1)}) custom-call(s32[4]{0:T(128)} %iota_xor_fusion.q_ref, bf16[1024,2048]{1,0:T(8,128)(2,1)} %bitcast.61, bf16[1,2048]{1,0:T(2,128)(2,1)} %reshape.175.gain_ref, bf16[1024,1024]{1,0:T(8,128)(2,1)} %attn.1._after.ctx_ref, bf16[1024,1024]{1,0:T(8,128)(2,1)} %collective-permute-done.peer_ref, ...), custom_call_target="tpu_custom_call" | custom-call | flops 10000000000 | bytes 24000000 | tf_op jit(solution)/shard_map/out_proj/pallas_call | solution.py:298
  205.3 34.5 %ffn.2 = (f32[256,2048]{1,0:T(8,128)}, f32[256,2048]{1,0:T(8,128)}) custom-call(s32[1]{0:T(128)} %bitcast.15.off_ref, bf16[1024,2048]{1,0:T(8,128)(2,1)} %get-tuple-element.13.x_ref, bf16[2048,4096]{1,0:T(8,128)(2,1)} %wg_ref.5, bf16[2048,4096]{1,0:T(8,128)(2,1)} %wu_ref.5, bf16[4096,2048]{1,0:T(8,128)(2,1)} %wd_ref.5, ...), custom_call_target="tpu_custom_call" | custom-call | flops 28672000000 | bytes 60000000 | tf_op jit(solution)/shard_map/ffn/pallas_call | solution.py:346
  241.3 7.6 %shard_map.172._after = f32[256,2048]{1,0:T(8,128)S(1)} custom-call(s32[4]{0:T(128)S(1)} %get-tuple-element.21.rows_ref, s32[512,8]{1,0:T(8,128)S(1)} %get-tuple-element.27.pos_ref, f32[512,8]{1,0:T(8,128)S(1)} %get-tuple-element.30.gate_ref, bf16[4,3328,2048]{2,1,0:T(8,128)(2,1)} %experts.1._after.y_hbm, f32[256,2048]{1,0:T(8,128)S(1)} %copy-done.9), custom_call_target="tpu_custom_call" | custom-call | flops 12000000000 | bytes 10000000 | tf_op jit(solution)/shard_map/pallas_call | solution.py:264
  249.1 7.8 %shard_map.173._after = f32[256,2048]{1,0:T(8,128)S(1)} custom-call(s32[4]{0:T(128)S(1)} %get-tuple-element.21.rows_ref, s32[512,8]{1,0:T(8,128)S(1)} %get-tuple-element.27.pos_ref, f32[512,8]{1,0:T(8,128)S(1)} %get-tuple-element.30.gate_ref, bf16[4,3328,2048]{2,1,0:T(8,128)(2,1)} %experts.1._after.y_hbm, f32[256,2048]{1,0:T(8,128)S(1)} %shard_map.172._after), custom_call_target="tpu_custom_call" | custom-call | flops 12000000000 | bytes 10000000 | tf_op jit(solution)/shard_map/pallas_call | solution.py:264
  259.5 8.6 %shard_map.174 = (f32[128,2048]{1,0:T(8,128)}, f32[128,2048]{1,0:T(8,128)S(1)}) custom-call(s32[4]{0:T(128)S(1)} %get-tuple-element.21.rows_ref, s32[512,8]{1,0:T(8,128)S(1)} %get-tuple-element.28.pos_ref, f32[512,8]{1,0:T(8,128)S(1)} %slice_bitcast_fusion.6.gate_ref, bf16[4,3328,2048]{2,1,0:T(8,128)(2,1)} %experts.1._after.y_hbm, ...), custom_call_target="tpu_custom_call" | custom-call | flops 12000000000 | bytes 10000000 | tf_op jit(solution)/shard_map/pallas_call | solution.py:264
  268.1 7.7 %shard_map.175 = (f32[128,2048]{1,0:T(8,128)S(1)}, f32[128,2048]{1,0:T(8,128)S(1)}) custom-call(s32[4]{0:T(128)S(1)} %get-tuple-element.21.rows_ref, s32[512,8]{1,0:T(8,128)S(1)} %get-tuple-element.28.pos_ref, f32[512,8]{1,0:T(8,128)S(1)} %slice_bitcast_fusion.6.gate_ref, bf16[4,3328,2048]{2,1,0:T(8,128)(2,1)} %experts.1._after.y_hbm, ...), custom_call_target="tpu_custom_call" | custom-call | flops 12000000000 | bytes 10000000 | tf_op jit(solution)/shard_map/pallas_call | solution.py:264
  277.8 34.9 %ffn.3._after.s_ref = f32[512,2048]{1,0:T(8,128)} custom-call(s32[1]{0:T(128)} %bitcast.off_ref, bf16[1024,2048]{1,0:T(8,128)(2,1)} %get-tuple-element.13.x_ref, bf16[2048,4096]{1,0:T(8,128)(2,1)} %wg_ref.5, bf16[2048,4096]{1,0:T(8,128)(2,1)} %wu_ref.5, bf16[4096,2048]{1,0:T(8,128)(2,1)} %wd_ref.5, f32[128,2048]{1,0:T(8,128)} %copy-done.12, ...), custom_call_target="tpu_custom_call" | custom-call | flops 28672000000 | bytes 60000000 | tf_op jit(solution)/shard_map/ffn/pallas_call | solution.py:346
  314.8 7.6 %shard_map.176._after = f32[256,2048]{1,0:T(8,128)S(1)} custom-call(s32[4]{0:T(128)S(1)} %get-tuple-element.21.rows_ref, s32[512,8]{1,0:T(8,128)S(1)} %get-tuple-element.25.pos_ref, f32[512,8]{1,0:T(8,128)S(1)} %get-tuple-element.29.gate_ref, bf16[4,3328,2048]{2,1,0:T(8,128)(2,1)} %experts.1._after.y_hbm, f32[512,2048]{1,0:T(8,128)S(1)} %copy-done.2), custom_call_target="tpu_custom_call" | custom-call | flops 12000000000 | bytes 10000000 | tf_op jit(solution)/shard_map/pallas_call | solution.py:264
  322.8 4.1 collective-permute-start.14
  326.9 7.7 %shard_map.177.m_ref = f32[256,2048]{1,0:T(8,128)S(1)} custom-call(s32[4]{0:T(128)S(1)} %get-tuple-element.21.rows_ref, s32[512,8]{1,0:T(8,128)S(1)} %get-tuple-element.26.pos_ref, f32[512,8]{1,0:T(8,128)S(1)} %slice_bitcast_fusion.2.gate_ref, bf16[4,3328,2048]{2,1,0:T(8,128)(2,1)} %experts.1._after.y_hbm, f32[256,2048]{1,0:T(8,128)S(1)} %shard_map.176._after), custom_call_target="tpu_custom_call" | custom-call | flops 12000000000 | bytes 10000000 | tf_op jit(solution)/shard_map/pallas_call | solution.py:264
  335.9 36.7 %collective-permute-done.16.x_ref = f32[128,2048]{1,0:T(8,128)S(1)} collective-permute-done((f32[128,2048]{1,0:T(8,128)S(1)}, f32[128,2048]{1,0:T(8,128)S(1)}, u32[]{:S(2)}, u32[]{:S(2)}) %collective-permute-start.16) | collective-permute-done | bytes 1048608 | tf_op jit(solution)/shard_map/ppermute | solution.py:379
  373.6 3.5 final.5._after
  379.1 7.6 %shard_map.178._after = f32[256,2048]{1,0:T(8,128)S(1)} custom-call(s32[4]{0:T(128)S(1)} %get-tuple-element.21.rows_ref, s32[512,8]{1,0:T(8,128)S(1)} %copy-done.8, f32[512,8]{1,0:T(8,128)S(1)} %get-tuple-element.29.gate_ref, bf16[4,3328,2048]{2,1,0:T(8,128)(2,1)} %experts.1._after.y_hbm, bf16[128,2048]{1,0:T(8,128)(2,1)S(1)} %copy-done.5), custom_call_target="tpu_custom_call" | custom-call | flops 12000000000 | bytes 10000000 | tf_op jit(solution)/shard_map/pallas_call | solution.py:264
  394.4 7.6 %shard_map.179.m_ref = f32[256,2048]{1,0:T(8,128)S(1)} custom-call(s32[4]{0:T(128)S(1)} %get-tuple-element.21.rows_ref, s32[512,8]{1,0:T(8,128)S(1)} %get-tuple-element.26.pos_ref, f32[512,8]{1,0:T(8,128)S(1)} %slice_bitcast_fusion.2.gate_ref, bf16[4,3328,2048]{2,1,0:T(8,128)(2,1)} %experts.1._after.y_hbm, f32[256,2048]{1,0:T(8,128)S(1)} %shard_map.178._after), custom_call_target="tpu_custom_call" | custom-call | flops 12000000000 | bytes 10000000 | tf_op jit(solution)/shard_map/pallas_call | solution.py:264
  403.4 9.7 %collective-permute-done.20.x_ref = f32[128,2048]{1,0:T(8,128)} collective-permute-done((f32[128,2048]{1,0:T(8,128)}, f32[128,2048]{1,0:T(8,128)}, u32[]{:S(2)}, u32[]{:S(2)}) %collective-permute-start.20) | collective-permute-done | bytes 1048608 | tf_op jit(solution)/shard_map/ppermute | solution.py:379
  418.7 16.4 %collective-permute-done.22.x_ref = f32[128,2048]{1,0:T(8,128)} collective-permute-done((f32[128,2048]{1,0:T(8,128)}, f32[128,2048]{1,0:T(8,128)}, u32[]{:S(2)}, u32[]{:S(2)}) %collective-permute-start.22) | collective-permute-done | bytes 1048608 | tf_op jit(solution)/shard_map/ppermute | solution.py:379
  441.4 10.8 %collective-permute-done.23 = bf16[128,2048]{1,0:T(8,128)(2,1)S(1)} collective-permute-done((bf16[128,2048]{1,0:T(8,128)(2,1)}, bf16[128,2048]{1,0:T(8,128)(2,1)S(1)}, u32[]{:S(2)}, u32[]{:S(2)}) %collective-permute-start.23) | collective-permute-done | bytes 524320 | tf_op jit(solution)/shard_map/ppermute | solution.py:385
  (159 shorter events, 68.6 us)
Async XLA Ops:
  5.4 85.0 %collective-permute-start.8 = (bf16[512,2048]{1,0:T(8,128)(2,1)S(1)}, bf16[512,2048]{1,0:T(8,128)(2,1)}, u32[]{:S(2)}, u32[]{:S(2)}) collective-permute-start(bf16[512,2048]{1,0:T(8,128)(2,1)S(1)} %fusion.11.u0_ref), channel_id=1, source_target_pairs={{0,1},{1,0},{2,3},{3,2},{4,5},{5,4},{6,7},{7,6}} | collective-permute-start | bytes 6291464 | tf_op jit(solution)/shard_map/ppermute | solution.py:382
  6.3 55.3 %collective-permute-start.7 = (bf16[512,2048]{1,0:T(8,128)(2,1)S(1)}, bf16[512,2048]{1,0:T(8,128)(2,1)}, u32[]{:S(2)}, u32[]{:S(2)}) collective-permute-start(bf16[512,2048]{1,0:T(8,128)(2,1)S(1)} %fusion.11.u0_ref), channel_id=1, source_target_pairs={{0,2},{1,3},{2,0},{3,1},{4,6},{5,7},{6,4},{7,5}} | collective-permute-start | bytes 6291464 | tf_op jit(solution)/shard_map/ppermute | solution.py:379
  11.1 53.7 %collective-permute-start.1 = (bf16[256,2048]{1,0:T(8,128)(2,1)}, bf16[256,2048]{1,0:T(8,128)(2,1)}, u32[]{:S(2)}, u32[]{:S(2)}) collective-permute-start(bf16[256,2048]{1,0:T(8,128)(2,1)} %constant_dynamic-slice_fusion), channel_id=1, source_target_pairs={{0,4},{4,0},{1,5},{5,1},{2,6},{6,2},{3,7},{7,3}} | collective-permute-start | bytes 3145736 | tf_op jit(solution)/shard_map/ppermute | solution.py:385
  13.8 46.9 %collective-permute-start.5 = (f32[512,16]{1,0:T(8,128)S(1)}, f32[512,16]{1,0:T(8,128)S(1)}, u32[]{:S(2)}, u32[]{:S(2)}) collective-permute-start(f32[512,16]{1,0:T(8,128)S(1)} %copy.35), channel_id=1, source_target_pairs={{0,2},{1,3},{2,0},{3,1},{4,6},{5,7},{6,4},{7,5}} | collective-permute-start | bytes 98312 | tf_op jit(solution)/shard_map/ppermute | solution.py:379
  52.3 136.3 %collective-permute-start = (bf16[1024,1024]{1,0:T(8,128)(2,1)}, bf16[1024,1024]{1,0:T(8,128)(2,1)}, u32[]{:S(2)}, u32[]{:S(2)}) collective-permute-start(bf16[1024,1024]{1,0:T(8,128)(2,1)} %attn.1._after.ctx_ref), channel_id=1, source_target_pairs={{0,4},{4,0},{1,5},{5,1},{2,6},{6,2},{3,7},{7,3}} | collective-permute-start | bytes 6291464 | tf_op jit(solution)/shard_map/ppermute | solution.py:385
  61.5 2.1 collective-permute-start.6
  61.6 28.9 %collective-permute-start.9 = (bf16[512,2048]{1,0:T(8,128)(2,1)}, bf16[512,2048]{1,0:T(8,128)(2,1)}, u32[]{:S(2)}, u32[]{:S(2)}) collective-permute-start(bf16[512,2048]{1,0:T(8,128)(2,1)} %collective-permute-done.7.u1_ref), channel_id=1, source_target_pairs={{0,1},{1,0},{2,3},{3,2},{4,5},{5,4},{6,7},{7,6}} | collective-permute-start | bytes 6291464 | tf_op jit(solution)/shard_map/ppermute | solution.py:382
  64.9 25.5 %collective-permute-start.3 = (bf16[256,2048]{1,0:T(8,128)(2,1)}, bf16[256,2048]{1,0:T(8,128)(2,1)}, u32[]{:S(2)}, u32[]{:S(2)}) collective-permute-start(bf16[256,2048]{1,0:T(8,128)(2,1)} %collective-permute-done.1.w0_ref), channel_id=1, source_target_pairs={{0,2},{1,3},{2,0},{3,1},{4,6},{5,7},{6,4},{7,5}} | collective-permute-start | bytes 3145736 | tf_op jit(solution)/shard_map/ppermute | solution.py:379
  72.2 116.3 %collective-permute-start.2 = (bf16[256,2048]{1,0:T(8,128)(2,1)}, bf16[256,2048]{1,0:T(8,128)(2,1)}, u32[]{:S(2)}, u32[]{:S(2)}) collective-permute-start(bf16[256,2048]{1,0:T(8,128)(2,1)} %collective-permute-done.1.w0_ref), channel_id=1, source_target_pairs={{0,1},{1,0},{2,3},{3,2},{4,5},{5,4},{6,7},{7,6}} | collective-permute-start | bytes 3145736 | tf_op jit(solution)/shard_map/ppermute | solution.py:382
  90.4 98.2 %collective-permute-start.4 = (bf16[256,2048]{1,0:T(8,128)(2,1)}, bf16[256,2048]{1,0:T(8,128)(2,1)}, u32[]{:S(2)}, u32[]{:S(2)}) collective-permute-start(bf16[256,2048]{1,0:T(8,128)(2,1)} %collective-permute-done.3.w2_ref), channel_id=1, source_target_pairs={{0,1},{1,0},{2,3},{3,2},{4,5},{5,4},{6,7},{7,6}} | collective-permute-start | bytes 3145736 | tf_op jit(solution)/shard_map/ppermute | solution.py:382
  249.0 10.5 %collective-permute-start.10 = (f32[256,2048]{1,0:T(8,128)S(1)}, f32[256,2048]{1,0:T(8,128)S(1)}, u32[]{:S(2)}, u32[]{:S(2)}) collective-permute-start(f32[256,2048]{1,0:T(8,128)S(1)} %shard_map.172._after), channel_id=1, source_target_pairs={{0,1},{1,0},{2,3},{3,2},{4,5},{5,4},{6,7},{7,6}} | collective-permute-start | bytes 6291464 | tf_op jit(solution)/shard_map/ppermute | solution.py:382
  256.8 11.3 %collective-permute-start.11 = (f32[256,2048]{1,0:T(8,128)S(1)}, f32[256,2048]{1,0:T(8,128)S(1)}, u32[]{:S(2)}, u32[]{:S(2)}) collective-permute-start(f32[256,2048]{1,0:T(8,128)S(1)} %shard_map.173._after), channel_id=1, source_target_pairs={{0,1},{1,0},{2,3},{3,2},{4,5},{5,4},{6,7},{7,6}} | collective-permute-start | bytes 6291464 | tf_op jit(solution)/shard_map/ppermute | solution.py:382
  257.4 78.5 %collective-permute-start.12 = (f32[256,2048]{1,0:T(8,128)S(1)}, f32[256,2048]{1,0:T(8,128)}, u32[]{:S(2)}, u32[]{:S(2)}) collective-permute-start(f32[256,2048]{1,0:T(8,128)S(1)} %copy-done.10), channel_id=1, source_target_pairs={{0,4},{4,0},{1,5},{5,1},{2,6},{6,2},{3,7},{7,3}} | collective-permute-start | bytes 6291464 | tf_op jit(solution)/shard_map/ppermute | solution.py:385
  322.5 51.1 %collective-permute-start.13 = (f32[256,2048]{1,0:T(8,128)S(1)}, f32[256,2048]{1,0:T(8,128)}, u32[]{:S(2)}, u32[]{:S(2)}) collective-permute-start(f32[256,2048]{1,0:T(8,128)S(1)} %shard_map.176._after), channel_id=1, source_target_pairs={{0,1},{1,0},{2,3},{3,2},{4,5},{5,4},{6,7},{7,6}} | collective-permute-start | bytes 6291464 | tf_op jit(solution)/shard_map/ppermute | solution.py:382
  322.7 70.8 %collective-permute-start.18 = (f32[256,2048]{1,0:T(8,128)}, f32[256,2048]{1,0:T(8,128)}, u32[]{:S(2)}, u32[]{:S(2)}) collective-permute-start(f32[256,2048]{1,0:T(8,128)} %get-tuple-element.19), channel_id=1, source_target_pairs={{0,4},{4,0},{1,5},{5,1},{2,6},{6,2},{3,7},{7,3}} | collective-permute-start | bytes 6291464 | tf_op jit(solution)/shard_map/ppermute | solution.py:385
  322.8 66.0 %collective-permute-start.14 = (f32[128,2048]{1,0:T(8,128)}, f32[128,2048]{1,0:T(8,128)}, u32[]{:S(2)}, u32[]{:S(2)}) collective-permute-start(f32[128,2048]{1,0:T(8,128)} %get-tuple-element.16._after), channel_id=1, source_target_pairs={{0,2},{1,3},{2,0},{3,1},{4,6},{5,7},{6,4},{7,5}} | collective-permute-start | bytes 3145736 | tf_op jit(solution)/shard_map/ppermute | solution.py:379
  326.9 45.7 %collective-permute-start.16 = (f32[128,2048]{1,0:T(8,128)S(1)}, f32[128,2048]{1,0:T(8,128)S(1)}, u32[]{:S(2)}, u32[]{:S(2)}) collective-permute-start(f32[128,2048]{1,0:T(8,128)S(1)} %copy-done.14), channel_id=1, source_target_pairs={{0,2},{1,3},{2,0},{3,1},{4,6},{5,7},{6,4},{7,5}} | collective-permute-start | bytes 3145736 | tf_op jit(solution)/shard_map/ppermute | solution.py:379
  386.7 26.4 %collective-permute-start.19 = (f32[256,2048]{1,0:T(8,128)S(1)}, f32[256,2048]{1,0:T(8,128)}, u32[]{:S(2)}, u32[]{:S(2)}) collective-permute-start(f32[256,2048]{1,0:T(8,128)S(1)} %shard_map.178._after), channel_id=1, source_target_pairs={{0,1},{1,0},{2,3},{3,2},{4,5},{5,4},{6,7},{7,6}} | collective-permute-start | bytes 6291464 | tf_op jit(solution)/shard_map/ppermute | solution.py:382
  386.8 26.4 %collective-permute-start.20 = (f32[128,2048]{1,0:T(8,128)}, f32[128,2048]{1,0:T(8,128)}, u32[]{:S(2)}, u32[]{:S(2)}) collective-permute-start(f32[128,2048]{1,0:T(8,128)} %copy-done.12), channel_id=1, source_target_pairs={{0,2},{1,3},{2,0},{3,1},{4,6},{5,7},{6,4},{7,5}} | collective-permute-start | bytes 3145736 | tf_op jit(solution)/shard_map/ppermute | solution.py:379
  388.5 46.6 %collective-permute-start.22 = (f32[128,2048]{1,0:T(8,128)}, f32[128,2048]{1,0:T(8,128)}, u32[]{:S(2)}, u32[]{:S(2)}) collective-permute-start(f32[128,2048]{1,0:T(8,128)} %copy-done.11), channel_id=1, source_target_pairs={{0,2},{1,3},{2,0},{3,1},{4,6},{5,7},{6,4},{7,5}} | collective-permute-start | bytes 3145736 | tf_op jit(solution)/shard_map/ppermute | solution.py:379
  388.8 50.7 %collective-permute-start.17 = (bf16[128,2048]{1,0:T(8,128)(2,1)S(1)}, bf16[128,2048]{1,0:T(8,128)(2,1)}, u32[]{:S(2)}, u32[]{:S(2)}) collective-permute-start(bf16[128,2048]{1,0:T(8,128)(2,1)S(1)} %copy-done.6), channel_id=1, source_target_pairs={{0,4},{4,0},{1,5},{5,1},{2,6},{6,2},{3,7},{7,3}} | collective-permute-start | bytes 1572872 | tf_op jit(solution)/shard_map/ppermute | solution.py:385
  393.5 24.3 %collective-permute-start.15 = (bf16[128,2048]{1,0:T(8,128)(2,1)}, bf16[128,2048]{1,0:T(8,128)(2,1)}, u32[]{:S(2)}, u32[]{:S(2)}) collective-permute-start(bf16[128,2048]{1,0:T(8,128)(2,1)} %final.4), channel_id=1, source_target_pairs={{0,4},{4,0},{1,5},{5,1},{2,6},{6,2},{3,7},{7,3}} | collective-permute-start | bytes 1572872 | tf_op jit(solution)/shard_map/ppermute | solution.py:385
  416.7 23.8 %collective-permute-start.21 = (bf16[128,2048]{1,0:T(8,128)(2,1)}, bf16[128,2048]{1,0:T(8,128)(2,1)S(1)}, u32[]{:S(2)}, u32[]{:S(2)}) collective-permute-start(bf16[128,2048]{1,0:T(8,128)(2,1)} %final.6), channel_id=1, source_target_pairs={{0,4},{4,0},{1,5},{5,1},{2,6},{6,2},{3,7},{7,3}} | collective-permute-start | bytes 1572872 | tf_op jit(solution)/shard_map/ppermute | solution.py:385
  438.6 13.7 %collective-permute-start.23 = (bf16[128,2048]{1,0:T(8,128)(2,1)}, bf16[128,2048]{1,0:T(8,128)(2,1)S(1)}, u32[]{:S(2)}, u32[]{:S(2)}) collective-permute-start(bf16[128,2048]{1,0:T(8,128)(2,1)} %final.7), channel_id=1, source_target_pairs={{0,4},{4,0},{1,5},{5,1},{2,6},{6,2},{3,7},{7,3}} | collective-permute-start | bytes 1572872 | tf_op jit(solution)/shard_map/ppermute | solution.py:385
  (34 other events, 603.0 us)

commit v5 on v4

--- a/solution.py
+++ b/solution.py
@@ -16,7 +16,7 @@
 OUT = 96
 CHUNKS = 4
 CT = 256
-VMEM_BIG = 60 * 1024 * 1024
+VMEM_BIG = 67_000_000
 
 
 def inv_rms_of(x_f32):
@@ -79,6 +79,7 @@
         in_specs=[col, col, col, tab, tab], out_specs=col,
         out_shape=jax.ShapeDtypeStruct((seq, width), BF16),
         scratch_shapes=[pltpu.VMEM((seq, pair * head_dim), BF16)] + [pltpu.VMEM((256, seq), F32), pltpu.VMEM((256, seq), BF16)] * pair,
+        compiler_params=pltpu.CompilerParams(vmem_limit_bytes=VMEM_BIG),
         cost_estimate=pl.CostEstimate(flops=width * seq * seq * 4, bytes_accessed=12 * seq * width, transcendentals=0),
         name="attn",
     )(q, k, v, cos_t, sin_t)
@@ -174,9 +175,14 @@
     )(n, loc, dst, rank_t, *u_four, wg, wu, wd, after)
 
 
-def combine_kernel(src, has_init, rows_ref, pos_ref, gate_ref, y_hbm, _after, *rest):
+def combine_kernel(src, has_init, n_adds, rows_ref, pos_ref, gate_ref, y_hbm, _after, *rest):
     init_ref = rest[0] if has_init else None
-    *o_refs, y_a, y_b, g_a, g_b, sems = rest[1:] if has_init else rest
+    adds, rest = rest[has_init:has_init + n_adds], rest[has_init + n_adds:]
+    if n_adds:
+        out_ref, y_a, y_b, g_a, g_b, sems, acc = rest
+        o_refs = [acc]
+    else:
+        *o_refs, y_a, y_b, g_a, g_b, sems = rest
     half, top_k = pos_ref.shape
     rc, d = o_refs[0].shape
     n_rows = rows_ref[src]
@@ -248,8 +254,12 @@
 
     lax.fori_loop(0, lax.shift_right_logical(n_tiles + 1, 1), body, 0)
 
-
-def run_combine(src, rows, pos, gates, y_all, after, init=None, n_out=1, part=(0, 1)):
+    if n_adds:
+        ffn_own, ffn_got, core_got, x_got = adds
+        out_ref[...] = ((ffn_own[...] + ffn_got[...]) + ((acc[...] + core_got[...]) + x_got[...])).astype(BF16)
+
+
+def run_combine(src, rows, pos, gates, y_all, after, init=None, n_out=1, part=(0, 1), adds=()):
     d = y_all.shape[2]
     half, top_k = pos.shape[1] // part[1], pos.shape[2]
     small = pl.BlockSpec((half, top_k), lambda i, r: (part[0], 0))
@@ -257,16 +267,18 @@
     extra = [] if init is None else [init]
     grid_spec = pltpu.PrefetchScalarGridSpec(
         num_scalar_prefetch=1, grid=(1,),
-        in_specs=[small, small, anywhere, anywhere] + [pl.BlockSpec((half, d), lambda i, r: (0, 0)) for _ in extra],
+        in_specs=[small, small, anywhere, anywhere] + [pl.BlockSpec((half, d), lambda i, r: (0, 0)) for _ in extra]
+        + [pl.BlockSpec((half, d), lambda i, r, b=b: (b, 0)) for _, b in adds],
         out_specs=[pl.BlockSpec((half // n_out, d), lambda i, r: (0, 0))] * n_out,
-        scratch_shapes=[pltpu.VMEM((CT, d), BF16)] * 2 + [pltpu.VMEM((half, 3 * CT), BF16)] * 2 + [pltpu.SemaphoreType.DMA((2,))],
+        scratch_shapes=[pltpu.VMEM((CT, d), BF16)] * 2 + [pltpu.VMEM((half, 3 * CT), BF16)] * 2 + [pltpu.SemaphoreType.DMA((2,))]
+        + ([pltpu.VMEM((half, d), F32)] if adds else []),
     )
     return pl.pallas_call(
-        functools.partial(combine_kernel, src, init is not None), grid_spec=grid_spec,
-        out_shape=[jax.ShapeDtypeStruct((half // n_out, d), F32)] * n_out,
-        compiler_params=pltpu.CompilerParams(vmem_limit_bytes=40 * 1024 * 1024),
+        functools.partial(combine_kernel, src, int(init is not None), len(adds)), grid_spec=grid_spec,
+        out_shape=[jax.ShapeDtypeStruct((half // n_out, d), BF16 if adds else F32)] * n_out,
+        compiler_params=pltpu.CompilerParams(vmem_limit_bytes=VMEM_BIG),
         cost_estimate=pl.CostEstimate(flops=12_000_000_000, bytes_accessed=10_000_000, transcendentals=0),
-    )(rows, pos[src], gates[src], y_all, after, *extra)
+    )(rows, pos[src], gates[src], y_all, after, *extra, *[v for v, _ in adds])
 
 
 def out_kernel(q_ref, x_ref, gain_ref, ctx_ref, peer_ref, wo_ref, w0_ref, w1_ref, w2_ref, w3_ref, _after, a_ref, n_ref):
@@ -352,19 +364,31 @@
     )(which.reshape(1), f_norm, wg, wu, wd, after, *[v for v, _ in adds])
 
 
-def final_kernel(s_ref, g_ref, m_ref, c_ref, x_ref, o_ref):
-    o_ref[...] = ((s_ref[...] + g_ref[...]) + ((m_ref[...] + c_ref[...]) + x_ref[...])).astype(BF16)
-
-
-def run_final(arrays):
-    rows, d = arrays[-1][0].shape
-    in_specs = [pl.BlockSpec((rows, d), lambda i, b=b: (b, 0)) for _, b in arrays]
+def place_kernel(n, _dest, *refs):
+    i = pl.program_id(0)
+    for k in range(n):
+        @pl.when(i == k)
+        def _():
+            refs[-1][...] = refs[k][...]
+
+
+def run_place(dest, pieces, seq, buf=None):
+    rows, d = pieces[0].shape
+    n = len(pieces)
+    extra = [] if buf is None else [buf]
+    grid_spec = pltpu.PrefetchScalarGridSpec(
+        num_scalar_prefetch=1, grid=(n,),
+        in_specs=[pl.BlockSpec((rows, d), lambda i, t: (0, 0), pipeline_mode=pl.Buffered(1))] * n + [pl.BlockSpec(memory_space=pl.ANY) for _ in extra],
+        out_specs=pl.BlockSpec((rows, d), lambda i, t: (t[i], 0)),
+    )
     return pl.pallas_call(
-        final_kernel, grid=(1,), in_specs=in_specs, out_specs=pl.BlockSpec((rows, d), lambda i: (0, 0)),
-        out_shape=jax.ShapeDtypeStruct((rows, d), BF16),
-        cost_estimate=pl.CostEstimate(flops=5 * rows * d, bytes_accessed=22 * rows * d, transcendentals=0),
-        name="final",
-    )(*[v for v, _ in arrays])
+        functools.partial(place_kernel, n), grid_spec=grid_spec,
+        out_shape=jax.ShapeDtypeStruct((seq, d), BF16),
+        input_output_aliases={n + 1: 0} if extra else {},
+        compiler_params=pltpu.CompilerParams(vmem_limit_bytes=VMEM_BIG),
+        cost_estimate=pl.CostEstimate(flops=n * rows * d, bytes_accessed=4 * n * rows * d, transcendentals=0),
+        name="place",
+    )(dest, *pieces, *extra)
 
 
 def solution(mesh):
@@ -473,22 +497,22 @@
                 m_x.append(over_x(m1[k]))
 
         s_own, = run_ffn(my_tp, half, f_norm, w_gate, w_up, w_down, tie, adds=((after, None),))
-        own, peer = [], []
+        own, peer, got2 = [], [], []
         tie = s_own
         per = CHUNKS // 2
         for p in range(2):
-            m2, = run_combine(2, rows, pos, gates_all, y_all, tie, part=(p, 2))
-            got2 = over_core(m2)
-            m0, = run_combine(0, rows, pos, gates_all, y_all, m2, part=(p, 2))
-            tie = m0
-            for k in range(per):
-                c = p * per + k
-                o_c = run_final(((s_own, c), (f_got[p], k), (m0, k), (got2, k), (m_x[c], 0)))
-                tie = o_c
-                own.append(o_c)
-                peer.append(over_tp(o_c))
-        first = my_tp == 0
-        out = jnp.concatenate([jnp.where(first, a, b) for a, b in zip(own, peer)] + [jnp.where(first, b, a) for a, b in zip(own, peer)], axis=0)
+            tie, = run_combine(2, rows, pos, gates_all, y_all, tie, part=(p, 2))
+            got2.append(over_core(tie))
+        for c in range(CHUNKS):
+            p, k = c // per, c % per
+            tie, = run_combine(0, rows, pos, gates_all, y_all, tie, part=(c, CHUNKS),
+                               adds=((s_own, c), (f_got[p], k), (got2[p], k), (m_x[c], 0)))
+            own.append(tie)
+            peer.append(over_tp(tie))
+        mine, other = my_tp * CHUNKS, (1 - my_tp) * CHUNKS
+        dest = jnp.stack([mine + c for c in range(CHUNKS)] + [other + c for c in range(CHUNKS)]).astype(jnp.int32)
+        out = run_place(dest[:-1], own + peer[:-1], seq)
+        out = run_place(dest[-1:], peer[-1:], seq, out)
         return out.reshape(1, seq, d)
 
     return jax.shard_map(layer, mesh=mesh, in_specs=in_specs, out_specs=tok_spec, check_vma=False)

time: 466 us -> 464 us (level)
  Pallas kernels: 276 us -> 308 us
  waiting for transfers between devices: 100 us -> 77.1 us
  other arithmetic: 20.4 us -> 10.7 us
  local copies, waits for them, and re-layouts: 18.5 us -> 13.5 us
    pallas_call x12, Pallas kernels: 76.3 us -> 108 us  [the longest x10 99.9 us: run_combine(): pl.pallas_call(functools.partial(combine_kernel, src, int(init is not Non...]
    ppermute x7, waiting for transfers between devices: 88.3 us -> 70.8 us  [over_x(): return lax.ppermute(v, 'ep', [(i, i ^ 2) for i in range(4)])]
    unnamed x68 -> x20, local copies, waits for them, and re-layouts: 11.4 us -> 0.04 us
    unnamed x7 -> x0, other arithmetic: 9.58 us -> none
  transfers between devices with their start and end apart: 24 -> 24, of which waited for: 7 -> 6; matrix products, arithmetic and copies ran while one was open for 8% -> 9% of each run, Pallas kernels for 47% -> 54%
where the time goes in v5:
time: 464 us; the launch traced here: 457 us
  Pallas kernels  308 us (66%)
  waiting for transfers between devices  77.1 us (17%)
  matrix products  24.9 us (5%)
  starting transfers between devices  22.6 us (5%)
  local copies, waits for them, and re-layouts  13.5 us (3%)
  other arithmetic  10.7 us (2%)
    pallas_call x10, Pallas kernels, run_combine(): pl.pallas_call(functools.partial(combine_kernel, src, int(init is not Non...  99.9 us
    pallas_call x1, Pallas kernels, run_experts(): pl.pallas_call(expert_kernel, grid_spec=grid_spec, out_shape=jax.ShapeDty...  98.2 us
    ppermute x7, waiting for transfers between devices, over_x(): return lax.ppermute(v, 'ep', [(i, i ^ 2) for i in range(4)])  70.8 us
    pallas_call x2, Pallas kernels, run_ffn(): pl.pallas_call(functools.partial(ffn_kernel, n_up, len(adds)), grid_spec=...  69.5 us
    pallas_call x1, Pallas kernels, run_out(): pl.pallas_call(out_kernel, grid_spec=grid_spec, out_shape=[jax.ShapeDtype...  16.6 us
    pallas_call x1, Pallas kernels, attention(): pl.pallas_call(attn_kernel, grid=(steps,), in_specs=[col, col, col, tab,...  15.6 us
    ppermute x7, starting transfers between devices, over_x(): return lax.ppermute(v, 'ep', [(i, i ^ 2) for i in range(4)])  13.3 us
    dot_general x1, matrix products, layer(): k = jnp.dot(x_norm, w_key.reshape(d, width), preferred_element_type=F32)  10.1 us
  transfers between devices with their start and end apart: 24, of which 6 were waited for; matrix products, arithmetic and copies ran while one was open for 9% of the time, Pallas kernels for 54%

profile of v5, /device:TPU:0, one launch (start us, length us, event | category | flops | bytes accessed | tf_op | source)
XLA Modules:
  0.0 457.4 jit_solution(6062703227971317825)
XLA Ops:
  17.9 10.1 %fusion.4.k_ref = f32[1024,1024]{1,0:T(8,128)} fusion(bf16[256,8,8,128]{3,2,1,0:T(8,128)(2,1)} %bitcast.72, bf16[1,1024,2048]{2,1,0:T(8,128)(2,1)} %param.19, f32[2048]{0:T(1024)S(1)} %convert_element_type.61, f32[1024]{0:T(1024)S(1)} %add_rsqrt_fusion), kind=kOutput, calls=%fused_computation.6 | convolution fusion | flops 4303355904 | bytes 12595200 | tf_op jit(solution)/shard_map/dot_general | solution.py:471
  28.0 6.4 %fusion.7.q_ref = f32[1024,1024]{1,0:T(8,128)} fusion(bf16[256,8,8,128]{3,2,1,0:T(8,128)(2,1)S(1)} %bitcast.73, bf16[1,1024,2048]{2,1,0:T(8,128)(2,1)S(1)} %copy-done, f32[2048]{0:T(1024)S(1)} %convert_element_type.61, f32[1024]{0:T(1024)S(1)} %add_rsqrt_fusion), kind=kOutput, calls=%fused_computation.9 | convolution fusion | flops 4303355904 | bytes 12595200 | tf_op jit(solution)/shard_map/dot_general | solution.py:470
  34.3 5.8 %fusion.12.v_ref = bf16[1024,1024]{1,0:T(8,128)(2,1)} fusion(bf16[256,8,8,128]{3,2,1,0:T(8,128)(2,1)S(1)} %bitcast.74, bf16[1,1024,2048]{2,1,0:T(8,128)(2,1)S(1)} %copy-done, f32[2048]{0:T(1024)S(1)} %convert_element_type.61, f32[1024]{0:T(1024)S(1)} %add_rsqrt_fusion), kind=kOutput, calls=%fused_computation.15 | convolution fusion | flops 4304404480 | bytes 10498048 | tf_op jit(solution)/shard_map/dot_general | solution.py:472
  40.2 15.6 %attn.1._after.ctx_ref = bf16[1024,1024]{1,0:T(8,128)(2,1)} custom-call(f32[1024,1024]{1,0:T(8,128)} %fusion.7.q_ref, f32[1024,1024]{1,0:T(8,128)} %fusion.4.k_ref, bf16[1024,1024]{1,0:T(8,128)(2,1)} %fusion.12.v_ref, f32[1024,128]{1,0:T(8,128)} %constant.67.clone.cos_ref, f32[1024,128]{1,0:T(8,128)} %constant.68.clone.sin_ref), custom_call_target="tpu_custom_call" | custom-call | flops 4294967296 | bytes 12582912 | tf_op jit(solution)/shard_map/attn/pallas_call | solution.py:77
  55.8 5.7 %collective-permute-done = f32[512,16]{1,0:T(8,128)} collective-permute-done((f32[512,16]{1,0:T(8,128)}, f32[512,16]{1,0:T(8,128)}, u32[]{:S(2)}, u32[]{:S(2)}) %collective-permute-start) | collective-permute-done | bytes 32800 | tf_op jit(solution)/shard_map/ppermute | solution.py:403
  74.1 19.5 %collective-permute-done.8.w2_ref = bf16[256,2048]{1,0:T(8,128)(2,1)} collective-permute-done((bf16[256,2048]{1,0:T(8,128)(2,1)}, bf16[256,2048]{1,0:T(8,128)(2,1)}, u32[]{:S(2)}, u32[]{:S(2)}) %collective-permute-start.8) | collective-permute-done | bytes 1048608 | tf_op jit(solution)/shard_map/ppermute | solution.py:403
  93.7 98.2 %experts.1._after.y_hbm = bf16[4,3328,2048]{2,1,0:T(8,128)(2,1)} custom-call(s32[4,16]{1,0:T(4,128)} %copy-done.3, s32[4,16]{1,0:T(4,128)} %select_reduce_fusion.3.loc_ref, s32[4,16]{1,0:T(4,128)} %copy-done.7, s32[4,16,1,512]{3,2,1,0:T(1,128)} %broadcast_in_dim.106.rank_ref, bf16[512,2048]{1,0:T(8,128)(2,1)} %fusion.11.u0_ref, ...), custom_call_target="tpu_custom_call" | custom-call | flops 89999998976 | bytes 241326592 | tf_op jit(solution)/shard_map/experts/pallas_call | solution.py:169
  191.9 16.6 %out_proj.1 = (bf16[1024,2048]{1,0:T(8,128)(2,1)}, bf16[1024,2048]{1,0:T(8,128)(2,1)}) custom-call(s32[4]{0:T(128)} %iota_xor_fusion.q_ref, bf16[1024,2048]{1,0:T(8,128)(2,1)} %bitcast.69, bf16[1,2048]{1,0:T(2,128)(2,1)} %reshape.178.gain_ref, bf16[1024,1024]{1,0:T(8,128)(2,1)} %attn.1._after.ctx_ref, bf16[1024,1024]{1,0:T(8,128)(2,1)} %collective-permute-done.5.peer_ref, ...), custom_call_target="tpu_custom_call" | custom-call | flops 10000000000 | bytes 24000000 | tf_op jit(solution)/shard_map/out_proj/pallas_call | solution.py:310
  208.5 34.5 %ffn.2 = (f32[256,2048]{1,0:T(8,128)}, f32[256,2048]{1,0:T(8,128)}) custom-call(s32[1]{0:T(128)} %bitcast.20.off_ref, bf16[1024,2048]{1,0:T(8,128)(2,1)} %get-tuple-element.13.x_ref, bf16[2048,4096]{1,0:T(8,128)(2,1)} %wg_ref.5, bf16[2048,4096]{1,0:T(8,128)(2,1)} %wu_ref.5, bf16[4096,2048]{1,0:T(8,128)(2,1)} %wd_ref.5, ...), custom_call_target="tpu_custom_call" | custom-call | flops 28672000000 | bytes 60000000 | tf_op jit(solution)/shard_map/ffn/pallas_call | solution.py:358
  243.1 9.9 %shard_map.172._after = f32[256,2048]{1,0:T(8,128)} custom-call(s32[4]{0:T(128)} %get-tuple-element.21.rows_ref, s32[512,8]{1,0:T(8,128)} %get-tuple-element.25.pos_ref, f32[512,8]{1,0:T(8,128)} %get-tuple-element.29.gate_ref, bf16[4,3328,2048]{2,1,0:T(8,128)(2,1)} %experts.1._after.y_hbm, f32[256,2048]{1,0:T(8,128)} %get-tuple-element.15._after), custom_call_target="tpu_custom_call" | custom-call | flops 12000000000 | bytes 10000000 | tf_op jit(solution)/shard_map/pallas_call | solution.py:276
  253.1 9.9 %shard_map.173._after = f32[256,2048]{1,0:T(8,128)} custom-call(s32[4]{0:T(128)} %get-tuple-element.21.rows_ref, s32[512,8]{1,0:T(8,128)} %get-tuple-element.25.pos_ref, f32[512,8]{1,0:T(8,128)} %get-tuple-element.29.gate_ref, bf16[4,3328,2048]{2,1,0:T(8,128)(2,1)} %experts.1._after.y_hbm, f32[256,2048]{1,0:T(8,128)} %shard_map.172._after), custom_call_target="tpu_custom_call" | custom-call | flops 12000000000 | bytes 10000000 | tf_op jit(solution)/shard_map/pallas_call | solution.py:276
  267.4 10.8 %shard_map.174 = (f32[128,2048]{1,0:T(8,128)}, f32[128,2048]{1,0:T(8,128)}) custom-call(s32[4]{0:T(128)} %get-tuple-element.21.rows_ref, s32[512,8]{1,0:T(8,128)} %get-tuple-element.26.pos_ref, f32[512,8]{1,0:T(8,128)} %slice_bitcast_fusion.2.gate_ref, bf16[4,3328,2048]{2,1,0:T(8,128)(2,1)} %experts.1._after.y_hbm, f32[256,2048]{1,0:T(8,128)} %shard_map.173._after, ...), custom_call_target="tpu_custom_call" | custom-call | flops 12000000000 | bytes 10000000 | tf_op jit(solution)/shard_map/pallas_call | solution.py:276
  278.2 10.7 %shard_map.175 = (f32[128,2048]{1,0:T(8,128)}, f32[128,2048]{1,0:T(8,128)}) custom-call(s32[4]{0:T(128)} %get-tuple-element.21.rows_ref, s32[512,8]{1,0:T(8,128)} %get-tuple-element.26.pos_ref, f32[512,8]{1,0:T(8,128)} %slice_bitcast_fusion.2.gate_ref, bf16[4,3328,2048]{2,1,0:T(8,128)(2,1)} %experts.1._after.y_hbm, f32[128,2048]{1,0:T(8,128)} %get-tuple-element.16._after, ...), custom_call_target="tpu_custom_call" | custom-call | flops 12000000000 | bytes 10000000 | tf_op jit(solution)/shard_map/pallas_call | solution.py:276
  288.9 34.9 %ffn.3._after.rest_0_ = f32[512,2048]{1,0:T(8,128)} custom-call(s32[1]{0:T(128)} %bitcast.14.off_ref, bf16[1024,2048]{1,0:T(8,128)(2,1)} %get-tuple-element.13.x_ref, bf16[2048,4096]{1,0:T(8,128)(2,1)} %wg_ref.5, bf16[2048,4096]{1,0:T(8,128)(2,1)} %wu_ref.5, bf16[4096,2048]{1,0:T(8,128)(2,1)} %wd_ref.5, f32[128,2048]{1,0:T(8,128)} %get-tuple-element.17._after, ...), custom_call_target="tpu_custom_call" | custom-call | flops 28672000000 | bytes 60000000 | tf_op jit(solution)/shard_map/ffn/pallas_call | solution.py:358
  323.8 9.9 %shard_map.176._after = f32[256,2048]{1,0:T(8,128)} custom-call(s32[4]{0:T(128)} %get-tuple-element.21.rows_ref, s32[512,8]{1,0:T(8,128)} %get-tuple-element.27.pos_ref, f32[512,8]{1,0:T(8,128)} %get-tuple-element.30.gate_ref, bf16[4,3328,2048]{2,1,0:T(8,128)(2,1)} %experts.1._after.y_hbm, f32[512,2048]{1,0:T(8,128)} %ffn.3._after.rest_0_), custom_call_target="tpu_custom_call" | custom-call | flops 12000000000 | bytes 10000000 | tf_op jit(solution)/shard_map/pallas_call | solution.py:276
  335.6 4.1 collective-permute-start.14
  339.8 10.0 %shard_map.177._after = f32[256,2048]{1,0:T(8,128)} custom-call(s32[4]{0:T(128)} %get-tuple-element.21.rows_ref, s32[512,8]{1,0:T(8,128)} %get-tuple-element.27.pos_ref, f32[512,8]{1,0:T(8,128)} %get-tuple-element.30.gate_ref, bf16[4,3328,2048]{2,1,0:T(8,128)(2,1)} %experts.1._after.y_hbm, f32[256,2048]{1,0:T(8,128)} %shard_map.176._after), custom_call_target="tpu_custom_call" | custom-call | flops 12000000000 | bytes 10000000 | tf_op jit(solution)/shard_map/pallas_call | solution.py:276
  351.8 12.3 %collective-permute-done.14.rest_3_ = f32[128,2048]{1,0:T(8,128)} collective-permute-done((f32[128,2048]{1,0:T(8,128)}, f32[128,2048]{1,0:T(8,128)}, u32[]{:S(2)}, u32[]{:S(2)}) %collective-permute-start.14) | collective-permute-done | bytes 1048608 | tf_op jit(solution)/shard_map/ppermute | solution.py:403
  366.1 9.7 %shard_map.178._after.refs_0_ = bf16[128,2048]{1,0:T(8,128)(2,1)} custom-call(s32[4]{0:T(128)} %get-tuple-element.21.rows_ref, s32[512,8]{1,0:T(8,128)} %get-tuple-element.28.pos_ref, f32[512,8]{1,0:T(8,128)} %slice_bitcast_fusion.6.gate_ref, bf16[4,3328,2048]{2,1,0:T(8,128)(2,1)} %experts.1._after.y_hbm, f32[256,2048]{1,0:T(8,128)} %shard_map.177._after, ...), custom_call_target="tpu_custom_call" | custom-call | flops 12000000000 | bytes 10000000 | tf_op jit(solution)/shard_map/pallas_call | solution.py:276
  375.8 33.2 %collective-permute-done.15.rest_3_ = f32[128,2048]{1,0:T(8,128)} collective-permute-done((f32[128,2048]{1,0:T(8,128)}, f32[128,2048]{1,0:T(8,128)}, u32[]{:S(2)}, u32[]{:S(2)}) %collective-permute-start.15) | collective-permute-done | bytes 1048608 | tf_op jit(solution)/shard_map/ppermute | solution.py:403
  409.6 9.6 %shard_map.179._after.refs_1_ = bf16[128,2048]{1,0:T(8,128)(2,1)} custom-call(s32[4]{0:T(128)} %get-tuple-element.21.rows_ref, s32[512,8]{1,0:T(8,128)} %get-tuple-element.28.pos_ref, f32[512,8]{1,0:T(8,128)} %slice_bitcast_fusion.6.gate_ref, bf16[4,3328,2048]{2,1,0:T(8,128)(2,1)} %experts.1._after.y_hbm, bf16[128,2048]{1,0:T(8,128)(2,1)} %shard_map.178._after.refs_0_, ...), custom_call_target="tpu_custom_call" | custom-call | flops 12000000000 | bytes 10000000 | tf_op jit(solution)/shard_map/pallas_call | solution.py:276
  420.7 9.7 %shard_map.180._after.refs_2_ = bf16[128,2048]{1,0:T(8,128)(2,1)} custom-call(s32[4]{0:T(128)} %get-tuple-element.21.rows_ref, s32[512,8]{1,0:T(8,128)} %get-tuple-element.28.pos_ref, f32[512,8]{1,0:T(8,128)} %slice_bitcast_fusion.6.gate_ref, bf16[4,3328,2048]{2,1,0:T(8,128)(2,1)} %experts.1._after.y_hbm, bf16[128,2048]{1,0:T(8,128)(2,1)} %shard_map.179._after.refs_1_, ...), custom_call_target="tpu_custom_call" | custom-call | flops 12000000000 | bytes 10000000 | tf_op jit(solution)/shard_map/pallas_call | solution.py:276
  431.0 9.7 %shard_map.181.refs_3_ = bf16[128,2048]{1,0:T(8,128)(2,1)} custom-call(s32[4]{0:T(128)} %get-tuple-element.21.rows_ref, s32[512,8]{1,0:T(8,128)} %get-tuple-element.28.pos_ref, f32[512,8]{1,0:T(8,128)} %slice_bitcast_fusion.6.gate_ref, bf16[4,3328,2048]{2,1,0:T(8,128)(2,1)} %experts.1._after.y_hbm, bf16[128,2048]{1,0:T(8,128)(2,1)} %shard_map.180._after.refs_2_, ...), custom_call_target="tpu_custom_call" | custom-call | flops 12000000000 | bytes 10000000 | tf_op jit(solution)/shard_map/pallas_call | solution.py:276
  445.7 6.1 %place.2.refs_1_ = bf16[1024,2048]{1,0:T(8,128)(2,1)} custom-call(s32[7]{0:T(128)} %stack.47._dest, bf16[128,2048]{1,0:T(8,128)(2,1)} %shard_map.178._after.refs_0_, bf16[128,2048]{1,0:T(8,128)(2,1)} %shard_map.179._after.refs_1_, bf16[128,2048]{1,0:T(8,128)(2,1)} %shard_map.180._after.refs_2_, bf16[128,2048]{1,0:T(8,128)(2,1)} %shard_map.181.refs_3_, ...), custom_call_target="tpu_custom_call" | custom-call | flops 1835008 | bytes 7340032 | tf_op jit(solution)/shard_map/place/pallas_call | solution.py:384
  (104 shorter events, 53.4 us)
Async XLA Ops:
  6.7 56.0 %collective-permute-start.2 = (bf16[512,2048]{1,0:T(8,128)(2,1)}, bf16[512,2048]{1,0:T(8,128)(2,1)}, u32[]{:S(2)}, u32[]{:S(2)}) collective-permute-start(bf16[512,2048]{1,0:T(8,128)(2,1)} %fusion.11.u0_ref), channel_id=1, source_target_pairs={{0,2},{1,3},{2,0},{3,1},{4,6},{5,7},{6,4},{7,5}} | collective-permute-start | bytes 6291464 | tf_op jit(solution)/shard_map/ppermute | solution.py:403
  10.0 83.6 %collective-permute-start.3 = (bf16[512,2048]{1,0:T(8,128)(2,1)}, bf16[512,2048]{1,0:T(8,128)(2,1)}, u32[]{:S(2)}, u32[]{:S(2)}) collective-permute-start(bf16[512,2048]{1,0:T(8,128)(2,1)} %fusion.11.u0_ref), channel_id=1, source_target_pairs={{0,1},{1,0},{2,3},{3,2},{4,5},{5,4},{6,7},{7,6}} | collective-permute-start | bytes 6291464 | tf_op jit(solution)/shard_map/ppermute | solution.py:406
  13.5 48.1 %collective-permute-start = (f32[512,16]{1,0:T(8,128)}, f32[512,16]{1,0:T(8,128)}, u32[]{:S(2)}, u32[]{:S(2)}) collective-permute-start(f32[512,16]{1,0:T(8,128)} %copy.36), channel_id=1, source_target_pairs={{0,2},{1,3},{2,0},{3,1},{4,6},{5,7},{6,4},{7,5}} | collective-permute-start | bytes 98312 | tf_op jit(solution)/shard_map/ppermute | solution.py:403
  15.8 52.4 %collective-permute-start.6 = (bf16[256,2048]{1,0:T(8,128)(2,1)}, bf16[256,2048]{1,0:T(8,128)(2,1)}, u32[]{:S(2)}, u32[]{:S(2)}) collective-permute-start(bf16[256,2048]{1,0:T(8,128)(2,1)} %constant_dynamic-slice_fusion), channel_id=1, source_target_pairs={{0,4},{4,0},{1,5},{5,1},{2,6},{6,2},{3,7},{7,3}} | collective-permute-start | bytes 3145736 | tf_op jit(solution)/shard_map/ppermute | solution.py:409
  55.8 136.1 %collective-permute-start.5 = (bf16[1024,1024]{1,0:T(8,128)(2,1)}, bf16[1024,1024]{1,0:T(8,128)(2,1)}, u32[]{:S(2)}, u32[]{:S(2)}) collective-permute-start(bf16[1024,1024]{1,0:T(8,128)(2,1)} %attn.1._after.ctx_ref), channel_id=1, source_target_pairs={{0,4},{4,0},{1,5},{5,1},{2,6},{6,2},{3,7},{7,3}} | collective-permute-start | bytes 6291464 | tf_op jit(solution)/shard_map/ppermute | solution.py:409
  62.6 3.8 collective-permute-start.1
  62.7 31.0 %collective-permute-start.4 = (bf16[512,2048]{1,0:T(8,128)(2,1)}, bf16[512,2048]{1,0:T(8,128)(2,1)}, u32[]{:S(2)}, u32[]{:S(2)}) collective-permute-start(bf16[512,2048]{1,0:T(8,128)(2,1)} %collective-permute-done.2.u1_ref), channel_id=1, source_target_pairs={{0,1},{1,0},{2,3},{3,2},{4,5},{5,4},{6,7},{7,6}} | collective-permute-start | bytes 6291464 | tf_op jit(solution)/shard_map/ppermute | solution.py:406
  68.2 25.4 %collective-permute-start.8 = (bf16[256,2048]{1,0:T(8,128)(2,1)}, bf16[256,2048]{1,0:T(8,128)(2,1)}, u32[]{:S(2)}, u32[]{:S(2)}) collective-permute-start(bf16[256,2048]{1,0:T(8,128)(2,1)} %collective-permute-done.6.w0_ref), channel_id=1, source_target_pairs={{0,2},{1,3},{2,0},{3,1},{4,6},{5,7},{6,4},{7,5}} | collective-permute-start | bytes 3145736 | tf_op jit(solution)/shard_map/ppermute | solution.py:403
  74.1 117.8 %collective-permute-start.7 = (bf16[256,2048]{1,0:T(8,128)(2,1)}, bf16[256,2048]{1,0:T(8,128)(2,1)}, u32[]{:S(2)}, u32[]{:S(2)}) collective-permute-start(bf16[256,2048]{1,0:T(8,128)(2,1)} %collective-permute-done.6.w0_ref), channel_id=1, source_target_pairs={{0,1},{1,0},{2,3},{3,2},{4,5},{5,4},{6,7},{7,6}} | collective-permute-start | bytes 3145736 | tf_op jit(solution)/shard_map/ppermute | solution.py:406
  93.6 98.2 %collective-permute-start.9 = (bf16[256,2048]{1,0:T(8,128)(2,1)}, bf16[256,2048]{1,0:T(8,128)(2,1)}, u32[]{:S(2)}, u32[]{:S(2)}) collective-permute-start(bf16[256,2048]{1,0:T(8,128)(2,1)} %collective-permute-done.8.w2_ref), channel_id=1, source_target_pairs={{0,1},{1,0},{2,3},{3,2},{4,5},{5,4},{6,7},{7,6}} | collective-permute-start | bytes 3145736 | tf_op jit(solution)/shard_map/ppermute | solution.py:406
  253.0 14.4 %collective-permute-start.10 = (f32[256,2048]{1,0:T(8,128)}, f32[256,2048]{1,0:T(8,128)}, u32[]{:S(2)}, u32[]{:S(2)}) collective-permute-start(f32[256,2048]{1,0:T(8,128)} %shard_map.172._after), channel_id=1, source_target_pairs={{0,1},{1,0},{2,3},{3,2},{4,5},{5,4},{6,7},{7,6}} | collective-permute-start | bytes 6291464 | tf_op jit(solution)/shard_map/ppermute | solution.py:406
  263.0 15.2 %collective-permute-start.11 = (f32[256,2048]{1,0:T(8,128)}, f32[256,2048]{1,0:T(8,128)}, u32[]{:S(2)}, u32[]{:S(2)}) collective-permute-start(f32[256,2048]{1,0:T(8,128)} %shard_map.173._after), channel_id=1, source_target_pairs={{0,1},{1,0},{2,3},{3,2},{4,5},{5,4},{6,7},{7,6}} | collective-permute-start | bytes 6291464 | tf_op jit(solution)/shard_map/ppermute | solution.py:406
  265.3 84.4 %collective-permute-start.12 = (f32[256,2048]{1,0:T(8,128)}, f32[256,2048]{1,0:T(8,128)}, u32[]{:S(2)}, u32[]{:S(2)}) collective-permute-start(f32[256,2048]{1,0:T(8,128)} %get-tuple-element.15._after), channel_id=1, source_target_pairs={{0,4},{4,0},{1,5},{5,1},{2,6},{6,2},{3,7},{7,3}} | collective-permute-start | bytes 6291464 | tf_op jit(solution)/shard_map/ppermute | solution.py:409
  333.8 30.3 %collective-permute-start.13 = (f32[256,2048]{1,0:T(8,128)}, f32[256,2048]{1,0:T(8,128)}, u32[]{:S(2)}, u32[]{:S(2)}) collective-permute-start(f32[256,2048]{1,0:T(8,128)} %shard_map.176._after), channel_id=1, source_target_pairs={{0,1},{1,0},{2,3},{3,2},{4,5},{5,4},{6,7},{7,6}} | collective-permute-start | bytes 6291464 | tf_op jit(solution)/shard_map/ppermute | solution.py:406
  335.6 83.7 %collective-permute-start.16 = (f32[256,2048]{1,0:T(8,128)}, f32[256,2048]{1,0:T(8,128)}, u32[]{:S(2)}, u32[]{:S(2)}) collective-permute-start(f32[256,2048]{1,0:T(8,128)} %get-tuple-element.19), channel_id=1, source_target_pairs={{0,4},{4,0},{1,5},{5,1},{2,6},{6,2},{3,7},{7,3}} | collective-permute-start | bytes 6291464 | tf_op jit(solution)/shard_map/ppermute | solution.py:409
  335.6 28.5 %collective-permute-start.14 = (f32[128,2048]{1,0:T(8,128)}, f32[128,2048]{1,0:T(8,128)}, u32[]{:S(2)}, u32[]{:S(2)}) collective-permute-start(f32[128,2048]{1,0:T(8,128)} %get-tuple-element.16._after), channel_id=1, source_target_pairs={{0,2},{1,3},{2,0},{3,1},{4,6},{5,7},{6,4},{7,5}} | collective-permute-start | bytes 3145736 | tf_op jit(solution)/shard_map/ppermute | solution.py:403
  339.7 81.0 %collective-permute-start.18 = (f32[128,2048]{1,0:T(8,128)}, f32[128,2048]{1,0:T(8,128)}, u32[]{:S(2)}, u32[]{:S(2)}) collective-permute-start(f32[128,2048]{1,0:T(8,128)} %get-tuple-element.17._after), channel_id=1, source_target_pairs={{0,2},{1,3},{2,0},{3,1},{4,6},{5,7},{6,4},{7,5}} | collective-permute-start | bytes 3145736 | tf_op jit(solution)/shard_map/ppermute | solution.py:403
  349.7 59.3 %collective-permute-start.15 = (f32[128,2048]{1,0:T(8,128)}, f32[128,2048]{1,0:T(8,128)}, u32[]{:S(2)}, u32[]{:S(2)}) collective-permute-start(f32[128,2048]{1,0:T(8,128)} %get-tuple-element.18), channel_id=1, source_target_pairs={{0,2},{1,3},{2,0},{3,1},{4,6},{5,7},{6,4},{7,5}} | collective-permute-start | bytes 3145736 | tf_op jit(solution)/shard_map/ppermute | solution.py:403
  364.1 56.6 %collective-permute-start.17 = (f32[256,2048]{1,0:T(8,128)}, f32[256,2048]{1,0:T(8,128)}, u32[]{:S(2)}, u32[]{:S(2)}) collective-permute-start(f32[256,2048]{1,0:T(8,128)} %shard_map.177._after), channel_id=1, source_target_pairs={{0,1},{1,0},{2,3},{3,2},{4,5},{5,4},{6,7},{7,6}} | collective-permute-start | bytes 6291464 | tf_op jit(solution)/shard_map/ppermute | solution.py:406
  364.1 67.0 %collective-permute-start.19 = (f32[128,2048]{1,0:T(8,128)}, f32[128,2048]{1,0:T(8,128)}, u32[]{:S(2)}, u32[]{:S(2)}) collective-permute-start(f32[128,2048]{1,0:T(8,128)} %get-tuple-element.20), channel_id=1, source_target_pairs={{0,2},{1,3},{2,0},{3,1},{4,6},{5,7},{6,4},{7,5}} | collective-permute-start | bytes 3145736 | tf_op jit(solution)/shard_map/ppermute | solution.py:403
  409.0 36.7 %collective-permute-start.21 = (bf16[128,2048]{1,0:T(8,128)(2,1)}, bf16[128,2048]{1,0:T(8,128)(2,1)}, u32[]{:S(2)}, u32[]{:S(2)}) collective-permute-start(bf16[128,2048]{1,0:T(8,128)(2,1)} %shard_map.178._after.refs_0_), channel_id=1, source_target_pairs={{0,4},{4,0},{1,5},{5,1},{2,6},{6,2},{3,7},{7,3}} | collective-permute-start | bytes 1572872 | tf_op jit(solution)/shard_map/ppermute | solution.py:409
  419.3 26.4 %collective-permute-start.22 = (bf16[128,2048]{1,0:T(8,128)(2,1)}, bf16[128,2048]{1,0:T(8,128)(2,1)}, u32[]{:S(2)}, u32[]{:S(2)}) collective-permute-start(bf16[128,2048]{1,0:T(8,128)(2,1)} %shard_map.179._after.refs_1_), channel_id=1, source_target_pairs={{0,4},{4,0},{1,5},{5,1},{2,6},{6,2},{3,7},{7,3}} | collective-permute-start | bytes 1572872 | tf_op jit(solution)/shard_map/ppermute | solution.py:409
  430.4 15.3 %collective-permute-start.23 = (bf16[128,2048]{1,0:T(8,128)(2,1)}, bf16[128,2048]{1,0:T(8,128)(2,1)}, u32[]{:S(2)}, u32[]{:S(2)}) collective-permute-start(bf16[128,2048]{1,0:T(8,128)(2,1)} %shard_map.180._after.refs_2_), channel_id=1, source_target_pairs={{0,4},{4,0},{1,5},{5,1},{2,6},{6,2},{3,7},{7,3}} | collective-permute-start | bytes 1572872 | tf_op jit(solution)/shard_map/ppermute | solution.py:409
  440.7 14.3 %collective-permute-start.20 = (bf16[128,2048]{1,0:T(8,128)(2,1)}, bf16[128,2048]{1,0:T(8,128)(2,1)}, u32[]{:S(2)}, u32[]{:S(2)}) collective-permute-start(bf16[128,2048]{1,0:T(8,128)(2,1)} %shard_map.181.refs_3_), channel_id=1, source_target_pairs={{0,4},{4,0},{1,5},{5,1},{2,6},{6,2},{3,7},{7,3}} | collective-permute-start | bytes 1572872 | tf_op jit(solution)/shard_map/ppermute | solution.py:409
  (10 other events, 140.5 us)

commit v6 on v5

--- a/solution.py
+++ b/solution.py
@@ -14,9 +14,9 @@
 SEG = 16
 GT = 128
 OUT = 96
-CHUNKS = 4
+CHUNKS = 2
 CT = 256
-VMEM_BIG = 67_000_000
+VMEM_BIG = 60 * 1024 * 1024
 
 
 def inv_rms_of(x_f32):
@@ -79,7 +79,6 @@
         in_specs=[col, col, col, tab, tab], out_specs=col,
         out_shape=jax.ShapeDtypeStruct((seq, width), BF16),
         scratch_shapes=[pltpu.VMEM((seq, pair * head_dim), BF16)] + [pltpu.VMEM((256, seq), F32), pltpu.VMEM((256, seq), BF16)] * pair,
-        compiler_params=pltpu.CompilerParams(vmem_limit_bytes=VMEM_BIG),
         cost_estimate=pl.CostEstimate(flops=width * seq * seq * 4, bytes_accessed=12 * seq * width, transcendentals=0),
         name="attn",
     )(q, k, v, cos_t, sin_t)
@@ -276,7 +275,7 @@
     return pl.pallas_call(
         functools.partial(combine_kernel, src, int(init is not None), len(adds)), grid_spec=grid_spec,
         out_shape=[jax.ShapeDtypeStruct((half // n_out, d), BF16 if adds else F32)] * n_out,
-        compiler_params=pltpu.CompilerParams(vmem_limit_bytes=VMEM_BIG),
+        compiler_params=pltpu.CompilerParams(vmem_limit_bytes=VMEM_BIG if adds else 40 * 1024 * 1024),
         cost_estimate=pl.CostEstimate(flops=12_000_000_000, bytes_accessed=10_000_000, transcendentals=0),
     )(rows, pos[src], gates[src], y_all, after, *extra, *[v for v, _ in adds])
 
@@ -496,17 +495,15 @@
             for k in range(CHUNKS // 2):
                 m_x.append(over_x(m1[k]))
 
-        s_own, = run_ffn(my_tp, half, f_norm, w_gate, w_up, w_down, tie, adds=((after, None),))
-        own, peer, got2 = [], [], []
+        m2, = run_combine(2, rows, pos, gates_all, y_all, tie)
+        got2 = over_core(m2)
+
+        s_own, = run_ffn(my_tp, half, f_norm, w_gate, w_up, w_down, m2, adds=((after, None),))
+        own, peer = [], []
         tie = s_own
-        per = CHUNKS // 2
-        for p in range(2):
-            tie, = run_combine(2, rows, pos, gates_all, y_all, tie, part=(p, 2))
-            got2.append(over_core(tie))
         for c in range(CHUNKS):
-            p, k = c // per, c % per
             tie, = run_combine(0, rows, pos, gates_all, y_all, tie, part=(c, CHUNKS),
-                               adds=((s_own, c), (f_got[p], k), (got2[p], k), (m_x[c], 0)))
+                               adds=((s_own, c), (f_got[c], 0), (got2, c), (m_x[c], 0)))
             own.append(tie)
             peer.append(over_tp(tie))
         mine, other = my_tp * CHUNKS, (1 - my_tp) * CHUNKS

time: 464 us -> 453 us (0.976)
  waiting for transfers between devices: 77.1 us -> 108 us
  Pallas kernels: 308 us -> 278 us
    pallas_call x10 -> x7, Pallas kernels: 99.9 us -> 70.9 us  [run_combine(): pl.pallas_call(functools.partial(combine_kernel, src, int(init is not Non...]
    ppermute x8 -> x6, waiting for transfers between devices: 6.26 us -> 32.7 us  [over_tp(): return lax.ppermute(v, 'tp', [(0, 1), (1, 0)])]
    ppermute x7 -> x5, waiting for transfers between devices: 70.8 us -> 74.6 us  [over_x(): return lax.ppermute(v, 'ep', [(i, i ^ 2) for i in range(4)])]
    ppermute x7 -> x5, starting transfers between devices: 13.3 us -> 9.93 us  [over_x(): return lax.ppermute(v, 'ep', [(i, i ^ 2) for i in range(4)])]
  transfers between devices with their start and end apart: 24 -> 19, of which waited for: 6 -> 7; matrix products, arithmetic and copies ran while one was open for 9% -> 8% of each run, Pallas kernels for 54% -> 44%
where the time goes in v6:
time: 453 us; the launch traced here: 448 us
  Pallas kernels  278 us (61%)
  waiting for transfers between devices  108 us (24%)
  matrix products  23 us (5%)
  starting transfers between devices  18.1 us (4%)
  other arithmetic  10.5 us (2%)
  local copies, waits for them, and re-layouts  9.53 us (2%)
    pallas_call x1, Pallas kernels, run_experts(): pl.pallas_call(expert_kernel, grid_spec=grid_spec, out_shape=jax.ShapeDty...  98.1 us
    ppermute x5, waiting for transfers between devices, over_x(): return lax.ppermute(v, 'ep', [(i, i ^ 2) for i in range(4)])  74.6 us
    pallas_call x7, Pallas kernels, run_combine(): pl.pallas_call(functools.partial(combine_kernel, src, int(init is not Non...  70.9 us
    pallas_call x2, Pallas kernels, run_ffn(): pl.pallas_call(functools.partial(ffn_kernel, n_up, len(adds)), grid_spec=...  69.3 us
    ppermute x6, waiting for transfers between devices, over_tp(): return lax.ppermute(v, 'tp', [(0, 1), (1, 0)])  32.7 us
    pallas_call x1, Pallas kernels, run_out(): pl.pallas_call(out_kernel, grid_spec=grid_spec, out_shape=[jax.ShapeDtype...  16.7 us
    pallas_call x1, Pallas kernels, attention(): pl.pallas_call(attn_kernel, grid=(steps,), in_specs=[col, col, col, tab,...  15.7 us
    ppermute x5, starting transfers between devices, over_x(): return lax.ppermute(v, 'ep', [(i, i ^ 2) for i in range(4)])  9.93 us
  transfers between devices with their start and end apart: 19, of which 7 were waited for; matrix products, arithmetic and copies ran while one was open for 8% of the time, Pallas kernels for 44%

profile of v6, /device:TPU:0, one launch (start us, length us, event | category | flops | bytes accessed | tf_op | source)
XLA Modules:
  0.0 447.7 jit_solution(6250931967092694863)
XLA Ops:
  0.0 3.1 multiply_reduce_fusion
  14.5 9.5 %fusion.12.v_ref = bf16[1024,1024]{1,0:T(8,128)(2,1)} fusion(bf16[256,8,8,128]{3,2,1,0:T(8,128)(2,1)} %bitcast.74, bf16[1,1024,2048]{2,1,0:T(8,128)(2,1)} %param.19, f32[2048]{0:T(1024)S(1)} %convert_element_type.61, f32[1024]{0:T(1024)S(1)} %add_rsqrt_fusion), kind=kOutput, calls=%fused_computation.15 | convolution fusion | flops 4304404480 | bytes 10498048 | tf_op jit(solution)/shard_map/dot_general | solution.py:471
  24.0 6.4 %fusion.4.k_ref = f32[1024,1024]{1,0:T(8,128)} fusion(bf16[256,8,8,128]{3,2,1,0:T(8,128)(2,1)S(1)} %bitcast.75, bf16[1,1024,2048]{2,1,0:T(8,128)(2,1)S(1)} %copy-done.3, f32[2048]{0:T(1024)S(1)} %convert_element_type.61, f32[1024]{0:T(1024)S(1)} %add_rsqrt_fusion), kind=kOutput, calls=%fused_computation.6 | convolution fusion | flops 4303355904 | bytes 12595200 | tf_op jit(solution)/shard_map/dot_general | solution.py:470
  30.4 6.1 %fusion.7.q_ref = f32[1024,1024]{1,0:T(8,128)} fusion(bf16[256,8,8,128]{3,2,1,0:T(8,128)(2,1)S(1)} %bitcast.76, bf16[1,1024,2048]{2,1,0:T(8,128)(2,1)S(1)} %copy-done.3, f32[2048]{0:T(1024)S(1)} %convert_element_type.61, f32[1024]{0:T(1024)S(1)} %add_rsqrt_fusion), kind=kOutput, calls=%fused_computation.9 | convolution fusion | flops 4303355904 | bytes 12595200 | tf_op jit(solution)/shard_map/dot_general | solution.py:469
  36.5 15.7 %attn.1._after.ctx_ref = bf16[1024,1024]{1,0:T(8,128)(2,1)} custom-call(f32[1024,1024]{1,0:T(8,128)} %fusion.7.q_ref, f32[1024,1024]{1,0:T(8,128)} %fusion.4.k_ref, bf16[1024,1024]{1,0:T(8,128)(2,1)} %fusion.12.v_ref, f32[1024,128]{1,0:T(8,128)} %constant.64.clone.cos_ref, f32[1024,128]{1,0:T(8,128)} %constant.65.clone.sin_ref), custom_call_target="tpu_custom_call" | custom-call | flops 4294967296 | bytes 12582912 | tf_op jit(solution)/shard_map/attn/pallas_call | solution.py:77
  53.3 7.4 %collective-permute-done = f32[512,16]{1,0:T(8,128)S(1)} collective-permute-done((f32[512,16]{1,0:T(8,128)S(1)}, f32[512,16]{1,0:T(8,128)S(1)}, u32[]{:S(2)}, u32[]{:S(2)}) %collective-permute-start) | collective-permute-done | bytes 32800 | tf_op jit(solution)/shard_map/ppermute | solution.py:402
  71.9 18.5 %collective-permute-done.8.w2_ref = bf16[256,2048]{1,0:T(8,128)(2,1)} collective-permute-done((bf16[256,2048]{1,0:T(8,128)(2,1)}, bf16[256,2048]{1,0:T(8,128)(2,1)}, u32[]{:S(2)}, u32[]{:S(2)}) %collective-permute-start.8) | collective-permute-done | bytes 1048608 | tf_op jit(solution)/shard_map/ppermute | solution.py:402
  90.4 98.1 %experts.1._after.y_hbm = bf16[4,3328,2048]{2,1,0:T(8,128)(2,1)} custom-call(s32[4,16]{1,0:T(4,128)} %copy-done.12, s32[4,16]{1,0:T(4,128)} %select_reduce_fusion.3.loc_ref, s32[4,16]{1,0:T(4,128)} %copy-done.16, s32[4,16,1,512]{3,2,1,0:T(1,128)} %broadcast_in_dim.106.rank_ref, bf16[512,2048]{1,0:T(8,128)(2,1)} %copy-done.4, ...), custom_call_target="tpu_custom_call" | custom-call | flops 89999998976 | bytes 241326592 | tf_op jit(solution)/shard_map/experts/pallas_call | solution.py:168
  188.6 16.7 %out_proj.1 = (bf16[1024,2048]{1,0:T(8,128)(2,1)}, bf16[1024,2048]{1,0:T(8,128)(2,1)}) custom-call(s32[4]{0:T(128)} %iota_xor_fusion.q_ref, bf16[1024,2048]{1,0:T(8,128)(2,1)} %bitcast.65, bf16[1,2048]{1,0:T(2,128)(2,1)} %reshape.178.gain_ref, bf16[1024,1024]{1,0:T(8,128)(2,1)} %attn.1._after.ctx_ref, bf16[1024,1024]{1,0:T(8,128)(2,1)} %collective-permute-done.5.peer_ref, ...), custom_call_target="tpu_custom_call" | custom-call | flops 10000000000 | bytes 24000000 | tf_op jit(solution)/shard_map/out_proj/pallas_call | solution.py:309
  205.3 34.5 %ffn.2 = (f32[256,2048]{1,0:T(8,128)}, f32[256,2048]{1,0:T(8,128)}) custom-call(s32[1]{0:T(128)} %bitcast.20.off_ref, bf16[1024,2048]{1,0:T(8,128)(2,1)} %get-tuple-element.9.x_ref, bf16[2048,4096]{1,0:T(8,128)(2,1)} %wg_ref.5, bf16[2048,4096]{1,0:T(8,128)(2,1)} %wu_ref.5, bf16[4096,2048]{1,0:T(8,128)(2,1)} %wd_ref.5, ...), custom_call_target="tpu_custom_call" | custom-call | flops 28672000000 | bytes 60000000 | tf_op jit(solution)/shard_map/ffn/pallas_call | solution.py:357
  239.8 7.5 %shard_map.172._after = f32[256,2048]{1,0:T(8,128)S(1)} custom-call(s32[4]{0:T(128)S(1)} %get-tuple-element.13.rows_ref, s32[512,8]{1,0:T(8,128)S(1)} %get-tuple-element.17.pos_ref, f32[512,8]{1,0:T(8,128)S(1)} %get-tuple-element.21.gate_ref, bf16[4,3328,2048]{2,1,0:T(8,128)(2,1)} %experts.1._after.y_hbm, f32[256,2048]{1,0:T(8,128)} %get-tuple-element.11._after), custom_call_target="tpu_custom_call" | custom-call | flops 12000000000 | bytes 10000000 | tf_op jit(solution)/shard_map/pallas_call | solution.py:275
  247.3 7.5 %shard_map.173._after = f32[256,2048]{1,0:T(8,128)S(1)} custom-call(s32[4]{0:T(128)S(1)} %get-tuple-element.13.rows_ref, s32[512,8]{1,0:T(8,128)S(1)} %get-tuple-element.17.pos_ref, f32[512,8]{1,0:T(8,128)S(1)} %get-tuple-element.21.gate_ref, bf16[4,3328,2048]{2,1,0:T(8,128)(2,1)} %experts.1._after.y_hbm, f32[256,2048]{1,0:T(8,128)S(1)} %shard_map.172._after), custom_call_target="tpu_custom_call" | custom-call | flops 12000000000 | bytes 10000000 | tf_op jit(solution)/shard_map/pallas_call | solution.py:275
  255.5 8.9 %shard_map.174._after = f32[256,2048]{1,0:T(8,128)} custom-call(s32[4]{0:T(128)S(1)} %get-tuple-element.13.rows_ref, s32[512,8]{1,0:T(8,128)S(1)} %get-tuple-element.18.pos_ref, f32[512,8]{1,0:T(8,128)S(1)} %slice_bitcast_fusion.2.gate_ref, bf16[4,3328,2048]{2,1,0:T(8,128)(2,1)} %experts.1._after.y_hbm, f32[256,2048]{1,0:T(8,128)S(1)} %shard_map.173._after, ...), custom_call_target="tpu_custom_call" | custom-call | flops 12000000000 | bytes 10000000 | tf_op jit(solution)/shard_map/pallas_call | solution.py:275
  264.5 7.5 %shard_map.175._after = f32[256,2048]{1,0:T(8,128)S(1)} custom-call(s32[4]{0:T(128)S(1)} %get-tuple-element.13.rows_ref, s32[512,8]{1,0:T(8,128)S(1)} %get-tuple-element.18.pos_ref, f32[512,8]{1,0:T(8,128)S(1)} %slice_bitcast_fusion.2.gate_ref, bf16[4,3328,2048]{2,1,0:T(8,128)(2,1)} %experts.1._after.y_hbm, f32[256,2048]{1,0:T(8,128)} %shard_map.174._after, ...), custom_call_target="tpu_custom_call" | custom-call | flops 12000000000 | bytes 10000000 | tf_op jit(solution)/shard_map/pallas_call | solution.py:275
  272.0 14.1 %shard_map.176._after = f32[512,2048]{1,0:T(8,128)} custom-call(s32[4]{0:T(128)S(1)} %get-tuple-element.13.rows_ref, s32[512,8]{1,0:T(8,128)S(1)} %get-tuple-element.19.pos_ref, f32[512,8]{1,0:T(8,128)S(1)} %get-tuple-element.22.gate_ref, bf16[4,3328,2048]{2,1,0:T(8,128)(2,1)} %experts.1._after.y_hbm, f32[256,2048]{1,0:T(8,128)S(1)} %shard_map.175._after), custom_call_target="tpu_custom_call" | custom-call | flops 12000000000 | bytes 10000000 | tf_op jit(solution)/shard_map/pallas_call | solution.py:275
  289.1 5.0 %collective-permute-start.16 = (f32[256,2048]{1,0:T(8,128)S(1)}, f32[256,2048]{1,0:T(8,128)}, u32[]{:S(2)}, u32[]{:S(2)}) collective-permute-start(f32[256,2048]{1,0:T(8,128)S(1)} %shard_map.175._after), channel_id=1, source_target_pairs={{0,2},{1,3},{2,0},{3,1},{4,6},{5,7},{6,4},{7,5}} | collective-permute-start | bytes 6291464 | tf_op jit(solution)/shard_map/ppermute | solution.py:402
  294.1 34.8 %ffn.3._after.rest_0_ = f32[512,2048]{1,0:T(8,128)} custom-call(s32[1]{0:T(128)} %bitcast.12.off_ref, bf16[1024,2048]{1,0:T(8,128)(2,1)} %get-tuple-element.9.x_ref, bf16[2048,4096]{1,0:T(8,128)(2,1)} %wg_ref.5, bf16[2048,4096]{1,0:T(8,128)(2,1)} %wu_ref.5, bf16[4096,2048]{1,0:T(8,128)(2,1)} %wd_ref.5, f32[512,2048]{1,0:T(8,128)} %shard_map.176._after, ...), custom_call_target="tpu_custom_call" | custom-call | flops 28672000000 | bytes 60000000 | tf_op jit(solution)/shard_map/ffn/pallas_call | solution.py:357
  329.0 6.9 %collective-permute-done.12.rest_1_ = f32[256,2048]{1,0:T(8,128)} collective-permute-done((f32[256,2048]{1,0:T(8,128)}, f32[256,2048]{1,0:T(8,128)}, u32[]{:S(2)}, u32[]{:S(2)}) %collective-permute-start.12) | collective-permute-done | bytes 2097184 | tf_op jit(solution)/shard_map/ppermute | solution.py:408
  335.9 48.8 %collective-permute-done.14.rest_3_ = f32[256,2048]{1,0:T(8,128)} collective-permute-done((f32[256,2048]{1,0:T(8,128)}, f32[256,2048]{1,0:T(8,128)}, u32[]{:S(2)}, u32[]{:S(2)}) %collective-permute-start.14) | collective-permute-done | bytes 2097184 | tf_op jit(solution)/shard_map/ppermute | solution.py:402
  384.7 12.7 %shard_map.177._after.refs_0_ = bf16[256,2048]{1,0:T(8,128)(2,1)} custom-call(s32[4]{0:T(128)} %copy-done.2, s32[512,8]{1,0:T(8,128)} %get-tuple-element.20.pos_ref, f32[512,8]{1,0:T(8,128)} %slice_bitcast_fusion.6.gate_ref, bf16[4,3328,2048]{2,1,0:T(8,128)(2,1)} %experts.1._after.y_hbm, f32[512,2048]{1,0:T(8,128)} %ffn.3._after.rest_0_, ...), custom_call_target="tpu_custom_call" | custom-call | flops 12000000000 | bytes 10000000 | tf_op jit(solution)/shard_map/pallas_call | solution.py:275
  399.1 12.6 %shard_map.178.refs_1_ = bf16[256,2048]{1,0:T(8,128)(2,1)} custom-call(s32[4]{0:T(128)} %copy-done.2, s32[512,8]{1,0:T(8,128)} %get-tuple-element.20.pos_ref, f32[512,8]{1,0:T(8,128)} %slice_bitcast_fusion.6.gate_ref, bf16[4,3328,2048]{2,1,0:T(8,128)(2,1)} %experts.1._after.y_hbm, bf16[256,2048]{1,0:T(8,128)(2,1)} %shard_map.177._after.refs_0_, ...), custom_call_target="tpu_custom_call" | custom-call | flops 12000000000 | bytes 10000000 | tf_op jit(solution)/shard_map/pallas_call | solution.py:275
  412.6 11.0 %collective-permute-done.18.refs_2_ = bf16[256,2048]{1,0:T(8,128)(2,1)S(1)} collective-permute-done((bf16[256,2048]{1,0:T(8,128)(2,1)}, bf16[256,2048]{1,0:T(8,128)(2,1)S(1)}, u32[]{:S(2)}, u32[]{:S(2)}) %collective-permute-start.18) | collective-permute-done | bytes 1048608 | tf_op jit(solution)/shard_map/ppermute | solution.py:408
  424.6 4.6 %place.2.refs_1_ = bf16[1024,2048]{1,0:T(8,128)(2,1)} custom-call(s32[3]{0:T(128)} %pad_add_fusion._dest, bf16[256,2048]{1,0:T(8,128)(2,1)} %shard_map.177._after.refs_0_, bf16[256,2048]{1,0:T(8,128)(2,1)} %shard_map.178.refs_1_, bf16[256,2048]{1,0:T(8,128)(2,1)} %copy-done.10), custom_call_target="tpu_custom_call" | custom-call | flops 1572864 | bytes 6291456 | tf_op jit(solution)/shard_map/place/pallas_call | solution.py:383
  429.2 14.8 %collective-permute-done.17.refs_0_ = bf16[256,2048]{1,0:T(8,128)(2,1)S(1)} collective-permute-done((bf16[256,2048]{1,0:T(8,128)(2,1)}, bf16[256,2048]{1,0:T(8,128)(2,1)S(1)}, u32[]{:S(2)}, u32[]{:S(2)}) %collective-permute-start.17) | collective-permute-done | bytes 1048608 | tf_op jit(solution)/shard_map/ppermute | solution.py:408
  (109 shorter events, 34.1 us)
Async XLA Ops:
  5.4 85.0 %collective-permute-start.3 = (bf16[512,2048]{1,0:T(8,128)(2,1)S(1)}, bf16[512,2048]{1,0:T(8,128)(2,1)}, u32[]{:S(2)}, u32[]{:S(2)}) collective-permute-start(bf16[512,2048]{1,0:T(8,128)(2,1)S(1)} %fusion.11.u0_ref), channel_id=1, source_target_pairs={{0,1},{1,0},{2,3},{3,2},{4,5},{5,4},{6,7},{7,6}} | collective-permute-start | bytes 6291464 | tf_op jit(solution)/shard_map/ppermute | solution.py:405
  6.3 55.3 %collective-permute-start.2 = (bf16[512,2048]{1,0:T(8,128)(2,1)S(1)}, bf16[512,2048]{1,0:T(8,128)(2,1)}, u32[]{:S(2)}, u32[]{:S(2)}) collective-permute-start(bf16[512,2048]{1,0:T(8,128)(2,1)S(1)} %fusion.11.u0_ref), channel_id=1, source_target_pairs={{0,2},{1,3},{2,0},{3,1},{4,6},{5,7},{6,4},{7,5}} | collective-permute-start | bytes 6291464 | tf_op jit(solution)/shard_map/ppermute | solution.py:402
  11.1 53.7 %collective-permute-start.6 = (bf16[256,2048]{1,0:T(8,128)(2,1)}, bf16[256,2048]{1,0:T(8,128)(2,1)}, u32[]{:S(2)}, u32[]{:S(2)}) collective-permute-start(bf16[256,2048]{1,0:T(8,128)(2,1)} %constant_dynamic-slice_fusion), channel_id=1, source_target_pairs={{0,4},{4,0},{1,5},{5,1},{2,6},{6,2},{3,7},{7,3}} | collective-permute-start | bytes 3145736 | tf_op jit(solution)/shard_map/ppermute | solution.py:408
  13.8 48.3 %copy-start.5 = (f32[512,16]{1,0:T(8,128)}, f32[512,16]{1,0:T(8,128)S(1)}, u32[]{:S(2)}) copy-start(f32[512,16]{1,0:T(8,128)S(1)} %copy.36) | copy-start | bytes 98308
  13.8 46.9 %collective-permute-start = (f32[512,16]{1,0:T(8,128)S(1)}, f32[512,16]{1,0:T(8,128)S(1)}, u32[]{:S(2)}, u32[]{:S(2)}) collective-permute-start(f32[512,16]{1,0:T(8,128)S(1)} %copy.36), channel_id=1, source_target_pairs={{0,2},{1,3},{2,0},{3,1},{4,6},{5,7},{6,4},{7,5}} | collective-permute-start | bytes 98312 | tf_op jit(solution)/shard_map/ppermute | solution.py:402
  36.5 25.6 %copy-start.15 = (bf16[2048]{0:T(1024)(128)(2,1)S(1)}, bf16[2048]{0:T(1024)(128)(2,1)}, u32[]{:S(2)}) copy-start(bf16[2048]{0:T(1024)(128)(2,1)} %param.26) | copy-start | bytes 12292
  52.2 136.4 %collective-permute-start.5 = (bf16[1024,1024]{1,0:T(8,128)(2,1)}, bf16[1024,1024]{1,0:T(8,128)(2,1)}, u32[]{:S(2)}, u32[]{:S(2)}) collective-permute-start(bf16[1024,1024]{1,0:T(8,128)(2,1)} %attn.1._after.ctx_ref), channel_id=1, source_target_pairs={{0,4},{4,0},{1,5},{5,1},{2,6},{6,2},{3,7},{7,3}} | collective-permute-start | bytes 6291464 | tf_op jit(solution)/shard_map/ppermute | solution.py:408
  61.5 2.1 collective-permute-start.1
  61.6 28.9 %collective-permute-start.4 = (bf16[512,2048]{1,0:T(8,128)(2,1)}, bf16[512,2048]{1,0:T(8,128)(2,1)}, u32[]{:S(2)}, u32[]{:S(2)}) collective-permute-start(bf16[512,2048]{1,0:T(8,128)(2,1)} %collective-permute-done.2.u1_ref), channel_id=1, source_target_pairs={{0,1},{1,0},{2,3},{3,2},{4,5},{5,4},{6,7},{7,6}} | collective-permute-start | bytes 6291464 | tf_op jit(solution)/shard_map/ppermute | solution.py:405
  64.3 26.1 %copy-start.12 = (s32[4,16]{1,0:T(4,128)}, s32[4,16]{1,0:T(4,128)S(1)}, u32[]{:S(2)}) copy-start(s32[4,16]{1,0:T(4,128)S(1)} %convert_reduce_fusion.n_ref) | copy-start | bytes 772
  64.5 207.5 %copy-start.2 = (s32[4]{0:T(128)}, s32[4]{0:T(128)S(1)}, u32[]{:S(2)}) copy-start(s32[4]{0:T(128)S(1)} %get-tuple-element.13.rows_ref) | copy-start | bytes 52
  64.6 25.8 %copy-start.16 = (s32[4,16]{1,0:T(4,128)}, s32[4,16]{1,0:T(4,128)S(1)}, u32[]{:S(2)}) copy-start(s32[4,16]{1,0:T(4,128)S(1)} %select_reduce_fusion.2.dst_ref) | copy-start | bytes 772
  64.9 25.5 %collective-permute-start.8 = (bf16[256,2048]{1,0:T(8,128)(2,1)}, bf16[256,2048]{1,0:T(8,128)(2,1)}, u32[]{:S(2)}, u32[]{:S(2)}) collective-permute-start(bf16[256,2048]{1,0:T(8,128)(2,1)} %collective-permute-done.6.w0_ref), channel_id=1, source_target_pairs={{0,2},{1,3},{2,0},{3,1},{4,6},{5,7},{6,4},{7,5}} | collective-permute-start | bytes 3145736 | tf_op jit(solution)/shard_map/ppermute | solution.py:402
  71.9 116.7 %collective-permute-start.7 = (bf16[256,2048]{1,0:T(8,128)(2,1)}, bf16[256,2048]{1,0:T(8,128)(2,1)}, u32[]{:S(2)}, u32[]{:S(2)}) collective-permute-start(bf16[256,2048]{1,0:T(8,128)(2,1)} %collective-permute-done.6.w0_ref), channel_id=1, source_target_pairs={{0,1},{1,0},{2,3},{3,2},{4,5},{5,4},{6,7},{7,6}} | collective-permute-start | bytes 3145736 | tf_op jit(solution)/shard_map/ppermute | solution.py:405
  90.4 98.2 %collective-permute-start.9 = (bf16[256,2048]{1,0:T(8,128)(2,1)}, bf16[256,2048]{1,0:T(8,128)(2,1)}, u32[]{:S(2)}, u32[]{:S(2)}) collective-permute-start(bf16[256,2048]{1,0:T(8,128)(2,1)} %collective-permute-done.8.w2_ref), channel_id=1, source_target_pairs={{0,1},{1,0},{2,3},{3,2},{4,5},{5,4},{6,7},{7,6}} | collective-permute-start | bytes 3145736 | tf_op jit(solution)/shard_map/ppermute | solution.py:405
  247.3 8.2 %collective-permute-start.10 = (f32[256,2048]{1,0:T(8,128)S(1)}, f32[256,2048]{1,0:T(8,128)S(1)}, u32[]{:S(2)}, u32[]{:S(2)}) collective-permute-start(f32[256,2048]{1,0:T(8,128)S(1)} %shard_map.172._after), channel_id=1, source_target_pairs={{0,1},{1,0},{2,3},{3,2},{4,5},{5,4},{6,7},{7,6}} | collective-permute-start | bytes 6291464 | tf_op jit(solution)/shard_map/ppermute | solution.py:405
  254.9 9.6 %collective-permute-start.11 = (f32[256,2048]{1,0:T(8,128)S(1)}, f32[256,2048]{1,0:T(8,128)S(1)}, u32[]{:S(2)}, u32[]{:S(2)}) collective-permute-start(f32[256,2048]{1,0:T(8,128)S(1)} %shard_map.173._after), channel_id=1, source_target_pairs={{0,1},{1,0},{2,3},{3,2},{4,5},{5,4},{6,7},{7,6}} | collective-permute-start | bytes 6291464 | tf_op jit(solution)/shard_map/ppermute | solution.py:405
  286.1 98.5 %collective-permute-start.13 = (f32[512,2048]{1,0:T(8,128)}, f32[512,2048]{1,0:T(8,128)}, u32[]{:S(2)}, u32[]{:S(2)}) collective-permute-start(f32[512,2048]{1,0:T(8,128)} %shard_map.176._after), channel_id=1, source_target_pairs={{0,1},{1,0},{2,3},{3,2},{4,5},{5,4},{6,7},{7,6}} | collective-permute-start | bytes 12582920 | tf_op jit(solution)/shard_map/ppermute | solution.py:405
  287.0 48.9 %collective-permute-start.12 = (f32[256,2048]{1,0:T(8,128)}, f32[256,2048]{1,0:T(8,128)}, u32[]{:S(2)}, u32[]{:S(2)}) collective-permute-start(f32[256,2048]{1,0:T(8,128)} %get-tuple-element.11._after), channel_id=1, source_target_pairs={{0,4},{4,0},{1,5},{5,1},{2,6},{6,2},{3,7},{7,3}} | collective-permute-start | bytes 6291464 | tf_op jit(solution)/shard_map/ppermute | solution.py:408
  289.1 110.0 %collective-permute-start.15 = (f32[256,2048]{1,0:T(8,128)}, f32[256,2048]{1,0:T(8,128)}, u32[]{:S(2)}, u32[]{:S(2)}) collective-permute-start(f32[256,2048]{1,0:T(8,128)} %get-tuple-element.12), channel_id=1, source_target_pairs={{0,4},{4,0},{1,5},{5,1},{2,6},{6,2},{3,7},{7,3}} | collective-permute-start | bytes 6291464 | tf_op jit(solution)/shard_map/ppermute | solution.py:408
  289.1 110.0 %collective-permute-start.16 = (f32[256,2048]{1,0:T(8,128)S(1)}, f32[256,2048]{1,0:T(8,128)}, u32[]{:S(2)}, u32[]{:S(2)}) collective-permute-start(f32[256,2048]{1,0:T(8,128)S(1)} %shard_map.175._after), channel_id=1, source_target_pairs={{0,2},{1,3},{2,0},{3,1},{4,6},{5,7},{6,4},{7,5}} | collective-permute-start | bytes 6291464 | tf_op jit(solution)/shard_map/ppermute | solution.py:402
  294.1 90.6 %collective-permute-start.14 = (f32[256,2048]{1,0:T(8,128)}, f32[256,2048]{1,0:T(8,128)}, u32[]{:S(2)}, u32[]{:S(2)}) collective-permute-start(f32[256,2048]{1,0:T(8,128)} %shard_map.174._after), channel_id=1, source_target_pairs={{0,2},{1,3},{2,0},{3,1},{4,6},{5,7},{6,4},{7,5}} | collective-permute-start | bytes 6291464 | tf_op jit(solution)/shard_map/ppermute | solution.py:402
  397.3 26.3 %collective-permute-start.18 = (bf16[256,2048]{1,0:T(8,128)(2,1)}, bf16[256,2048]{1,0:T(8,128)(2,1)S(1)}, u32[]{:S(2)}, u32[]{:S(2)}) collective-permute-start(bf16[256,2048]{1,0:T(8,128)(2,1)} %shard_map.177._after.refs_0_), channel_id=1, source_target_pairs={{0,4},{4,0},{1,5},{5,1},{2,6},{6,2},{3,7},{7,3}} | collective-permute-start | bytes 3145736 | tf_op jit(solution)/shard_map/ppermute | solution.py:408
  411.7 32.3 %collective-permute-start.17 = (bf16[256,2048]{1,0:T(8,128)(2,1)}, bf16[256,2048]{1,0:T(8,128)(2,1)S(1)}, u32[]{:S(2)}, u32[]{:S(2)}) collective-permute-start(bf16[256,2048]{1,0:T(8,128)(2,1)} %shard_map.178.refs_1_), channel_id=1, source_target_pairs={{0,4},{4,0},{1,5},{5,1},{2,6},{6,2},{3,7},{7,3}} | collective-permute-start | bytes 3145736 | tf_op jit(solution)/shard_map/ppermute | solution.py:408
  (14 other events, 117.1 us)
